TPU v7x, 16 devices: a whole 2x2x2 slice. The times are simulated.
16 devices in a mesh: tp: 2 (over z), ep: 8 (over y, x, core).
Axes of the slice: x: 2, y: 2, z: 2, core: 2. Of those that a mesh axis runs over, the one named last changes fastest.
Arguments:
- hidden_in: bfloat16 [1536, 2048], P(('tp', 'ep'))
- cache0: bfloat16 [1536, 256, 576], P(('tp', 'ep'))
- cache1: bfloat16 [1536, 256, 576], P(('tp', 'ep'))
- kv_lens: int32 [1536], P(('tp', 'ep'))
- route_ids: int32 [1536, 6], P(('tp', 'ep'))
- route_wts: float32 [1536, 6], P(('tp', 'ep'))
- att0_q: bfloat16 [2048, 16, 192], replicated
- att0_uk: bfloat16 [16, 128, 512], replicated
- att0_uv: bfloat16 [16, 512, 128], replicated
- att0_o: bfloat16 [16, 128, 2048], replicated
- att1_q: bfloat16 [2048, 16, 192], replicated
- att1_uk: bfloat16 [16, 128, 512], replicated
- att1_uv: bfloat16 [16, 512, 128], replicated
- att1_o: bfloat16 [16, 128, 2048], replicated
- ffn0_gate: bfloat16 [2048, 10944], P(None, 'tp')
- ffn0_up: bfloat16 [2048, 10944], P(None, 'tp')
- ffn0_down: bfloat16 [10944, 2048], P('tp')
- ffn1_gate: bfloat16 [2048, 10944], P(None, 'tp')
- ffn1_up: bfloat16 [2048, 10944], P(None, 'tp')
- ffn1_down: bfloat16 [10944, 2048], P('tp')
- exp_gate: bfloat16 [16, 2048, 1408], P(('tp', 'ep'))
- exp_up: bfloat16 [16, 2048, 1408], P(('tp', 'ep'))
- exp_down: bfloat16 [16, 1408, 2048], P(('tp', 'ep'))
Outputs:
- output: bfloat16 [1536, 2048], P(('tp', 'ep'))
All inputs are finite; a program needn't handle non-finite values.
Results may differ from a plain program's by a relative error of at most 0.0155603.
Values are sent between devices in bfloat16 or wider.
A program may use at most 1 GiB of HBM per device.

v0:
```python
import jax
import jax.numpy as jnp
from jax import lax
from jax.sharding import PartitionSpec as P

FLAT_AXES = ('tp', 'ep')


def rms_norm(vec):
    vec32 = vec.astype(jnp.float32)
    return (vec32 * lax.rsqrt(jnp.mean(vec32 * vec32, axis=-1, keepdims=True) + 1e-6)).astype(jnp.bfloat16)


def rope_rotate(vals, pos):
    half_dim = vals.shape[-1] // 2
    inv_freq = 10000.0 ** (-2.0 * jnp.arange(half_dim, dtype=jnp.float32) / vals.shape[-1])
    rot_angle = pos.astype(jnp.float32)[..., None, None] * inv_freq
    cos_ang = jnp.cos(rot_angle)
    sin_ang = jnp.sin(rot_angle)
    lead_half = vals[..., :half_dim]
    tail_half = vals[..., half_dim:]
    return jnp.concatenate([lead_half * cos_ang - tail_half * sin_ang, tail_half * cos_ang + lead_half * sin_ang], axis=-1)


def swiglu(rows, w_gate, w_up, w_down):
    gate_val = jnp.dot(rows, w_gate, preferred_element_type=jnp.float32)
    up_val = jnp.dot(rows, w_up, preferred_element_type=jnp.float32)
    act_val = (jax.nn.silu(gate_val) * up_val).astype(jnp.bfloat16)
    return jnp.dot(act_val, w_down, preferred_element_type=jnp.float32)


def attention(normed, cache, kv_lens, w_q, w_uk, w_uv, w_o):
    nope_dim = w_uk.shape[1]
    latent = w_uk.shape[2]
    scale = w_q.shape[2] ** -0.5
    q_full = jnp.einsum('bd,dhc->bhc', normed, w_q, preferred_element_type=jnp.float32).astype(jnp.bfloat16)
    q_rope = rope_rotate(q_full[..., nope_dim:].astype(jnp.float32), kv_lens).astype(jnp.bfloat16)
    q_lat = jnp.einsum('bhn,hnl->bhl', q_full[..., :nope_dim], w_uk, preferred_element_type=jnp.float32).astype(jnp.bfloat16)
    q_cat = jnp.concatenate([q_lat, q_rope], axis=-1)
    scores = jnp.einsum('bhc,bpc->bhp', q_cat, cache, preferred_element_type=jnp.float32) * scale
    valid = jnp.arange(cache.shape[1])[None, None, :] < kv_lens[:, None, None]
    probs = jax.nn.softmax(jnp.where(valid, scores, -1e30), axis=-1).astype(jnp.bfloat16)
    o_lat = jnp.einsum('bhp,bpl->bhl', probs, cache[:, :, :latent], preferred_element_type=jnp.float32).astype(jnp.bfloat16)
    o_val = jnp.einsum('bhl,hlv->bhv', o_lat, w_uv, preferred_element_type=jnp.float32).astype(jnp.bfloat16)
    return jnp.einsum('bhv,hvd->bd', o_val, w_o, preferred_element_type=jnp.float32)


def dense_ffn(normed, w_gate, w_up, w_down):
    group_rows = lax.all_gather(normed, 'tp', axis=0, tiled=True)
    part_out = swiglu(group_rows, w_gate, w_up, w_down)
    return lax.psum_scatter(part_out, 'tp', scatter_dimension=0, tiled=True)


def expert_mix(normed, route_ids, route_wts, w_gate, w_up, w_down, n_dev):
    tok_dev, top_k = route_ids.shape
    slot_cap = min(tok_dev, (2 * tok_dev * top_k + n_dev - 1) // n_dev)
    flat_ids = route_ids.reshape(-1)
    is_real = flat_ids < n_dev
    dest_dev = jnp.where(is_real, flat_ids, n_dev)
    onehot = (dest_dev[:, None] == jnp.arange(n_dev + 1)[None, :]).astype(jnp.int32)
    slot_rank = jnp.sum((jnp.cumsum(onehot, axis=0) - onehot) * onehot, axis=1)
    target = jnp.where(is_real, dest_dev * slot_cap + slot_rank, -1).reshape(tok_dev, top_k)
    disp_mat = jnp.sum(target[None, :, :] == jnp.arange(n_dev * slot_cap)[:, None, None], axis=2).astype(jnp.bfloat16)
    send_buf = jnp.dot(disp_mat, normed, preferred_element_type=jnp.float32).astype(jnp.bfloat16)
    recv_buf = lax.all_to_all(send_buf, FLAT_AXES, 0, 0, tiled=True)
    exp_out = swiglu(recv_buf, w_gate[0], w_up[0], w_down[0]).astype(jnp.bfloat16)
    back_buf = lax.all_to_all(exp_out, FLAT_AXES, 0, 0, tiled=True)
    picked = jnp.take(back_buf, jnp.maximum(target, 0).reshape(-1), axis=0).reshape(tok_dev, top_k, -1)
    slot_vals = jnp.where((target >= 0)[..., None], picked, normed[:, None, :])
    return jnp.sum(route_wts[..., None] * slot_vals.astype(jnp.float32), axis=1)


def solution(mesh):
    n_dev = mesh.shape['tp'] * mesh.shape['ep']
    rows_spec = P(FLAT_AXES, None)
    cube_spec = P(FLAT_AXES, None, None)
    whole_spec = P(None, None, None)
    col_split = P(None, 'tp')
    row_split = P('tp', None)
    in_specs = (rows_spec, cube_spec, cube_spec, P(FLAT_AXES), rows_spec, rows_spec,
                whole_spec, whole_spec, whole_spec, whole_spec, whole_spec, whole_spec, whole_spec, whole_spec,
                col_split, col_split, row_split, col_split, col_split, row_split,
                cube_spec, cube_spec, cube_spec)

    def body(hidden_in, cache0, cache1, kv_lens, route_ids, route_wts, att0_q, att0_uk, att0_uv, att0_o, att1_q, att1_uk, att1_uv, att1_o, ffn0_gate, ffn0_up, ffn0_down, ffn1_gate, ffn1_up, ffn1_down, exp_gate, exp_up, exp_down):
        att_zero = attention(rms_norm(hidden_in), cache0, kv_lens, att0_q, att0_uk, att0_uv, att0_o)
        h_zero = (hidden_in.astype(jnp.float32) + att_zero).astype(jnp.bfloat16)
        u_zero = rms_norm(h_zero)
        mix = expert_mix(u_zero, route_ids, route_wts, exp_gate, exp_up, exp_down, n_dev)
        f_zero = (h_zero.astype(jnp.float32) + dense_ffn(u_zero, ffn0_gate, ffn0_up, ffn0_down)).astype(jnp.bfloat16)
        att_one = attention(rms_norm(f_zero), cache1, kv_lens, att1_q, att1_uk, att1_uv, att1_o)
        h_one = (f_zero.astype(jnp.float32) + att_one).astype(jnp.bfloat16)
        dense_one = dense_ffn(rms_norm(h_one), ffn1_gate, ffn1_up, ffn1_down)
        return (h_one.astype(jnp.float32) + dense_one + mix).astype(jnp.bfloat16)

    return jax.shard_map(body, mesh=mesh, in_specs=in_specs, out_specs=rows_spec, check_vma=False)
```

profile of v0, /device:TPU:0, one launch (start us, length us, event | category | flops | bytes accessed | tf_op | source)
XLA Modules:
  0.0 375.9 jit_solution(10991450829211895276)
XLA Ops:
  6.6 0.8 convert_element_type.128
  7.4 0.7 iota_compare_fusion.1
  8.1 1.2 fusion.57
  9.3 9.0 %convolution_convert_fusion.5 = bf16[96,16,192]{2,0,1:T(8,128)(2,1)S(1)} fusion(bf16[2048,16,192]{0,2,1:T(8,128)(2,1)} %param.29, bf16[96,2048]{1,0:T(8,128)(2,1)} %param.23, f32[96]{0:T(128)S(1)} %add_rsqrt_fusion.3), kind=kOutput, calls=%fused_computation.55 | convolution fusion | flops 1208844288 | bytes 13566336 | tf_op jit(solution)/shard_map/bd,dhc->bhc/dot_general | solution.py:36
  18.4 0.6 fusion.35
  19.0 0.2 multiply_cosine_fusion
  19.2 0.4 subtract_convert_fusion.1
  19.6 0.3 pad_maximum_fusion
  19.9 11.6 %fusion.21 = f32[96,16,256]{2,1,0:T(8,128)S(1)} fusion(bf16[96,256,576]{1,2,0:T(8,128)(2,1)} %param.24, bf16[96,16,576]{2,0,1:T(8,128)(2,1)S(1)} %pad_maximum_fusion), kind=kOutput, calls=%fused_computation.34 | convolution fusion | flops 452984832 | bytes 31653888 | tf_op jit(solution)/shard_map/bhc,bpc->bhp/dot_general | solution.py:40
  31.5 1.2 copy-done.6
  32.7 0.6 fusion.98
  33.3 13.0 %fusion.25 = bf16[96,16,512]{2,1,0:T(8,128)(2,1)} fusion(bf16[96,256,576]{1,2,0:T(8,128)(2,1)} %param.24, f32[96,16]{1,0:T(8,128)S(1)} %fusion.98, f32[96,16,256]{2,1,0:T(8,128)} %copy-done.6, pred[96,256]{1,0:T(8,128)(4,1)S(1)} %iota_compare_fusion.1), kind=kOutput, calls=%fused_computation.40 | convolution fusion | flops 405407488 | bytes 28342272 | tf_op jit(solution)/shard_map/bhp,bpl->bhl/dot_general | solution.py:43
  46.3 7.9 %multiply_reduce_fusion.2 = (f32[96]{0:T(128)S(1)}, f32[96,2048]{1,0:T(8,128)S(1)}) fusion(bf16[16,128,2048]{2,1,0:T(8,128)(2,1)} %param.32, bf16[16,512,128]{2,1,0:T(8,128)(2,1)} %param.31, bf16[96,16,512]{2,1,0:T(8,128)(2,1)} %fusion.25, bf16[96,2048]{1,0:T(8,128)(2,1)S(1)} %copy-done.2), kind=kOutput, calls=%fused_computation.78 | convolution fusion | flops 1008009088 | bytes 13238656 | tf_op jit(solution)/shard_map/bhv,hvd->bd/dot_general | solution.py:45
  54.4 13.1 %all_gather.6 = bf16[192,2048]{1,0:T(8,128)(2,1)S(1)} all-gather(bf16[96,2048]{1,0:T(8,128)(2,1)S(1)} %multiply_convert_fusion.1), channel_id=1, replica_groups=mesh['tp'=2,'ep'=8] {'tp'}, dimensions={0}, use_global_device_ids=true | all-gather | bytes 1179648 | tf_op jit(solution)/shard_map/all_gather | solution.py:49
  67.5 14.4 %fusion.104 = f32[192,5472]{1,0:T(8,128)} fusion(bf16[192,2048]{1,0:T(8,128)(2,1)S(1)} %all_gather.6, bf16[2048,5472]{0,1:T(8,128)(2,1)} %param.37), kind=kOutput, calls=%fused_computation.135 | convolution fusion | flops 4303355904 | bytes 27402240 | tf_op jit(solution)/shard_map/dot_general | solution.py:26
  81.8 21.1 %fusion.105 = f32[192,2048]{1,0:T(8,128)} fusion(bf16[5472,2048]{1,0:T(8,128)(2,1)} %param.39, bf16[192,2048]{1,0:T(8,128)(2,1)S(1)} %all_gather.6, bf16[2048,5472]{0,1:T(8,128)(2,1)} %param.38, f32[192,5472]{1,0:T(8,128)} %fusion.104), kind=kOutput, calls=%fused_computation.136 | convolution fusion | flops 8613015552 | bytes 51388416 | tf_op jit(solution)/shard_map/dot_general | solution.py:29
  103.1 0.1 copy.57
  103.2 0.1 reshape.200
  103.5 1.4 reduce-window.6
  104.9 0.3 slice_reduce_fusion
  105.4 0.1 reduce_sum.90
  105.6 0.4 convert_reduce_fusion
  106.0 3.5 convolution_convert_fusion
  109.6 3.9 %all-to-all-start = ((bf16[16,72,2048]{2,1,0:T(8,128)(2,1)}), bf16[16,72,2048]{2,1,0:T(8,128)(2,1)}, u32[]{:S(2)}, u32[]{:S(2)}) async-start(bf16[16,72,2048]{2,1,0:T(8,128)(2,1)} %bitcast.100), calls=%async_computation.2 | async-start | bytes 9437184 | tf_op jit(solution)/shard_map/all_to_all | solution.py:65
  113.5 63.2 %reduce-scatter.3.cloned.1.call-done = f32[96,2048]{1,0:T(8,128)} async-done(((f32[192,2048]{1,0:T(8,128)}), f32[96,2048]{1,0:T(8,128)}) %reduce-scatter.3.cloned.1.call-update) | async-done | bytes 786448 | tf_op jit(solution)/shard_map/reduce_scatter | solution.py:51
  176.7 1.3 fusion.59
  178.1 9.0 %convolution_convert_fusion.4 = bf16[96,16,192]{2,0,1:T(8,128)(2,1)S(1)} fusion(bf16[2048,16,192]{0,2,1:T(8,128)(2,1)} %param.33, bf16[96,2048]{1,0:T(8,128)(2,1)S(1)} %get-tuple-element.6, f32[96]{0:T(128)S(1)} %add_rsqrt_fusion.1), kind=kOutput, calls=%fused_computation.54 | convolution fusion | flops 1208844288 | bytes 13566336 | tf_op jit(solution)/shard_map/bd,dhc->bhc/dot_general | solution.py:36
  187.2 0.3 subtract_convert_fusion
  187.5 1.2 copy-done.7
  188.7 0.6 fusion.36
  189.3 0.3 pad_maximum_fusion.1
  189.6 11.3 %fusion.19 = f32[96,16,256]{2,1,0:T(8,128)S(1)} fusion(bf16[96,256,576]{1,2,0:T(8,128)(2,1)} %param.25, bf16[96,16,576]{2,0,1:T(8,128)(2,1)S(1)} %pad_maximum_fusion.1), kind=kOutput, calls=%fused_computation.32 | convolution fusion | flops 452984832 | bytes 31653888 | tf_op jit(solution)/shard_map/bhc,bpc->bhp/dot_general | solution.py:40
  200.9 1.2 copy-done.5
  202.1 0.6 fusion.101
  202.7 12.1 %fusion.28 = bf16[96,16,512]{2,1,0:T(8,128)(2,1)S(1)} fusion(bf16[96,256,576]{1,2,0:T(8,128)(2,1)} %param.25, f32[96,16]{1,0:T(8,128)S(1)} %fusion.101, f32[96,16,256]{2,1,0:T(8,128)} %copy-done.5, pred[96,256]{1,0:T(8,128)(4,1)S(1)} %iota_compare_fusion.1), kind=kOutput, calls=%fused_computation.41 | convolution fusion | flops 405407488 | bytes 28342272 | tf_op jit(solution)/shard_map/bhp,bpl->bhl/dot_general | solution.py:43
  214.8 7.5 %multiply_reduce_fusion.1 = (f32[96]{0:T(128)S(1)}, f32[96,2048]{1,0:T(8,128)S(1)}) fusion(bf16[16,128,2048]{2,1,0:T(8,128)(2,1)} %param.36, bf16[16,512,128]{2,1,0:T(8,128)(2,1)} %param.35, bf16[96,16,512]{2,1,0:T(8,128)(2,1)S(1)} %fusion.28, bf16[96,2048]{1,0:T(8,128)(2,1)S(1)} %copy-done.4), kind=kOutput, calls=%fused_computation.72 | convolution fusion | flops 1008009088 | bytes 13238656 | tf_op jit(solution)/shard_map/bhv,hvd->bd/dot_general | solution.py:45
  222.4 10.2 %all_gather.7 = bf16[192,2048]{1,0:T(8,128)(2,1)S(1)} all-gather(bf16[96,2048]{1,0:T(8,128)(2,1)S(1)} %multiply_convert_fusion), channel_id=1, replica_groups=mesh['tp'=2,'ep'=8] {'tp'}, dimensions={0}, use_global_device_ids=true | all-gather | bytes 1179648 | tf_op jit(solution)/shard_map/all_gather | solution.py:49
  232.6 14.1 %fusion.106 = f32[192,5472]{1,0:T(8,128)} fusion(bf16[192,2048]{1,0:T(8,128)(2,1)S(1)} %all_gather.7, bf16[2048,5472]{0,1:T(8,128)(2,1)} %param.40), kind=kOutput, calls=%fused_computation.137 | convolution fusion | flops 4303355904 | bytes 27402240 | tf_op jit(solution)/shard_map/dot_general | solution.py:26
  246.7 12.7 %fusion.11 = f32[1152,1408]{1,0:T(8,128)} fusion(bf16[1152,2048]{1,0:T(8,128)(2,1)} %bitcast.10, bf16[1,2048,1408]{2,1,0:T(8,128)(2,1)} %param.43), kind=kOutput, calls=%fused_computation.18 | convolution fusion | flops 6643777536 | bytes 16973824 | tf_op jit(solution)/shard_map/dot_general | solution.py:26
  259.4 22.5 %convolution_convert_fusion.1 = bf16[1152,2048]{1,0:T(8,128)(2,1)} fusion(bf16[1,1408,2048]{2,1,0:T(8,128)(2,1)} %param.45, bf16[1152,2048]{1,0:T(8,128)(2,1)} %bitcast.10, f32[1152,1408]{1,0:T(8,128)} %fusion.11, bf16[1,2048,1408]{2,1,0:T(8,128)(2,1)} %param.44), kind=kOutput, calls=%fused_computation.12 | convolution fusion | flops 13299646464 | bytes 27459584 | tf_op jit(solution)/shard_map/dot_general | solution.py:29
  281.9 3.3 all-to-all-start.1
  285.3 21.4 %fusion.107 = f32[192,2048]{1,0:T(8,128)} fusion(bf16[5472,2048]{1,0:T(8,128)(2,1)} %param.42, bf16[192,2048]{1,0:T(8,128)(2,1)S(1)} %all_gather.7, bf16[2048,5472]{0,1:T(8,128)(2,1)} %param.41, f32[192,5472]{1,0:T(8,128)} %fusion.106), kind=kOutput, calls=%fused_computation.138 | convolution fusion | flops 8613015552 | bytes 51388416 | tf_op jit(solution)/shard_map/dot_general | solution.py:29
  306.8 0.1 reshape.203
  307.1 38.9 %all-to-all-done.1 = bf16[16,72,2048]{2,1,0:T(8,128)(2,1)} async-done(((bf16[16,72,2048]{2,1,0:T(8,128)(2,1)}), bf16[16,72,2048]{2,1,0:T(8,128)(2,1)}, u32[]{:S(2)}, u32[]{:S(2)}) %all-to-all-start.1) | async-done | bytes 4718624 | tf_op jit(solution)/shard_map/all_to_all | solution.py:67
  346.0 9.8 %gather_fusion = bf16[576,2048]{1,0:T(8,128)(2,1)} fusion(bf16[1152,2048]{1,0:T(8,128)(2,1)} %bitcast.15, s32[1024]{0:T(1024)S(1)} %pad_clamp_fusion), kind=kCustom, calls=%fused_computation | custom fusion | bytes 4720896 | tf_op jit(solution)/shard_map/jit(_take)/gather | solution.py:68
  355.7 5.0 %gather.7 = bf16[96,6,2048]{2,1,0:T(8,128)(2,1)} reshape(bf16[576,2048]{1,0:T(8,128)(2,1)} %gather_fusion) | data formatting | bytes 4718592 | tf_op jit(solution)/shard_map/jit(_take)/gather | solution.py:68
  360.8 5.8 %multiply_reduce_fusion = f32[96,2048]{1,0:T(8,128)} fusion(bf16[96,6,2048]{2,1,0:T(8,128)(2,1)} %gather.7, f32[96,6]{1,0:T(8,128)S(1)} %copy.50, pred[96,6]{1,0:T(8,128)(4,1)S(1)} %broadcast_compare_fusion, pred[96,6]{1,0:T(8,128)(4,1)S(1)} %get-tuple-element.7, bf16[96,2048]{1,0:T(8,128)(2,1)S(1)} %multiply_convert_fusion.1), kind=kLoop, calls=%fused_computation.15 | loop fusion | flops 5701632 | bytes 3542400 | tf_op jit(solution)/shard_map/reduce_sum | solution.py:70
  366.5 2.2 add_convert_fusion
  (52 shorter events, 1.1 us)
Async XLA Ops:
  6.5 11.9 %copy-start = (bf16[16,128,512]{2,1,0:T(8,128)(2,1)S(1)}, bf16[16,128,512]{2,1,0:T(8,128)(2,1)}, u32[]{:S(2)}) copy-start(bf16[16,128,512]{2,1,0:T(8,128)(2,1)} %param.30) | copy-start | bytes 6291460
  6.5 170.2 %reduce-scatter.3.cloned.1.call-start = ((), (), s32[]{:S(2)}) async-start(), calls=%async_computation.4 | async-start | bytes 2359296 | tf_op jit(solution)/shard_map/reduce_scatter | solution.py:51
  31.5 1.2 copy-start.6
  33.3 13.0 %copy-start.2 = (bf16[96,2048]{1,0:T(8,128)(2,1)S(1)}, bf16[96,2048]{1,0:T(8,128)(2,1)}, u32[]{:S(2)}) copy-start(bf16[96,2048]{1,0:T(8,128)(2,1)} %param.23) | copy-start | bytes 1179652
  81.8 21.2 %copy-start.8 = (s32[96,6]{0,1:T(8,128)S(1)}, s32[96,6]{0,1:T(8,128)}, u32[]{:S(2)}) copy-start(s32[96,6]{0,1:T(8,128)} %param.27) | copy-start | bytes 6916
  109.6 137.1 %all-to-all-start = ((bf16[16,72,2048]{2,1,0:T(8,128)(2,1)}), bf16[16,72,2048]{2,1,0:T(8,128)(2,1)}, u32[]{:S(2)}, u32[]{:S(2)}) async-start(bf16[16,72,2048]{2,1,0:T(8,128)(2,1)} %bitcast.100), calls=%async_computation.2 | async-start | bytes 9437184 | tf_op jit(solution)/shard_map/all_to_all | solution.py:65
  178.0 9.1 %copy-start.3 = (bf16[96,2048]{1,0:T(8,128)(2,1)}, bf16[96,2048]{1,0:T(8,128)(2,1)S(1)}, u32[]{:S(2)}) copy-start(bf16[96,2048]{1,0:T(8,128)(2,1)S(1)} %get-tuple-element.6) | copy-start | bytes 1179652
  187.1 1.6 copy-start.7
  200.9 1.2 copy-start.5
  202.7 12.1 %copy-start.4 = (bf16[96,2048]{1,0:T(8,128)(2,1)S(1)}, bf16[96,2048]{1,0:T(8,128)(2,1)}, u32[]{:S(2)}) copy-start(bf16[96,2048]{1,0:T(8,128)(2,1)} %copy-done.3) | copy-start | bytes 1179652
  281.9 64.0 %all-to-all-start.1 = ((bf16[16,72,2048]{2,1,0:T(8,128)(2,1)}), bf16[16,72,2048]{2,1,0:T(8,128)(2,1)}, u32[]{:S(2)}, u32[]{:S(2)}) async-start(bf16[16,72,2048]{2,1,0:T(8,128)(2,1)} %bitcast.101), calls=%async_computation.3 | async-start | bytes 9437184 | tf_op jit(solution)/shard_map/all_to_all | solution.py:67
  285.2 21.7 %copy-start.9 = (f32[96,6]{0,1:T(8,128)S(1)}, f32[96,6]{0,1:T(8,128)}, u32[]{:S(2)}) copy-start(f32[96,6]{0,1:T(8,128)} %param.28) | copy-start | bytes 6916
  285.2 81.3 %reduce-scatter.5.cloned.1.call-start = ((), (), s32[]{:S(2)}) async-start(), calls=%async_computation.5 | async-start | bytes 2359296 | tf_op jit(solution)/shard_map/reduce_scatter | solution.py:51
  360.7 8.0 %copy-start.1 = (bf16[16,128,512]{2,1,0:T(8,128)(2,1)S(1)}, bf16[16,128,512]{2,1,0:T(8,128)(2,1)}, u32[]{:S(2)}) copy-start(bf16[16,128,512]{2,1,0:T(8,128)(2,1)} %param.30) | copy-start | bytes 6291460
Sparse Core Ops, SparseCore 0:
  103.1 73.5 reduce-scatter.2
  306.9 48.6 reduce-scatter.4
where the time goes:
time: 380 us; the launch traced here: 376 us
  matrix products  192 us (51%)
  waiting for transfers between devices  102 us (27%)
  blocking collectives  23.3 us (6%)
  local copies, waits for them, and re-layouts  19.5 us (5%)
  other arithmetic  17.3 us (5%)
  between operations  14.1 us (4%)
  starting transfers between devices  7.28 us (2%)
    dot_general x3, matrix products, swiglu(): return jnp.dot(act_val, w_down, preferred_element_type=jnp.float32)  65.1 us
    reduce_scatter x2, waiting for transfers between devices, dense_ffn(): return lax.psum_scatter(part_out, 'tp', scatter_dimension=0, tiled=True)  63.2 us
    dot_general x3, matrix products, swiglu(): gate_val = jnp.dot(rows, w_gate, preferred_element_type=jnp.float32)  41.2 us
    all_to_all x1, waiting for transfers between devices, expert_mix(): back_buf = lax.all_to_all(exp_out, FLAT_AXES, 0, 0, tiled=True)  38.9 us
    dot_general x2, matrix products, attention(): jnp.einsum('bhp,bpl->bhl', probs, cache[:, :, :latent], preferred_element...  25.1 us
    all_gather x2, blocking collectives, dense_ffn(): group_rows = lax.all_gather(normed, 'tp', axis=0, tiled=True)  23.3 us
    dot_general x2, matrix products, attention(): jnp.einsum('bhc,bpc->bhp', q_cat, cache, preferred_element_type=jnp.float32)  22.9 us
    dot_general x2, matrix products, attention(): jnp.einsum('bd,dhc->bhc', normed, w_q, preferred_element_type=jnp.float32)  18 us
  transfers between devices with their start and end apart: 4, of which 2 were waited for; matrix products, arithmetic and copies ran while one was open for 28% of the time, Pallas kernels for 0%

commit v1 on v0

v1 whole, which is shorter than its diff:
```python
import functools

import jax
import jax.numpy as jnp
from jax import lax
from jax.experimental import pallas as pl
from jax.experimental.pallas import tpu as pltpu
from jax.sharding import PartitionSpec as P

FLAT_AXES = ('tp', 'ep')
MESH = pl.DeviceIdType.MESH
F32, BF16 = jnp.float32, jnp.bfloat16
SLOT_CAP = 72
VMEM_LIMIT = 66_000_000


def rms_norm(vec):
    vec32 = vec.astype(F32)
    return (vec32 * lax.rsqrt(jnp.mean(vec32 * vec32, axis=-1, keepdims=True) + 1e-6)).astype(BF16)


def rope_rotate(vals, pos):
    half_dim = vals.shape[-1] // 2
    inv_freq = 10000.0 ** (-2.0 * jnp.arange(half_dim, dtype=F32) / vals.shape[-1])
    rot_angle = pos.astype(F32)[..., None, None] * inv_freq
    cos_ang = jnp.cos(rot_angle)
    sin_ang = jnp.sin(rot_angle)
    lead_half = vals[..., :half_dim]
    tail_half = vals[..., half_dim:]
    return jnp.concatenate([lead_half * cos_ang - tail_half * sin_ang, tail_half * cos_ang + lead_half * sin_ang], axis=-1)


def attention(normed, cache, kv_lens, w_q, w_uk, w_uv, w_o):
    nope_dim = w_uk.shape[1]
    latent = w_uk.shape[2]
    scale = w_q.shape[2] ** -0.5
    q_full = jnp.einsum('bd,dhc->bhc', normed, w_q, preferred_element_type=F32).astype(BF16)
    q_rope = rope_rotate(q_full[..., nope_dim:].astype(F32), kv_lens).astype(BF16)
    q_lat = jnp.einsum('bhn,hnl->bhl', q_full[..., :nope_dim], w_uk, preferred_element_type=F32).astype(BF16)
    q_cat = jnp.concatenate([q_lat, q_rope], axis=-1)
    scores = jnp.einsum('bhc,bpc->bhp', q_cat, cache, preferred_element_type=F32) * scale
    valid = jnp.arange(cache.shape[1])[None, None, :] < kv_lens[:, None, None]
    probs = jax.nn.softmax(jnp.where(valid, scores, -1e30), axis=-1).astype(BF16)
    o_lat = jnp.einsum('bhp,bpl->bhl', probs, cache[:, :, :latent], preferred_element_type=F32).astype(BF16)
    o_val = jnp.einsum('bhl,hlv->bhv', o_lat, w_uv, preferred_element_type=F32).astype(BF16)
    return jnp.einsum('bhv,hvd->bd', o_val, w_o, preferred_element_type=F32)


def dot_t(lhs, rhs):
    return lax.dot_general(lhs, rhs, (((1,), (1,)), ((), ())), preferred_element_type=F32)


def dot_n(lhs, rhs):
    return jnp.dot(lhs, rhs, preferred_element_type=F32)


TILE = 512
COLS = 256


def ffn_kernel(with_expert, n_buf, d_buf, *refs):
    refs = list(refs)
    u_ref, h_ref, gate_hbm, up_hbm, down_hbm = refs[:5]
    del refs[:5]
    if with_expert:
        eg_hbm, eu_hbm, ed_hbm = refs[:3]
        del refs[:3]
    out_ref = refs.pop(0)
    if with_expert:
        eo_hbm = refs.pop(0)
    rows_ref, act_ref, gate_ring, up_ring, down_ring, send_buf, recv_buf, part_buf = refs[:8]
    ring_sem, down_sem, ex_send, ex_recv, rs_send, rs_recv = refs[8:14]
    if with_expert:
        blocks, eg, eu, ed, x_buf, h_buf, e_buf, ew_sem, eo_sem = refs[14:]
    else:
        blocks, = refs[14:]

    tok, hid = h_ref.shape
    ff = gate_hbm.shape[0]
    n_full, tail = ff // TILE, ff % TILE
    n_step = n_full + 1
    n_col = hid // COLS
    k_main = (ff // 256) * 256

    z = lax.axis_index('tp')
    e = lax.axis_index('ep')
    y, x, c = e // 4, (e // 2) % 2, e % 2
    zn = (1 - z, e)
    me = z * 8 + e
    z_blk = (1 - z) * 8 + e

    def ring_copies(step, slot, rows):
        src = pl.ds(step * TILE, rows)
        return [pltpu.make_async_copy(hbm.at[src], ring.at[slot, pl.ds(0, rows)], ring_sem.at[k, slot])
                for k, (hbm, ring) in enumerate(((gate_hbm, gate_ring), (up_hbm, up_ring)))]

    def down_copy(col, slot):
        return pltpu.make_async_copy(down_hbm.at[:, pl.ds(col * COLS, COLS)], down_ring.at[slot], down_sem.at[slot])

    for step in range(n_buf):
        for cp in ring_copies(step, step, TILE):
            cp.start()
    for col in range(d_buf):
        down_copy(col, col).start()
    if with_expert:
        expert_cps = [pltpu.make_async_copy(s.at[0], d, ew_sem.at[k])
                      for k, (s, d) in enumerate(((eg_hbm, eg), (eu_hbm, eu), (ed_hbm, ed)))]
        for cp in expert_cps:
            cp.start()

    if with_expert:
        xn = (z, e + 2 - 4 * x)
        yn = (z, e + 4 - 8 * y)
        cn = (z, e + 1 - 2 * c)
        peers = (zn, xn, yn, cn)
    else:
        peers = (zn,)
    barrier = pltpu.get_barrier_semaphore()
    for peer in peers:
        pl.semaphore_signal(barrier, inc=1, device_id=peer, device_id_type=MESH)
    pl.semaphore_wait(barrier, len(peers))

    def remote(k, src, dst, peer):
        return pltpu.make_async_remote_copy(src_ref=src, dst_ref=dst, send_sem=ex_send.at[k], recv_sem=ex_recv.at[k],
                                            device_id=peer, device_id_type=MESH)

    if with_expert:
        half = tok // 2
        lo, hi = pl.ds(0, half), pl.ds(half, half)

        def plane(z_at):
            base = z_at * 8
            own = base + e
            xb = base + e + 2 - 4 * x
            yb = base + e + 4 - 8 * y
            db = base + (1 - y) * 4 + (1 - x) * 2 + c
            return own, xb, yb, db

        pa = plane(z)
        pb = plane(1 - z)
        z_copy = remote(0, u_ref, blocks.at[me], zn)
        z_copy.start()
        own_cp = pltpu.make_async_copy(u_ref, blocks.at[me], eo_sem.at[0])
        own_cp.start()

        def plane_sends(first, blks, own_src):
            own, xb, yb, db = blks
            return {
                'x': remote(first, own_src, blocks.at[own], xn),
                'y': remote(first + 1, own_src, blocks.at[own], yn),
                'xr': remote(first + 2, blocks.at[yb, hi], blocks.at[yb, hi], xn),
                'yr': remote(first + 3, blocks.at[xb, lo], blocks.at[xb, lo], yn),
                'c0': remote(first + 4, own_src, blocks.at[own], cn),
                'c1': remote(first + 5, blocks.at[xb], blocks.at[xb], cn),
                'c2': remote(first + 6, blocks.at[yb], blocks.at[yb], cn),
                'c3': remote(first + 7, blocks.at[db], blocks.at[db], cn),
            }

        sa = plane_sends(1, pa, u_ref)
        sb = plane_sends(9, pb, blocks.at[z_blk])

        def start_a0():
            sa['x'].start()
            sa['y'].start()
            sa['c0'].start()

        def start_relay(s):
            s['x'].wait_recv()
            s['y'].wait_recv()
            s['xr'].start()
            s['yr'].start()
            s['c1'].start()
            s['c2'].start()

        def start_last(s):
            s['xr'].wait_recv()
            s['yr'].wait_recv()
            s['c3'].start()

        start_a0()
        rows_ref[pl.ds(0, tok)] = u_ref[:, pl.ds(0, hid)]
        z_copy.wait_recv()
        rows_ref[pl.ds(tok, tok)] = blocks[z_blk, :, pl.ds(0, hid)]
        start_relay(sa)
        sb['x'].start()
        sb['y'].start()
        sb['c0'].start()
    else:
        z_copy = remote(0, u_ref, blocks, zn)
        z_copy.start()
        rows_ref[pl.ds(0, tok)] = u_ref[...]
        z_copy.wait_recv()
        rows_ref[pl.ds(tok, tok)] = blocks[...]

    def swiglu_tile(slot, rows, offset):
        gate_val = dot_t(rows_ref[...], gate_ring[slot, pl.ds(0, rows)])
        up_val = dot_t(rows_ref[...], up_ring[slot, pl.ds(0, rows)])
        act_ref[:, pl.ds(offset, rows)] = (jax.nn.silu(gate_val) * up_val).astype(BF16)

    @pl.loop(0, n_full)
    def _(step):
        slot = lax.rem(step, n_buf)
        for cp in ring_copies(step, slot, TILE):
            cp.wait()
        swiglu_tile(slot, TILE, pl.multiple_of(step * TILE, TILE))

        @pl.when(step + n_buf < n_full)
        def _():
            for cp in ring_copies(step + n_buf, slot, TILE):
                cp.start()

        @pl.when(step + n_buf == n_full)
        def _():
            for cp in ring_copies(n_full, slot, tail):
                cp.start()

        if with_expert:
            @pl.when(step == 5)
            def _():
                start_last(sa)

    tail_slot = n_full % n_buf
    for cp in ring_copies(n_full, tail_slot, tail):
        cp.wait()
    swiglu_tile(tail_slot, tail, n_full * TILE)

    if with_expert:
        start_relay(sb)

    def rs_copy(col):
        return pltpu.make_async_remote_copy(src_ref=send_buf.at[col], dst_ref=recv_buf.at[col], send_sem=rs_send.at[col],
                                            recv_sem=rs_recv.at[col], device_id=zn, device_id_type=MESH)

    @pl.loop(0, n_col)
    def _(col):
        slot = lax.rem(col, d_buf)
        down_copy(col, slot).wait()
        val = dot_n(act_ref[:, pl.ds(0, k_main)], down_ring[slot, pl.ds(0, k_main)])
        val += dot_n(act_ref[:, pl.ds(k_main, ff - k_main)], down_ring[slot, pl.ds(k_main, ff - k_main)])
        send_buf[col] = val[tok:]
        part_buf[col] = val[:tok]
        rs_copy(col).start()

        @pl.when(col + d_buf < n_col)
        def _():
            down_copy(col + d_buf, slot).start()

    if with_expert:
        start_last(sb)
        own_cp.wait()
        for cp in expert_cps:
            cp.wait()
        for s in (sa, sb):
            for k in ('c0', 'c1', 'c2', 'c3'):
                s[k].wait_recv()
        lane = lax.broadcasted_iota(jnp.int32, (tok, 128), 1)
        slot_id = lax.broadcasted_iota(jnp.int32, (tok, 2 * SLOT_CAP), 1).astype(F32)
        q_rows = 4 * SLOT_CAP

        def eo_copy(quad, buf):
            return pltpu.make_async_copy(e_buf.at[buf], eo_hbm.at[pl.ds(pl.multiple_of(quad * q_rows, q_rows), q_rows)],
                                         eo_sem.at[buf])

        @pl.loop(0, 4)
        def _(it):
            zq = lax.rem(z + it // 2, 2)
            yq = lax.rem(y + it, 2)
            quad = zq * 2 + yq
            buf = lax.rem(it, 2)
            for pair in range(2):
                acc = None
                for k in range(2):
                    blk = quad * 4 + pair * 2 + k
                    table = blocks[blk, :, pl.ds(hid, 128)].astype(F32)
                    rank = jnp.sum(jnp.where(lane == me, table, 0.0), axis=1, keepdims=True)
                    want = jnp.where(rank >= 0.0, rank + k * SLOT_CAP, -1.0)
                    hot = jnp.where(slot_id == want, 1.0, 0.0).astype(BF16)
                    got = lax.dot_general(hot, blocks[blk, :, pl.ds(0, hid)], (((0,), (0,)), ((), ())),
                                          preferred_element_type=F32)
                    acc = got if acc is None else acc + got
                x_buf[pl.ds(pair * 2 * SLOT_CAP, 2 * SLOT_CAP)] = acc.astype(BF16)
            for off, width in ((0, 512), (512, 512), (1024, 384)):
                gate_val = dot_n(x_buf[...], eg[:, pl.ds(off, width)])
                up_val = dot_n(x_buf[...], eu[:, pl.ds(off, width)])
                h_buf[:, pl.ds(off, width)] = (jax.nn.silu(gate_val) * up_val).astype(BF16)

            @pl.when(it >= 2)
            def _():
                eo_copy(0, buf).wait()

            for off in range(0, hid, 512):
                e_buf[buf, :, pl.ds(off, 512)] = dot_n(h_buf[...], ed[:, pl.ds(off, 512)]).astype(BF16)
            eo_copy(quad, buf).start()

        eo_copy(0, 0).wait()
        eo_copy(0, 1).wait()

    @pl.loop(0, n_col)
    def _(col):
        rs_copy(col).wait()
        cols = pl.ds(pl.multiple_of(col * COLS, COLS), COLS)
        total = h_ref[:, cols].astype(F32) + (part_buf[col] + recv_buf[col])
        out_ref[:, cols] = total.astype(out_ref.dtype)

    z_copy.wait_send()
    if with_expert:
        for s in (sa, sb):
            for cp in s.values():
                cp.wait_send()


def dense_call(u, h, w_gate_t, w_up_t, w_down, out_dtype, expert=None):
    tok, hid = h.shape
    ff = w_gate_t.shape[0]
    width = u.shape[1]
    with_expert = expert is not None
    n_buf, d_buf = (3, 3) if with_expert else (7, 4)
    vmem, hbm = pl.BlockSpec(memory_space=pltpu.VMEM), pl.BlockSpec(memory_space=pl.ANY)
    n_col = hid // COLS
    args = [u, h, w_gate_t, w_up_t, w_down]
    in_specs = [vmem, vmem, hbm, hbm, hbm]
    out_shape = [jax.ShapeDtypeStruct((tok, hid), out_dtype)]
    out_specs = [vmem]
    ff_pad = (ff // TILE + 1) * TILE
    n_ex = 17 if with_expert else 1
    scratch = [
        pltpu.VMEM((2 * tok, hid), BF16),
        pltpu.VMEM((2 * tok, ff_pad), BF16),
        pltpu.VMEM((n_buf, TILE, hid), BF16),
        pltpu.VMEM((n_buf, TILE, hid), BF16),
        pltpu.VMEM((d_buf, ff, COLS), BF16),
        pltpu.VMEM((n_col, tok, COLS), F32),
        pltpu.VMEM((n_col, tok, COLS), F32),
        pltpu.VMEM((n_col, tok, COLS), F32),
        pltpu.SemaphoreType.DMA((2, n_buf)),
        pltpu.SemaphoreType.DMA((d_buf,)),
        pltpu.SemaphoreType.DMA((n_ex,)),
        pltpu.SemaphoreType.DMA((n_ex,)),
        pltpu.SemaphoreType.DMA((n_col,)),
        pltpu.SemaphoreType.DMA((n_col,)),
    ]
    if with_expert:
        inner = expert[0].shape[2]
        args += list(expert)
        in_specs += [hbm, hbm, hbm]
        out_shape.append(jax.ShapeDtypeStruct((16 * SLOT_CAP, hid), BF16))
        out_specs.append(hbm)
        scratch += [
            pltpu.VMEM((16, tok, width), BF16),
            pltpu.VMEM((hid, inner), BF16),
            pltpu.VMEM((hid, inner), BF16),
            pltpu.VMEM((inner, hid), BF16),
            pltpu.VMEM((4 * SLOT_CAP, hid), BF16),
            pltpu.VMEM((4 * SLOT_CAP, inner), BF16),
            pltpu.VMEM((2, 4 * SLOT_CAP, hid), BF16),
            pltpu.SemaphoreType.DMA((3,)),
            pltpu.SemaphoreType.DMA((2,)),
        ]
    else:
        scratch.append(pltpu.VMEM((tok, width), BF16))
    flops = 2 * 2 * tok * hid * ff * 3 + (2 * 16 * SLOT_CAP * hid * 1408 * 3 if with_expert else 0)
    return pl.pallas_call(
        functools.partial(ffn_kernel, with_expert, n_buf, d_buf),
        out_shape=out_shape, in_specs=in_specs, out_specs=out_specs, scratch_shapes=scratch,
        compiler_params=pltpu.CompilerParams(collective_id=0 if with_expert else 1, has_side_effects=True,
                                             vmem_limit_bytes=VMEM_LIMIT),
        cost_estimate=pl.CostEstimate(flops=flops, bytes_accessed=6 * hid * ff, transcendentals=0),
        name='dense_expert' if with_expert else 'dense',
    )(*args)


def slot_ranks(route_ids, n_dev):
    tok = route_ids.shape[0]
    member = jnp.any(route_ids[:, :, None] == jnp.arange(n_dev)[None, None, :], axis=1)
    before = (jnp.arange(tok)[:, None] > jnp.arange(tok)[None, :]).astype(BF16)
    rank = jnp.dot(before, member.astype(BF16), preferred_element_type=F32)
    return jnp.where(member, rank, -1.0)


def combine(back, ranks, route_ids, route_wts, normed, n_dev):
    tok = route_ids.shape[0]
    by_expert = jnp.sum(jnp.where(route_ids[:, :, None] == jnp.arange(n_dev)[None, None, :], route_wts[:, :, None], 0.0), axis=1)
    zero_wt = jnp.sum(jnp.where(route_ids >= n_dev, route_wts, 0.0), axis=1)
    pieces, rest = [], by_expert
    for _ in range(3):
        top = lax.reduce_precision(rest, 8, 7)
        pieces.append(top)
        rest = rest - top
    hit = ranks[:, :, None] == jnp.arange(SLOT_CAP, dtype=F32)[None, None, :]
    mats = [jnp.where(hit, p[:, :, None], 0.0).astype(BF16).reshape(tok, n_dev * SLOT_CAP) for p in pieces]
    mixed = jnp.dot(jnp.concatenate(mats, axis=0), back, preferred_element_type=F32)
    mixed = (mixed[2 * tok:] + mixed[tok:2 * tok]) + mixed[:tok]
    return mixed + zero_wt[:, None] * normed.astype(F32)


def solution(mesh):
    n_dev = mesh.shape['tp'] * mesh.shape['ep']
    rows_spec = P(FLAT_AXES, None)
    cube_spec = P(FLAT_AXES, None, None)
    whole_spec = P(None, None, None)
    col_split = P(None, 'tp')
    row_split = P('tp', None)
    in_specs = (rows_spec, cube_spec, cube_spec, P(FLAT_AXES), rows_spec, rows_spec,
                whole_spec, whole_spec, whole_spec, whole_spec, whole_spec, whole_spec, whole_spec, whole_spec,
                col_split, col_split, row_split, col_split, col_split, row_split,
                cube_spec, cube_spec, cube_spec)

    def body(hidden_in, cache0, cache1, kv_lens, route_ids, route_wts, att0_q, att0_uk, att0_uv, att0_o, att1_q, att1_uk, att1_uv, att1_o, ffn0_gate, ffn0_up, ffn0_down, ffn1_gate, ffn1_up, ffn1_down, exp_gate, exp_up, exp_down):
        ranks = slot_ranks(route_ids, n_dev)
        att_zero = attention(rms_norm(hidden_in), cache0, kv_lens, att0_q, att0_uk, att0_uv, att0_o)
        h_zero = (hidden_in.astype(F32) + att_zero).astype(BF16)
        u_zero = rms_norm(h_zero)
        table = jnp.pad(ranks, ((0, 0), (0, 128 - n_dev))).astype(BF16)
        u_ext = jnp.concatenate([u_zero, table], axis=1)
        f_zero, exp_out = dense_call(u_ext, h_zero, ffn0_gate.T, ffn0_up.T, ffn0_down, BF16, (exp_gate, exp_up, exp_down))
        back = lax.all_to_all(exp_out, FLAT_AXES, 0, 0, tiled=True)
        att_one = attention(rms_norm(f_zero), cache1, kv_lens, att1_q, att1_uk, att1_uv, att1_o)
        h_one = (f_zero.astype(F32) + att_one).astype(BF16)
        dense_one, = dense_call(rms_norm(h_one), h_one, ffn1_gate.T, ffn1_up.T, ffn1_down, F32)
        mix = combine(back, ranks, route_ids, route_wts, u_zero, n_dev)
        return (dense_one + mix).astype(BF16)

    return jax.shard_map(body, mesh=mesh, in_specs=in_specs, out_specs=rows_spec, check_vma=False)
```

time: 380 us -> 230 us (0.61)
  Pallas kernels: 0 us -> 123 us
  matrix products: 192 us -> 87.6 us
  waiting for transfers between devices: 102 us -> 0.01 us
  blocking collectives: 23.3 us -> 0 us
  local copies, waits for them, and re-layouts: 19.5 us -> 1.46 us
  between operations: 14.1 us -> 0.78 us
  other arithmetic: 17.3 us -> 9.64 us
    pallas_call x0 -> x2, Pallas kernels: none -> 123 us  [dense_call(): pl.pallas_call(functools.partial(ffn_kernel, with_expert, n_buf, d_buf),...]
    dot_general x13 -> x8, matrix products: 166 us -> 61.1 us  [the longest x2 22.8 us: attention(): jnp.einsum('bhc,bpc->bhp', q_cat, cache, preferred_element_type=F32) * scale]
    reduce_scatter x2 -> x0, waiting for transfers between devices: 63.2 us -> none  [dense_ffn(): return lax.psum_scatter(part_out, 'tp', scatter_dimension=0, tiled=True)]
    all_to_all x2 -> x1, waiting for transfers between devices: 38.9 us -> 0.01 us  [body(): back = lax.all_to_all(exp_out, FLAT_AXES, 0, 0, tiled=True)]
    all_gather x2 -> x0, blocking collectives: 23.3 us -> none  [dense_ffn(): group_rows = lax.all_gather(normed, 'tp', axis=0, tiled=True)]
    gather x2 -> x0, local copies, waits for them, and re-layouts: 14.8 us -> none  [expert_mix(): jnp.take(back_buf, jnp.maximum(target, 0).reshape(-1), axis=0)]
    reduce_sum x3 -> x2, other arithmetic: 6.23 us -> 0.03 us  [the longest x1 0.02 us: combine(): zero_wt = jnp.sum(jnp.where(route_ids >= n_dev, route_wts, 0.0), axis=1)]
  transfers between devices with their start and end apart: 4 -> 1, of which waited for: 2 -> 0; matrix products, arithmetic and copies ran while one was open for 28% -> 20% of each run, Pallas kernels for 0% -> 24%
where the time goes in v1:
time: 230 us; the launch traced here: 226 us
  Pallas kernels  123 us (53%)
  matrix products  87.6 us (38%)
  other arithmetic  9.64 us (4%)
  starting transfers between devices  3.69 us (2%)
    pallas_call x2, Pallas kernels, dense_call(): pl.pallas_call(functools.partial(ffn_kernel, with_expert, n_buf, d_buf),...  123 us
    dot_general x2, matrix products, attention(): jnp.einsum('bhp,bpl->bhl', probs, cache[:, :, :latent], preferred_element...  25.3 us
    dot_general x2, matrix products, attention(): jnp.einsum('bhc,bpc->bhp', q_cat, cache, preferred_element_type=F32) * scale  22.8 us
    dot_general x2, matrix products, attention(): jnp.einsum('bd,dhc->bhc', normed, w_q, preferred_element_type=F32)  18 us
    dot_general x2, matrix products, attention(): return jnp.einsum('bhv,hvd->bd', o_val, w_o, preferred_element_type=F32)  15.8 us
  transfers between devices with their start and end apart: 1, of which 0 were waited for; matrix products, arithmetic and copies ran while one was open for 20% of the time, Pallas kernels for 24%

profile of v1, /device:TPU:0, one launch (start us, length us, event | category | flops | bytes accessed | tf_op | source)
XLA Modules:
  0.0 225.8 jit_solution(13701422324615870125)
XLA Ops:
  0.0 0.7 convert_element_type.115
  0.7 0.7 iota_compare_fusion.1
  1.4 1.2 fusion.59
  2.6 0.0 copy-start.6
  2.6 9.1 %convolution_convert_fusion.3 = bf16[96,16,192]{2,0,1:T(8,128)(2,1)S(1)} fusion(bf16[2048,16,192]{0,2,1:T(8,128)(2,1)} %param.29, bf16[96,2048]{1,0:T(8,128)(2,1)} %param.23, f32[96]{0:T(128)S(1)} %add_rsqrt_fusion.3), kind=kOutput, calls=%fused_computation.37 | convolution fusion | flops 1208844288 | bytes 13566336 | tf_op jit(solution)/shard_map/bd,dhc->bhc/dot_general | solution.py:37
  11.8 0.1 slice_convert_fusion.1
  11.8 0.6 fusion.26
  12.4 0.2 multiply_cosine_fusion
  12.7 0.4 subtract_convert_fusion.1
  13.0 0.3 pad_maximum_fusion
  13.4 11.5 %fusion.12 = f32[96,16,256]{2,1,0:T(8,128)S(1)} fusion(bf16[96,256,576]{1,2,0:T(8,128)(2,1)} %param.24, bf16[96,16,576]{2,0,1:T(8,128)(2,1)S(1)} %pad_maximum_fusion), kind=kOutput, calls=%fused_computation.16 | convolution fusion | flops 452984832 | bytes 31653888 | tf_op jit(solution)/shard_map/bhc,bpc->bhp/dot_general | solution.py:41
  24.9 0.6 fusion.104
  25.5 0.0 copy-start.1
  25.5 12.6 %fusion.16 = bf16[96,16,512]{2,1,0:T(8,128)(2,1)} fusion(bf16[96,256,576]{1,2,0:T(8,128)(2,1)} %param.24, f32[96,16]{1,0:T(8,128)S(1)} %fusion.104, f32[96,16,256]{2,1,0:T(8,128)S(1)} %fusion.12, pred[96,256]{1,0:T(8,128)(4,1)S(1)} %iota_compare_fusion.1), kind=kOutput, calls=%fused_computation.22 | convolution fusion | flops 405407488 | bytes 28342272 | tf_op jit(solution)/shard_map/bhp,bpl->bhl/dot_general | solution.py:44
  38.0 0.0 copy-done.1
  38.0 7.9 %fusion.55 = (f32[96]{0:T(128)S(1)}, bf16[96,2048]{1,0:T(8,128)(2,1)S(1)}) fusion(bf16[16,128,2048]{2,1,0:T(8,128)(2,1)} %param.32, bf16[16,512,128]{2,1,0:T(8,128)(2,1)} %param.31, bf16[96,16,512]{2,1,0:T(8,128)(2,1)} %fusion.16, bf16[96,2048]{1,0:T(8,128)(2,1)S(1)} %copy-done.1), kind=kOutput, calls=%fused_computation.61 | convolution fusion | flops 1008009088 | bytes 12845440 | tf_op jit(solution)/shard_map/bhv,hvd->bd/dot_general | solution.py:46
  45.9 0.0 copy-start.3
  46.0 0.1 copy.42
  46.1 0.1 fusion.103
  46.2 0.1 fusion.56
  46.4 0.8 fusion.77.refs_0_
  47.2 68.1 %dense_expert.1 = (bf16[96,2048]{1,0:T(8,128)(2,1)}, bf16[1152,2048]{1,0:T(8,128)(2,1)}) custom-call(bf16[96,2176]{1,0:T(8,128)(2,1)} %fusion.77.refs_0_, bf16[96,2048]{1,0:T(8,128)(2,1)} %copy-done.3, bf16[5472,2048]{1,0:T(8,128)(2,1)} %bitcast.75, bf16[5472,2048]{1,0:T(8,128)(2,1)} %bitcast.76, bf16[5472,2048]{1,0:T(8,128)(2,1)} %refs_4_.2, ...), custom_call_target="tpu_custom_call" | custom-call | flops 32841400320 | bytes 67239936 | tf_op jit(solution)/shard_map/dense_expert/pallas_call | solution.py:362
  115.3 0.0 copy-start.9
  115.3 0.0 copy-start.2
  115.3 3.7 %all-to-all-start = ((bf16[16,72,2048]{2,1,0:T(8,128)(2,1)}), bf16[16,72,2048]{2,1,0:T(8,128)(2,1)}, u32[]{:S(2)}, u32[]{:S(2)}) async-start(bf16[16,72,2048]{2,1,0:T(8,128)(2,1)} %bitcast.74), calls=%async_computation | async-start | bytes 9437184 | tf_op jit(solution)/shard_map/all_to_all | solution.py:416
  119.0 0.0 copy-done.9
  119.1 0.0 copy-done.2
  119.1 0.2 fusion.61
  119.3 8.9 %convolution_convert_fusion.2 = bf16[96,16,192]{2,0,1:T(8,128)(2,1)S(1)} fusion(bf16[2048,16,192]{0,2,1:T(8,128)(2,1)} %param.33, bf16[96,2048]{1,0:T(8,128)(2,1)S(1)} %copy-done.2, f32[96]{0:T(128)S(1)} %add_rsqrt_fusion.1), kind=kOutput, calls=%fused_computation.36 | convolution fusion | flops 1208844288 | bytes 13566336 | tf_op jit(solution)/shard_map/bd,dhc->bhc/dot_general | solution.py:37
  128.1 0.0 copy-start.7
  128.2 0.1 slice_convert_fusion
  128.2 0.3 subtract_convert_fusion
  128.6 1.2 copy-done.7
  129.7 0.6 fusion.27
  130.3 0.3 pad_maximum_fusion.1
  130.6 11.3 %fusion.10 = f32[96,16,256]{2,1,0:T(8,128)S(1)} fusion(bf16[96,256,576]{1,2,0:T(8,128)(2,1)} %param.25, bf16[96,16,576]{2,0,1:T(8,128)(2,1)S(1)} %pad_maximum_fusion.1), kind=kOutput, calls=%fused_computation.14 | convolution fusion | flops 452984832 | bytes 31653888 | tf_op jit(solution)/shard_map/bhc,bpc->bhp/dot_general | solution.py:41
  142.0 0.6 fusion.107
  142.6 0.1 copy.47
  142.7 0.1 eq.48
  142.7 1.0 fusion.76
  143.7 12.8 %fusion.19 = bf16[96,16,512]{2,1,0:T(8,128)(2,1)} fusion(bf16[96,256,576]{1,2,0:T(8,128)(2,1)} %param.25, f32[96,16]{1,0:T(8,128)S(1)} %fusion.107, f32[96,16,256]{2,1,0:T(8,128)S(1)} %fusion.10, pred[96,256]{1,0:T(8,128)(4,1)S(1)} %iota_compare_fusion.1), kind=kOutput, calls=%fused_computation.23 | convolution fusion | flops 405407488 | bytes 28342272 | tf_op jit(solution)/shard_map/bhp,bpl->bhl/dot_general | solution.py:44
  156.5 7.9 %fusion.57 = (f32[96]{0:T(128)S(1)}, bf16[96,2048]{1,0:T(8,128)(2,1)S(1)}) fusion(bf16[16,128,2048]{2,1,0:T(8,128)(2,1)} %param.36, bf16[16,512,128]{2,1,0:T(8,128)(2,1)} %param.35, bf16[96,16,512]{2,1,0:T(8,128)(2,1)} %fusion.19, bf16[96,2048]{1,0:T(8,128)(2,1)S(1)} %copy-done.2), kind=kOutput, calls=%fused_computation.63 | convolution fusion | flops 1008009088 | bytes 12845440 | tf_op jit(solution)/shard_map/bhv,hvd->bd/dot_general | solution.py:46
  164.4 0.9 fusion.58.refs_0_
  165.3 54.5 %dense.1 = f32[96,2048]{1,0:T(8,128)} custom-call(bf16[96,2048]{1,0:T(8,128)(2,1)} %fusion.58.refs_0_, bf16[96,2048]{1,0:T(8,128)(2,1)} %copy-done, bf16[5472,2048]{1,0:T(8,128)(2,1)} %bitcast.72, bf16[5472,2048]{1,0:T(8,128)(2,1)} %bitcast.73, bf16[5472,2048]{1,0:T(8,128)(2,1)} %refs_4_.3), custom_call_target="tpu_custom_call" | custom-call | flops 12910067712 | bytes 67239936 | tf_op jit(solution)/shard_map/dense/pallas_call | solution.py:362
  219.8 0.0 all-to-all-done
  219.8 0.0 copy-start.4
  219.9 4.4 %fusion.48 = f32[288,2048]{1,0:T(8,128)S(1)} fusion(bf16[1152,2048]{1,0:T(8,128)(2,1)} %bitcast.17, bf16[96,1152]{0,1:T(8,128)(2,1)S(1)} %get-tuple-element.14, bf16[96,1152]{0,1:T(8,128)(2,1)} %get-tuple-element.15, bf16[96,1152]{0,1:T(8,128)(2,1)S(1)} %get-tuple-element.13), kind=kOutput, calls=%fused_computation.53 | convolution fusion | flops 1360945152 | bytes 7741440 | tf_op jit(solution)/shard_map/dot_general | solution.py:391
  224.2 1.1 fusion.65
  (19 shorter events, 0.1 us)
Async XLA Ops:
  2.6 9.2 %copy-start.6 = (bf16[16,128,512]{2,1,0:T(8,128)(2,1)S(1)}, bf16[16,128,512]{2,1,0:T(8,128)(2,1)}, u32[]{:S(2)}) copy-start(bf16[16,128,512]{2,1,0:T(8,128)(2,1)} %param.30) | copy-start | bytes 6291460
  25.5 12.6 %copy-start.1 = (bf16[96,2048]{1,0:T(8,128)(2,1)S(1)}, bf16[96,2048]{1,0:T(8,128)(2,1)}, u32[]{:S(2)}) copy-start(bf16[96,2048]{1,0:T(8,128)(2,1)} %param.23) | copy-start | bytes 1179652
  38.0 7.9 %copy-start.8 = (s32[96,6]{0,1:T(8,128)S(1)}, s32[96,6]{0,1:T(8,128)}, u32[]{:S(2)}) copy-start(s32[96,6]{0,1:T(8,128)} %param.27) | copy-start | bytes 6916
  45.9 1.2 copy-start.3
  115.3 3.7 %copy-start.9 = (f32[96,6]{0,1:T(8,128)S(1)}, f32[96,6]{0,1:T(8,128)}, u32[]{:S(2)}) copy-start(f32[96,6]{0,1:T(8,128)} %param.28) | copy-start | bytes 6916
  115.3 3.8 %copy-start.2 = (bf16[96,2048]{1,0:T(8,128)(2,1)S(1)}, bf16[96,2048]{1,0:T(8,128)(2,1)}, u32[]{:S(2)}) copy-start(bf16[96,2048]{1,0:T(8,128)(2,1)} %get-tuple-element.7) | copy-start | bytes 1179652
  115.3 104.5 %all-to-all-start = ((bf16[16,72,2048]{2,1,0:T(8,128)(2,1)}), bf16[16,72,2048]{2,1,0:T(8,128)(2,1)}, u32[]{:S(2)}, u32[]{:S(2)}) async-start(bf16[16,72,2048]{2,1,0:T(8,128)(2,1)} %bitcast.74), calls=%async_computation | async-start | bytes 9437184 | tf_op jit(solution)/shard_map/all_to_all | solution.py:416
  128.1 1.6 copy-start.7
  164.4 0.9 copy-start
  219.8 4.4 %copy-start.4 = (bf16[96,2048]{1,0:T(8,128)(2,1)S(1)}, bf16[96,2048]{1,0:T(8,128)(2,1)}, u32[]{:S(2)}) copy-start(bf16[96,2048]{1,0:T(8,128)(2,1)} %copy-done.3) | copy-start | bytes 1179652
  219.8 4.4 %copy-start.5 = (f32[96,2048]{1,0:T(8,128)S(1)}, f32[96,2048]{1,0:T(8,128)}, u32[]{:S(2)}) copy-start(f32[96,2048]{1,0:T(8,128)} %dense.1) | copy-start | bytes 2359300

commit v2 on v1

--- a/solution.py
+++ b/solution.py
@@ -12,38 +12,6 @@
 F32, BF16 = jnp.float32, jnp.bfloat16
 SLOT_CAP = 72
 VMEM_LIMIT = 66_000_000
-
-
-def rms_norm(vec):
-    vec32 = vec.astype(F32)
-    return (vec32 * lax.rsqrt(jnp.mean(vec32 * vec32, axis=-1, keepdims=True) + 1e-6)).astype(BF16)
-
-
-def rope_rotate(vals, pos):
-    half_dim = vals.shape[-1] // 2
-    inv_freq = 10000.0 ** (-2.0 * jnp.arange(half_dim, dtype=F32) / vals.shape[-1])
-    rot_angle = pos.astype(F32)[..., None, None] * inv_freq
-    cos_ang = jnp.cos(rot_angle)
-    sin_ang = jnp.sin(rot_angle)
-    lead_half = vals[..., :half_dim]
-    tail_half = vals[..., half_dim:]
-    return jnp.concatenate([lead_half * cos_ang - tail_half * sin_ang, tail_half * cos_ang + lead_half * sin_ang], axis=-1)
-
-
-def attention(normed, cache, kv_lens, w_q, w_uk, w_uv, w_o):
-    nope_dim = w_uk.shape[1]
-    latent = w_uk.shape[2]
-    scale = w_q.shape[2] ** -0.5
-    q_full = jnp.einsum('bd,dhc->bhc', normed, w_q, preferred_element_type=F32).astype(BF16)
-    q_rope = rope_rotate(q_full[..., nope_dim:].astype(F32), kv_lens).astype(BF16)
-    q_lat = jnp.einsum('bhn,hnl->bhl', q_full[..., :nope_dim], w_uk, preferred_element_type=F32).astype(BF16)
-    q_cat = jnp.concatenate([q_lat, q_rope], axis=-1)
-    scores = jnp.einsum('bhc,bpc->bhp', q_cat, cache, preferred_element_type=F32) * scale
-    valid = jnp.arange(cache.shape[1])[None, None, :] < kv_lens[:, None, None]
-    probs = jax.nn.softmax(jnp.where(valid, scores, -1e30), axis=-1).astype(BF16)
-    o_lat = jnp.einsum('bhp,bpl->bhl', probs, cache[:, :, :latent], preferred_element_type=F32).astype(BF16)
-    o_val = jnp.einsum('bhl,hlv->bhv', o_lat, w_uv, preferred_element_type=F32).astype(BF16)
-    return jnp.einsum('bhv,hvd->bd', o_val, w_o, preferred_element_type=F32)
 
 
 def dot_t(lhs, rhs):
@@ -369,6 +337,159 @@
     )(*args)
 
 
+GROUP = 8
+RING = 4
+
+
+def att_kernel(with_table, *refs):
+    refs = list(refs)
+    lens_ref, x_ref, cos_ref, sin_ref = refs[:4]
+    del refs[:4]
+    table_ref = refs.pop(0) if with_table else None
+    wq_hbm, uk_hbm, uv_hbm, wo_hbm, cache_hbm, h_ref, u_ref = refs[:7]
+    wq, uk, uv, wo, ring, xn_buf, q_buf, o_buf, ov_buf, w_sem, ring_sem = refs[7:]
+    tok, hid = x_ref.shape
+    heads, nope, latent = uk.shape
+    qk_dim = wq.shape[1]
+    rope = qk_dim - nope
+    scale = qk_dim ** -0.5
+    n_group = tok // GROUP
+    span = latent + rope
+
+    def head_copy(quad):
+        return pltpu.make_async_copy(wq_hbm.at[pl.ds(quad * 4, 4)], wq.at[pl.ds(quad * 4, 4)], w_sem.at[quad])
+
+    def ring_copy(group, slot):
+        return pltpu.make_async_copy(cache_hbm.at[pl.ds(group * GROUP, GROUP)], ring.at[slot], ring_sem.at[slot])
+
+    uk_cp = pltpu.make_async_copy(uk_hbm, uk, w_sem.at[4])
+    uv_cp = pltpu.make_async_copy(uv_hbm, uv, w_sem.at[5])
+    wo_cp = pltpu.make_async_copy(wo_hbm, wo, w_sem.at[6])
+    head_copy(0).start()
+    uk_cp.start()
+    for quad in range(1, heads // 4):
+        head_copy(quad).start()
+    for group in range(RING):
+        ring_copy(group, group).start()
+
+    def norm(val):
+        return (val * lax.rsqrt(jnp.mean(val * val, axis=-1, keepdims=True) + 1e-6)).astype(BF16)
+
+    xn_buf[...] = norm(x_ref[...].astype(F32))
+    uk_cp.wait()
+    lane = lax.broadcasted_iota(jnp.int32, (tok, 128), 1)
+    first_half = lax.rem(lane, rope) < rope // 2
+
+    @pl.loop(0, heads // 4)
+    def _(quad):
+        head_copy(quad).wait()
+        w_nope = jnp.concatenate([wq[quad * 4 + k, pl.ds(0, nope)] for k in range(4)], axis=0)
+        w_rope = jnp.concatenate([wq[quad * 4 + k, pl.ds(nope, rope)] for k in range(4)], axis=0)
+        q_nope = dot_t(xn_buf[...], w_nope).astype(BF16)
+        q_rope = dot_t(xn_buf[...], w_rope).astype(BF16).astype(F32)
+        for k in range(4):
+            q_lat = dot_n(q_nope[:, k * nope:(k + 1) * nope], uk[quad * 4 + k]).astype(BF16).astype(F32)
+            for j in range(latent // 128):
+                q_buf[j, pl.ds(quad * 4 + k, tok, stride=heads)] = q_lat[:, j * 128:(j + 1) * 128]
+        for k in range(2):
+            val = q_rope[:, k * 128:(k + 1) * 128]
+            swap = jnp.where(first_half, pltpu.roll(val, 128 - rope // 2, 1), pltpu.roll(val, rope // 2, 1))
+            rot = (val * cos_ref[...] + swap * sin_ref[...]).astype(BF16).astype(F32)
+            q_buf[latent // 128, pl.ds(quad * 4 + 2 * k, tok, stride=heads)] = rot
+            q_buf[latent // 128, pl.ds(quad * 4 + 2 * k + 1, tok, stride=heads)] = pltpu.roll(rot, rope, 1)
+
+    place = lax.broadcasted_iota(jnp.int32, (heads, cache_hbm.shape[2]), 1)
+
+    @pl.loop(0, n_group)
+    def _(group):
+        slot = lax.rem(group, RING)
+        ring_copy(group, slot).wait()
+        for k in range(GROUP):
+            t = group * GROUP + k
+            rows = pl.ds(pl.multiple_of(t * heads, heads), heads)
+            q_cat = jnp.concatenate([q_buf[j, rows] for j in range(latent // 128 + 1)], axis=1)[:, :span].astype(BF16)
+            score = dot_n(q_cat, ring[slot, k]) * scale
+            score = jnp.where(place < lens_ref[t], score, -1e30)
+            top = jnp.max(score, axis=1, keepdims=True)
+            num = jnp.exp(score - top)
+            prob = (num * (1.0 / jnp.sum(num, axis=1, keepdims=True))).astype(BF16)
+            o_lat = dot_t(prob, ring[slot, k, pl.ds(0, latent)])
+            for j in range(latent // 128):
+                o_buf[j, rows] = o_lat[:, j * 128:(j + 1) * 128]
+
+        @pl.when(group + RING < n_group)
+        def _():
+            ring_copy(group + RING, slot).start()
+
+        @pl.when(group == 4)
+        def _():
+            uv_cp.start()
+            wo_cp.start()
+
+    uv_cp.wait()
+
+    @pl.loop(0, heads)
+    def _(h):
+        o_lat = jnp.concatenate([o_buf[j, pl.ds(h, tok, stride=heads)] for j in range(latent // 128)], axis=1).astype(BF16)
+        vals = dot_n(o_lat, uv[h]).astype(BF16)
+        ov_buf[:, pl.ds(pl.multiple_of(h * nope, nope), nope)] = vals
+
+    wo_cp.wait()
+    for off in range(0, hid, 512):
+        cols = pl.ds(off, 512)
+        att = dot_n(ov_buf[...], wo[:, cols])
+        h_ref[:, cols] = (x_ref[:, cols].astype(F32) + att).astype(BF16)
+    u_ref[:, pl.ds(0, hid)] = norm(h_ref[...].astype(F32))
+    if with_table:
+        u_ref[:, pl.ds(hid, 128)] = table_ref[...]
+
+
+def att_call(x, cache, kv_lens, cos, sin, w_q, w_uk, w_uv, w_o, table=None):
+    tok, hid = x.shape
+    heads, nope, latent = w_uk.shape
+    val_dim = w_uv.shape[2]
+    assert val_dim == nope
+    qk_dim = w_q.shape[2]
+    pos = cache.shape[1]
+    span = cache.shape[2]
+    with_table = table is not None
+    vmem, hbm = pl.BlockSpec(memory_space=pltpu.VMEM), pl.BlockSpec(memory_space=pl.ANY)
+    smem = pl.BlockSpec(memory_space=pltpu.SMEM)
+    args = [kv_lens, x, cos, sin] + ([table] if with_table else [])
+    args += [w_q.transpose(1, 2, 0), w_uk, w_uv, w_o.reshape(heads * val_dim, hid), cache.transpose(0, 2, 1)]
+    width = hid + (128 if with_table else 0)
+    return pl.pallas_call(
+        functools.partial(att_kernel, with_table),
+        out_shape=[jax.ShapeDtypeStruct((tok, hid), BF16), jax.ShapeDtypeStruct((tok, width), BF16)],
+        in_specs=[smem] + [vmem] * (4 if with_table else 3) + [hbm] * 5,
+        out_specs=[vmem, vmem],
+        scratch_shapes=[
+            pltpu.VMEM((heads, qk_dim, hid), BF16),
+            pltpu.VMEM((heads, nope, latent), BF16),
+            pltpu.VMEM((heads, latent, val_dim), BF16),
+            pltpu.VMEM((heads * val_dim, hid), BF16),
+            pltpu.VMEM((RING, GROUP, span, pos), BF16),
+            pltpu.VMEM((tok, hid), BF16),
+            pltpu.VMEM((latent // 128 + 1, tok * heads, 128), F32),
+            pltpu.VMEM((latent // 128, tok * heads, 128), F32),
+            pltpu.VMEM((tok, heads * val_dim), BF16),
+            pltpu.SemaphoreType.DMA((7,)),
+            pltpu.SemaphoreType.DMA((RING,)),
+        ],
+        compiler_params=pltpu.CompilerParams(vmem_limit_bytes=VMEM_LIMIT),
+        cost_estimate=pl.CostEstimate(flops=6 * tok * hid * 3072, bytes_accessed=54_000_000, transcendentals=0),
+        name='latent_attention',
+    )(*args)
+
+
+def rope_tables(kv_lens, rope):
+    half = rope // 2
+    inv_freq = 10000.0 ** (-2.0 * jnp.arange(half, dtype=F32) / rope)
+    angle = kv_lens.astype(F32)[:, None] * inv_freq
+    cos, sin = jnp.cos(angle), jnp.sin(angle)
+    return jnp.concatenate([cos] * 4, axis=1), jnp.concatenate([-sin, sin, -sin, sin], axis=1)
+
+
 def slot_ranks(route_ids, n_dev):
     tok = route_ids.shape[0]
     member = jnp.any(route_ids[:, :, None] == jnp.arange(n_dev)[None, None, :], axis=1)
@@ -407,17 +528,14 @@
 
     def body(hidden_in, cache0, cache1, kv_lens, route_ids, route_wts, att0_q, att0_uk, att0_uv, att0_o, att1_q, att1_uk, att1_uv, att1_o, ffn0_gate, ffn0_up, ffn0_down, ffn1_gate, ffn1_up, ffn1_down, exp_gate, exp_up, exp_down):
         ranks = slot_ranks(route_ids, n_dev)
-        att_zero = attention(rms_norm(hidden_in), cache0, kv_lens, att0_q, att0_uk, att0_uv, att0_o)
-        h_zero = (hidden_in.astype(F32) + att_zero).astype(BF16)
-        u_zero = rms_norm(h_zero)
         table = jnp.pad(ranks, ((0, 0), (0, 128 - n_dev))).astype(BF16)
-        u_ext = jnp.concatenate([u_zero, table], axis=1)
+        cos, sin = rope_tables(kv_lens, att0_q.shape[2] - att0_uk.shape[1])
+        h_zero, u_ext = att_call(hidden_in, cache0, kv_lens, cos, sin, att0_q, att0_uk, att0_uv, att0_o, table)
         f_zero, exp_out = dense_call(u_ext, h_zero, ffn0_gate.T, ffn0_up.T, ffn0_down, BF16, (exp_gate, exp_up, exp_down))
         back = lax.all_to_all(exp_out, FLAT_AXES, 0, 0, tiled=True)
-        att_one = attention(rms_norm(f_zero), cache1, kv_lens, att1_q, att1_uk, att1_uv, att1_o)
-        h_one = (f_zero.astype(F32) + att_one).astype(BF16)
-        dense_one, = dense_call(rms_norm(h_one), h_one, ffn1_gate.T, ffn1_up.T, ffn1_down, F32)
-        mix = combine(back, ranks, route_ids, route_wts, u_zero, n_dev)
+        h_one, u_one = att_call(f_zero, cache1, kv_lens, cos, sin, att1_q, att1_uk, att1_uv, att1_o)
+        dense_one, = dense_call(u_one, h_one, ffn1_gate.T, ffn1_up.T, ffn1_down, F32)
+        mix = combine(back, ranks, route_ids, route_wts, u_ext[:, :hidden_in.shape[1]], n_dev)
         return (dense_one + mix).astype(BF16)
 
     return jax.shard_map(body, mesh=mesh, in_specs=in_specs, out_specs=rows_spec, check_vma=False)

time: 230 us -> 232 us (level); the launches traced: 226 us -> 231 us
  Pallas kernels: 123 us -> 218 us
  matrix products: 87.6 us -> 4.42 us
  other arithmetic: 9.64 us -> 3.7 us
    pallas_call x0 -> x2, Pallas kernels: none -> 98.8 us  [att_call(): pl.pallas_call(functools.partial(att_kernel, with_table), out_shape=[jax....]
    dot_general x10 -> x0, matrix products: 83.1 us -> none  [the longest x2 25.3 us: attention(): jnp.einsum('bhp,bpl->bhl', probs, cache[:, :, :latent], preferred_element...]
    pallas_call x2, Pallas kernels: 123 us -> 119 us  [dense_call(): pl.pallas_call(functools.partial(ffn_kernel, with_expert, n_buf, d_buf),...]
  transfers between devices with their start and end apart: 1 -> 1, of which waited for: 0 -> 0; matrix products, arithmetic and copies ran while one was open for 20% -> 0% of each run, Pallas kernels for 24% -> 44%
where the time goes in v2:
time: 232 us; the launch traced here: 231 us
  Pallas kernels  218 us (94%)
  matrix products  4.42 us (2%)
  other arithmetic  3.7 us (2%)
  starting transfers between devices  3.63 us (2%)
    pallas_call x2, Pallas kernels, dense_call(): pl.pallas_call(functools.partial(ffn_kernel, with_expert, n_buf, d_buf),...  119 us
    pallas_call x2, Pallas kernels, att_call(): pl.pallas_call(functools.partial(att_kernel, with_table), out_shape=[jax....  98.8 us
  transfers between devices with their start and end apart: 1, of which 0 were waited for; matrix products, arithmetic and copies ran while one was open for 0% of the time, Pallas kernels for 44%

profile of v2, /device:TPU:0, one launch (start us, length us, event | category | flops | bytes accessed | tf_op | source)
XLA Modules:
  0.0 230.8 jit_solution(16614177999888532092)
XLA Ops:
  0.0 0.7 convert_element_type.26
  0.7 0.7 fusion.12
  1.4 0.1 copy.31
  1.5 0.1 fusion.16
  1.6 0.2 fusion.13
  1.9 0.6 pad.5.refs_4_
  2.5 0.8 pad_maximum_fusion
  3.3 49.4 %latent_attention.2 = (bf16[96,2048]{1,0:T(8,128)(2,1)}, bf16[96,2176]{1,0:T(8,128)(2,1)}) custom-call(s32[96]{0:T(128)} %refs_0_.3, bf16[96,2048]{1,0:T(8,128)(2,1)} %refs_1_.1, f32[96,128]{1,0:T(8,128)} %get-tuple-element.28.refs_2_, f32[96,128]{1,0:T(8,128)} %get-tuple-element.29.refs_3_, bf16[96,128]{1,0:T(8,128)(2,1)} %pad.5.refs_4_, ...), custom_call_target="tpu_custom_call" | custom-call | flops 3623878656 | bytes 54000000 | tf_op jit(solution)/shard_map/latent_attention/pallas_call | solution.py:461
  52.6 68.1 %dense_expert.1 = (bf16[96,2048]{1,0:T(8,128)(2,1)}, bf16[1152,2048]{1,0:T(8,128)(2,1)}) custom-call(bf16[96,2176]{1,0:T(8,128)(2,1)} %get-tuple-element.11.refs_0_, bf16[96,2048]{1,0:T(8,128)(2,1)} %get-tuple-element.12.refs_1_, bf16[5472,2048]{1,0:T(8,128)(2,1)} %bitcast.43, bf16[5472,2048]{1,0:T(8,128)(2,1)} %bitcast.44, bf16[5472,2048]{1,0:T(8,128)(2,1)} %refs_4_.2, ...), custom_call_target="tpu_custom_call" | custom-call | flops 32841400320 | bytes 67239936 | tf_op jit(solution)/shard_map/dense_expert/pallas_call | solution.py:330
  120.7 0.0 copy-start.2
  120.7 0.0 copy-start.3
  120.7 3.6 %all-to-all-start = ((bf16[16,72,2048]{2,1,0:T(8,128)(2,1)}), bf16[16,72,2048]{2,1,0:T(8,128)(2,1)}, u32[]{:S(2)}, u32[]{:S(2)}) async-start(bf16[16,72,2048]{2,1,0:T(8,128)(2,1)} %bitcast.42), calls=%async_computation | async-start | bytes 9437184 | tf_op jit(solution)/shard_map/all_to_all | solution.py:535
  124.4 0.1 copy.33
  124.4 0.1 eq.48
  124.5 0.0 copy-done.2
  124.6 0.0 copy-done.3
  124.6 0.2 fusion.11
  124.9 49.4 %latent_attention.3 = (bf16[96,2048]{1,0:T(8,128)(2,1)}, bf16[96,2048]{1,0:T(8,128)(2,1)}) custom-call(s32[96]{0:T(128)} %refs_0_.3, bf16[96,2048]{1,0:T(8,128)(2,1)} %get-tuple-element.13.refs_1_, f32[96,128]{1,0:T(8,128)} %get-tuple-element.28.refs_2_, f32[96,128]{1,0:T(8,128)} %get-tuple-element.29.refs_3_, bf16[16,192,2048]{2,1,0:T(8,128)(2,1)} %bitcast.39, ...), custom_call_target="tpu_custom_call" | custom-call | flops 3623878656 | bytes 54000000 | tf_op jit(solution)/shard_map/latent_attention/pallas_call | solution.py:461
  174.2 51.2 %dense.1 = f32[96,2048]{1,0:T(8,128)} custom-call(bf16[96,2048]{1,0:T(8,128)(2,1)} %get-tuple-element.14.refs_0_, bf16[96,2048]{1,0:T(8,128)(2,1)} %get-tuple-element.15.refs_1_, bf16[5472,2048]{1,0:T(8,128)(2,1)} %bitcast.36, bf16[5472,2048]{1,0:T(8,128)(2,1)} %bitcast.37, bf16[5472,2048]{1,0:T(8,128)(2,1)} %refs_4_.3), custom_call_target="tpu_custom_call" | custom-call | flops 12910067712 | bytes 67239936 | tf_op jit(solution)/shard_map/dense/pallas_call | solution.py:330
  225.4 0.0 copy-start
  225.4 0.0 copy-start.1
  225.4 0.0 all-to-all-done
  225.4 4.3 %fusion = f32[288,2048]{1,0:T(8,128)S(1)} fusion(bf16[1152,2048]{1,0:T(8,128)(2,1)} %bitcast.15, bf16[96,1152]{0,1:T(8,128)(2,1)S(1)} %get-tuple-element.18, bf16[96,1152]{0,1:T(8,128)(2,1)S(1)} %get-tuple-element.19, bf16[96,1152]{0,1:T(8,128)(2,1)S(1)} %get-tuple-element.17), kind=kOutput, calls=%fused_computation.1 | convolution fusion | flops 1360945152 | bytes 7741440 | tf_op jit(solution)/shard_map/dot_general | solution.py:512
  229.7 0.0 copy-done
  229.7 0.0 copy-done.1
  229.8 1.0 fusion.8
  (5 shorter events, 0.1 us)
Async XLA Ops:
  120.7 3.8 %copy-start.2 = (s32[96,6]{0,1:T(8,128)S(1)}, s32[96,6]{0,1:T(8,128)}, u32[]{:S(2)}) copy-start(s32[96,6]{0,1:T(8,128)} %param.27) | copy-start | bytes 6916
  120.7 3.8 %copy-start.3 = (f32[96,6]{0,1:T(8,128)S(1)}, f32[96,6]{0,1:T(8,128)}, u32[]{:S(2)}) copy-start(f32[96,6]{0,1:T(8,128)} %param.28) | copy-start | bytes 6916
  120.7 104.7 %all-to-all-start = ((bf16[16,72,2048]{2,1,0:T(8,128)(2,1)}), bf16[16,72,2048]{2,1,0:T(8,128)(2,1)}, u32[]{:S(2)}, u32[]{:S(2)}) async-start(bf16[16,72,2048]{2,1,0:T(8,128)(2,1)} %bitcast.42), calls=%async_computation | async-start | bytes 9437184 | tf_op jit(solution)/shard_map/all_to_all | solution.py:535
  225.4 4.3 %copy-start = (f32[96,2048]{1,0:T(8,128)S(1)}, f32[96,2048]{1,0:T(8,128)}, u32[]{:S(2)}) copy-start(f32[96,2048]{1,0:T(8,128)} %dense.1) | copy-start | bytes 2359300
  225.4 4.3 %copy-start.1 = (bf16[96,2176]{1,0:T(8,128)(2,1)S(1)}, bf16[96,2176]{1,0:T(8,128)(2,1)}, u32[]{:S(2)}) copy-start(bf16[96,2176]{1,0:T(8,128)(2,1)} %get-tuple-element.11.refs_0_) | copy-start | bytes 1253380

commit v3 on v2

--- a/solution.py
+++ b/solution.py
@@ -337,8 +337,9 @@
     )(*args)
 
 
-GROUP = 8
+GROUP = 16
 RING = 4
+SUB = 16
 
 
 def att_kernel(with_table, *refs):
@@ -347,7 +348,7 @@
     del refs[:4]
     table_ref = refs.pop(0) if with_table else None
     wq_hbm, uk_hbm, uv_hbm, wo_hbm, cache_hbm, h_ref, u_ref = refs[:7]
-    wq, uk, uv, wo, ring, xn_buf, q_buf, o_buf, ov_buf, w_sem, ring_sem = refs[7:]
+    wq, uk, uv, wo, ring, xn_buf, q_buf, o_buf, ov_buf, p_buf, w_sem, ring_sem = refs[7:]
     tok, hid = x_ref.shape
     heads, nope, latent = uk.shape
     qk_dim = wq.shape[1]
@@ -369,8 +370,6 @@
     uk_cp.start()
     for quad in range(1, heads // 4):
         head_copy(quad).start()
-    for group in range(RING):
-        ring_copy(group, group).start()
 
     def norm(val):
         return (val * lax.rsqrt(jnp.mean(val * val, axis=-1, keepdims=True) + 1e-6)).astype(BF16)
@@ -383,6 +382,17 @@
     @pl.loop(0, heads // 4)
     def _(quad):
         head_copy(quad).wait()
+
+        @pl.when(quad == 0)
+        def _():
+            for group in range(RING):
+                ring_copy(group, group).start()
+
+        @pl.when(quad == 3)
+        def _():
+            uv_cp.start()
+            wo_cp.start()
+
         w_nope = jnp.concatenate([wq[quad * 4 + k, pl.ds(0, nope)] for k in range(4)], axis=0)
         w_rope = jnp.concatenate([wq[quad * 4 + k, pl.ds(nope, rope)] for k in range(4)], axis=0)
         q_nope = dot_t(xn_buf[...], w_nope).astype(BF16)
@@ -404,31 +414,36 @@
     def _(group):
         slot = lax.rem(group, RING)
         ring_copy(group, slot).wait()
-        for k in range(GROUP):
-            t = group * GROUP + k
-            rows = pl.ds(pl.multiple_of(t * heads, heads), heads)
-            q_cat = jnp.concatenate([q_buf[j, rows] for j in range(latent // 128 + 1)], axis=1)[:, :span].astype(BF16)
-            score = dot_n(q_cat, ring[slot, k]) * scale
-            score = jnp.where(place < lens_ref[t], score, -1e30)
-            top = jnp.max(score, axis=1, keepdims=True)
-            num = jnp.exp(score - top)
-            prob = (num * (1.0 / jnp.sum(num, axis=1, keepdims=True))).astype(BF16)
-            o_lat = dot_t(prob, ring[slot, k, pl.ds(0, latent)])
-            for j in range(latent // 128):
-                o_buf[j, rows] = o_lat[:, j * 128:(j + 1) * 128]
+        @pl.loop(0, GROUP // SUB)
+        def _(sub):
+            for k in range(SUB):
+                at = sub * SUB + k
+                t = group * GROUP + at
+                rows = pl.ds(pl.multiple_of(t * heads, heads), heads)
+                q_cat = jnp.concatenate([q_buf[j, rows] for j in range(latent // 128 + 1)], axis=1)[:, :span].astype(BF16)
+                score = dot_n(q_cat, ring[slot, at]) * scale
+                score = jnp.where(place < lens_ref[t], score, -1e30)
+                top = jnp.max(score, axis=1, keepdims=True)
+                num = jnp.exp(score - top)
+                p_buf[at] = (num * (1.0 / jnp.sum(num, axis=1, keepdims=True))).astype(BF16)
+
+        @pl.loop(0, GROUP // SUB)
+        def _(sub):
+            for k in range(SUB):
+                at = sub * SUB + k
+                rows = pl.ds(pl.multiple_of((group * GROUP + at) * heads, heads), heads)
+                o_lat = dot_t(p_buf[at], ring[slot, at, pl.ds(0, latent)])
+                for j in range(latent // 128):
+                    o_buf[j, rows] = o_lat[:, j * 128:(j + 1) * 128]
 
         @pl.when(group + RING < n_group)
         def _():
             ring_copy(group + RING, slot).start()
 
-        @pl.when(group == 4)
-        def _():
-            uv_cp.start()
-            wo_cp.start()
 
     uv_cp.wait()
 
-    @pl.loop(0, heads)
+    @pl.loop(0, heads, unroll=8)
     def _(h):
         o_lat = jnp.concatenate([o_buf[j, pl.ds(h, tok, stride=heads)] for j in range(latent // 128)], axis=1).astype(BF16)
         vals = dot_n(o_lat, uv[h]).astype(BF16)
@@ -473,6 +488,7 @@
             pltpu.VMEM((latent // 128 + 1, tok * heads, 128), F32),
             pltpu.VMEM((latent // 128, tok * heads, 128), F32),
             pltpu.VMEM((tok, heads * val_dim), BF16),
+            pltpu.VMEM((GROUP, heads, pos), BF16),
             pltpu.SemaphoreType.DMA((7,)),
             pltpu.SemaphoreType.DMA((RING,)),
         ],

time: 232 us -> 204 us (0.88)
  Pallas kernels: 218 us -> 191 us
    pallas_call x2, Pallas kernels: 98.8 us -> 51 us  [att_call(): pl.pallas_call(functools.partial(att_kernel, with_table), out_shape=[jax....]
    pallas_call x2, Pallas kernels: 119 us -> 140 us  [dense_call(): pl.pallas_call(functools.partial(ffn_kernel, with_expert, n_buf, d_buf),...]
  transfers between devices with their start and end apart: 1 -> 1, of which waited for: 0 -> 0; matrix products, arithmetic and copies ran while one was open for 0% -> 0% of each run, Pallas kernels for 44% -> 48%
where the time goes in v3:
time: 204 us
  Pallas kernels  191 us (94%)
  matrix products  4.42 us (2%)
  other arithmetic  3.7 us (2%)
  starting transfers between devices  3.64 us (2%)
    pallas_call x2, Pallas kernels, dense_call(): pl.pallas_call(functools.partial(ffn_kernel, with_expert, n_buf, d_buf),...  140 us
    pallas_call x2, Pallas kernels, att_call(): pl.pallas_call(functools.partial(att_kernel, with_table), out_shape=[jax....  51 us
    dot_general x1, matrix products, combine(): jnp.dot(jnp.concatenate(mats, axis=0), back, preferred_element_type=F32)  4.29 us
  transfers between devices with their start and end apart: 1, of which 0 were waited for; matrix products, arithmetic and copies ran while one was open for 0% of the time, Pallas kernels for 48%

profile of v3, /device:TPU:0, one launch (start us, length us, event | category | flops | bytes accessed | tf_op | source)
XLA Modules:
  0.0 203.5 jit_solution(12892702208587075269)
XLA Ops:
  0.0 0.7 convert_element_type.26
  0.7 0.7 fusion.12
  1.4 0.1 copy.31
  1.5 0.1 fusion.16
  1.6 0.2 fusion.13
  1.9 0.6 pad.5.refs_4_
  2.5 0.8 pad_maximum_fusion
  3.3 25.5 %latent_attention.2 = (bf16[96,2048]{1,0:T(8,128)(2,1)}, bf16[96,2176]{1,0:T(8,128)(2,1)}) custom-call(s32[96]{0:T(128)} %refs_0_.3, bf16[96,2048]{1,0:T(8,128)(2,1)} %refs_1_.1, f32[96,128]{1,0:T(8,128)} %get-tuple-element.28.refs_2_, f32[96,128]{1,0:T(8,128)} %get-tuple-element.29.refs_3_, bf16[96,128]{1,0:T(8,128)(2,1)} %pad.5.refs_4_, ...), custom_call_target="tpu_custom_call" | custom-call | flops 3623878656 | bytes 54000000 | tf_op jit(solution)/shard_map/latent_attention/pallas_call | solution.py:476
  28.8 68.1 %dense_expert.1 = (bf16[96,2048]{1,0:T(8,128)(2,1)}, bf16[1152,2048]{1,0:T(8,128)(2,1)}) custom-call(bf16[96,2176]{1,0:T(8,128)(2,1)} %get-tuple-element.11.refs_0_, bf16[96,2048]{1,0:T(8,128)(2,1)} %get-tuple-element.12.refs_1_, bf16[5472,2048]{1,0:T(8,128)(2,1)} %bitcast.43, bf16[5472,2048]{1,0:T(8,128)(2,1)} %bitcast.44, bf16[5472,2048]{1,0:T(8,128)(2,1)} %refs_4_.2, ...), custom_call_target="tpu_custom_call" | custom-call | flops 32841400320 | bytes 67239936 | tf_op jit(solution)/shard_map/dense_expert/pallas_call | solution.py:330
  96.9 0.0 copy-start.2
  96.9 0.0 copy-start.3
  96.9 3.6 %all-to-all-start = ((bf16[16,72,2048]{2,1,0:T(8,128)(2,1)}), bf16[16,72,2048]{2,1,0:T(8,128)(2,1)}, u32[]{:S(2)}, u32[]{:S(2)}) async-start(bf16[16,72,2048]{2,1,0:T(8,128)(2,1)} %bitcast.42), calls=%async_computation | async-start | bytes 9437184 | tf_op jit(solution)/shard_map/all_to_all | solution.py:551
  100.5 0.1 copy.33
  100.6 0.1 eq.48
  100.7 0.0 copy-done.2
  100.7 0.0 copy-done.3
  100.8 0.2 fusion.11
  101.0 25.5 %latent_attention.3 = (bf16[96,2048]{1,0:T(8,128)(2,1)}, bf16[96,2048]{1,0:T(8,128)(2,1)}) custom-call(s32[96]{0:T(128)} %refs_0_.3, bf16[96,2048]{1,0:T(8,128)(2,1)} %get-tuple-element.13.refs_1_, f32[96,128]{1,0:T(8,128)} %get-tuple-element.28.refs_2_, f32[96,128]{1,0:T(8,128)} %get-tuple-element.29.refs_3_, bf16[16,192,2048]{2,1,0:T(8,128)(2,1)} %bitcast.39, ...), custom_call_target="tpu_custom_call" | custom-call | flops 3623878656 | bytes 54000000 | tf_op jit(solution)/shard_map/latent_attention/pallas_call | solution.py:476
  126.5 71.6 %dense.1 = f32[96,2048]{1,0:T(8,128)} custom-call(bf16[96,2048]{1,0:T(8,128)(2,1)} %get-tuple-element.14.refs_0_, bf16[96,2048]{1,0:T(8,128)(2,1)} %get-tuple-element.15.refs_1_, bf16[5472,2048]{1,0:T(8,128)(2,1)} %bitcast.36, bf16[5472,2048]{1,0:T(8,128)(2,1)} %bitcast.37, bf16[5472,2048]{1,0:T(8,128)(2,1)} %refs_4_.3), custom_call_target="tpu_custom_call" | custom-call | flops 12910067712 | bytes 67239936 | tf_op jit(solution)/shard_map/dense/pallas_call | solution.py:330
  198.1 0.0 copy-start
  198.1 0.0 copy-start.1
  198.1 0.0 all-to-all-done
  198.2 4.3 %fusion = f32[288,2048]{1,0:T(8,128)S(1)} fusion(bf16[1152,2048]{1,0:T(8,128)(2,1)} %bitcast.15, bf16[96,1152]{0,1:T(8,128)(2,1)S(1)} %get-tuple-element.18, bf16[96,1152]{0,1:T(8,128)(2,1)S(1)} %get-tuple-element.19, bf16[96,1152]{0,1:T(8,128)(2,1)S(1)} %get-tuple-element.17), kind=kOutput, calls=%fused_computation.1 | convolution fusion | flops 1360945152 | bytes 7741440 | tf_op jit(solution)/shard_map/dot_general | solution.py:528
  202.4 0.0 copy-done
  202.5 0.0 copy-done.1
  202.5 1.0 fusion.8
  (5 shorter events, 0.1 us)
Async XLA Ops:
  96.9 3.8 %copy-start.2 = (s32[96,6]{0,1:T(8,128)S(1)}, s32[96,6]{0,1:T(8,128)}, u32[]{:S(2)}) copy-start(s32[96,6]{0,1:T(8,128)} %param.27) | copy-start | bytes 6916
  96.9 3.8 %copy-start.3 = (f32[96,6]{0,1:T(8,128)S(1)}, f32[96,6]{0,1:T(8,128)}, u32[]{:S(2)}) copy-start(f32[96,6]{0,1:T(8,128)} %param.28) | copy-start | bytes 6916
  96.9 101.3 %all-to-all-start = ((bf16[16,72,2048]{2,1,0:T(8,128)(2,1)}), bf16[16,72,2048]{2,1,0:T(8,128)(2,1)}, u32[]{:S(2)}, u32[]{:S(2)}) async-start(bf16[16,72,2048]{2,1,0:T(8,128)(2,1)} %bitcast.42), calls=%async_computation | async-start | bytes 9437184 | tf_op jit(solution)/shard_map/all_to_all | solution.py:551
  198.1 4.3 %copy-start = (f32[96,2048]{1,0:T(8,128)S(1)}, f32[96,2048]{1,0:T(8,128)}, u32[]{:S(2)}) copy-start(f32[96,2048]{1,0:T(8,128)} %dense.1) | copy-start | bytes 2359300
  198.1 4.3 %copy-start.1 = (bf16[96,2176]{1,0:T(8,128)(2,1)S(1)}, bf16[96,2176]{1,0:T(8,128)(2,1)}, u32[]{:S(2)}) copy-start(bf16[96,2176]{1,0:T(8,128)(2,1)} %get-tuple-element.11.refs_0_) | copy-start | bytes 1253380

commit v4 on v3

--- a/solution.py
+++ b/solution.py
@@ -26,27 +26,27 @@
 COLS = 256
 
 
-def ffn_kernel(with_expert, n_buf, d_buf, *refs):
+def ffn_kernel(with_expert, *refs):
     refs = list(refs)
     u_ref, h_ref, gate_hbm, up_hbm, down_hbm = refs[:5]
     del refs[:5]
     if with_expert:
         eg_hbm, eu_hbm, ed_hbm = refs[:3]
         del refs[:3]
+    else:
+        mix_ref = refs.pop(0)
     out_ref = refs.pop(0)
     if with_expert:
-        eo_hbm = refs.pop(0)
-    rows_ref, act_ref, gate_ring, up_ring, down_ring, send_buf, recv_buf, part_buf = refs[:8]
-    ring_sem, down_sem, ex_send, ex_recv, rs_send, rs_recv = refs[8:14]
-    if with_expert:
-        blocks, eg, eu, ed, x_buf, h_buf, e_buf, ew_sem, eo_sem = refs[14:]
-    else:
-        blocks, = refs[14:]
+        near_hbm, far_hbm = refs[:2]
+        del refs[:2]
+    blocks, rows_ref, act_ref, gate_w, up_w, down_w, part_buf, z_out, z_in, d_out, d_in, p_out, p_in = refs[:13]
+    w_sem, ex_send, ex_recv, z_send, z_recv, d_send, d_recv, p_send, p_recv, own_sem = refs[13:23]
+    if with_expert:
+        x_buf, h_buf, e_buf, ew_sem, eo_sem = refs[23:]
 
     tok, hid = h_ref.shape
-    ff = gate_hbm.shape[0]
+    ff = gate_w.shape[0]
     n_full, tail = ff // TILE, ff % TILE
-    n_step = n_full + 1
     n_col = hid // COLS
     k_main = (ff // 256) * 256
 
@@ -54,35 +54,29 @@
     e = lax.axis_index('ep')
     y, x, c = e // 4, (e // 2) % 2, e % 2
     zn = (1 - z, e)
-    me = z * 8 + e
-    z_blk = (1 - z) * 8 + e
-
-    def ring_copies(step, slot, rows):
-        src = pl.ds(step * TILE, rows)
-        return [pltpu.make_async_copy(hbm.at[src], ring.at[slot, pl.ds(0, rows)], ring_sem.at[k, slot])
-                for k, (hbm, ring) in enumerate(((gate_hbm, gate_ring), (up_hbm, up_ring)))]
-
-    def down_copy(col, slot):
-        return pltpu.make_async_copy(down_hbm.at[:, pl.ds(col * COLS, COLS)], down_ring.at[slot], down_sem.at[slot])
-
-    for step in range(n_buf):
-        for cp in ring_copies(step, step, TILE):
+    cn = (z, e + 1 - 2 * c)
+    base = pl.multiple_of(c * ff, 16)
+
+    def tile_copies(step, rows):
+        at = pl.multiple_of(step * TILE, TILE)
+        return [pltpu.make_async_copy(hbm.at[pl.ds(pl.multiple_of(base + at, 16), rows)], buf.at[pl.ds(at, rows)], w_sem.at[k, step])
+                for k, (hbm, buf) in enumerate(((gate_hbm, gate_w), (up_hbm, up_w)))]
+
+    down_cp = pltpu.make_async_copy(down_hbm.at[pl.ds(base, ff)], down_w, w_sem.at[2, 0])
+    for step in range(n_full):
+        for cp in tile_copies(step, TILE):
             cp.start()
-    for col in range(d_buf):
-        down_copy(col, col).start()
-    if with_expert:
-        expert_cps = [pltpu.make_async_copy(s.at[0], d, ew_sem.at[k])
-                      for k, (s, d) in enumerate(((eg_hbm, eg), (eu_hbm, eu), (ed_hbm, ed)))]
-        for cp in expert_cps:
-            cp.start()
-
-    if with_expert:
+    for cp in tile_copies(n_full, tail):
+        cp.start()
+    down_cp.start()
+
+    if with_expert:
+        me = z * 8 + e
         xn = (z, e + 2 - 4 * x)
         yn = (z, e + 4 - 8 * y)
-        cn = (z, e + 1 - 2 * c)
-        peers = (zn, xn, yn, cn)
+        peers = (zn, cn, xn, yn)
     else:
-        peers = (zn,)
+        peers = (zn, cn)
     barrier = pltpu.get_barrier_semaphore()
     for peer in peers:
         pl.semaphore_signal(barrier, inc=1, device_id=peer, device_id_type=MESH)
@@ -97,19 +91,9 @@
         lo, hi = pl.ds(0, half), pl.ds(half, half)
 
         def plane(z_at):
-            base = z_at * 8
-            own = base + e
-            xb = base + e + 2 - 4 * x
-            yb = base + e + 4 - 8 * y
-            db = base + (1 - y) * 4 + (1 - x) * 2 + c
-            return own, xb, yb, db
-
-        pa = plane(z)
-        pb = plane(1 - z)
-        z_copy = remote(0, u_ref, blocks.at[me], zn)
-        z_copy.start()
-        own_cp = pltpu.make_async_copy(u_ref, blocks.at[me], eo_sem.at[0])
-        own_cp.start()
+            first = z_at * 8
+            return (first + e, first + e + 2 - 4 * x, first + e + 4 - 8 * y,
+                    first + (1 - y) * 4 + (1 - x) * 2 + c)
 
         def plane_sends(first, blks, own_src):
             own, xb, yb, db = blks
@@ -124,14 +108,6 @@
                 'c3': remote(first + 7, blocks.at[db], blocks.at[db], cn),
             }
 
-        sa = plane_sends(1, pa, u_ref)
-        sb = plane_sends(9, pb, blocks.at[z_blk])
-
-        def start_a0():
-            sa['x'].start()
-            sa['y'].start()
-            sa['c0'].start()
-
         def start_relay(s):
             s['x'].wait_recv()
             s['y'].wait_recv()
@@ -145,100 +121,162 @@
             s['yr'].wait_recv()
             s['c3'].start()
 
-        start_a0()
-        rows_ref[pl.ds(0, tok)] = u_ref[:, pl.ds(0, hid)]
-        z_copy.wait_recv()
-        rows_ref[pl.ds(tok, tok)] = blocks[z_blk, :, pl.ds(0, hid)]
+        z_blk = (1 - z) * 8 + e
+        c_blk = z * 8 + e + 1 - 2 * c
+        zc_blk = (1 - z) * 8 + e + 1 - 2 * c
+        sa = plane_sends(1, plane(z), u_ref)
+        sb = plane_sends(9, plane(1 - z), blocks.at[z_blk])
+        z_copy = remote(0, u_ref, blocks.at[me], zn)
+        ca_copy, cb_copy = sa['c0'], sb['c0']
+        own_cp = pltpu.make_async_copy(u_ref, blocks.at[me], own_sem.at[0])
+        own_cp.start()
+    else:
+        z_blk, c_blk, zc_blk = 0, 1, 2
+        z_copy = remote(0, u_ref, blocks.at[0], zn)
+        ca_copy = remote(1, u_ref, blocks.at[1], cn)
+        cb_copy = remote(2, blocks.at[0], blocks.at[2], cn)
+
+    z_copy.start()
+    ca_copy.start()
+    if with_expert:
+        sa['x'].start()
+        sa['y'].start()
+    rows_ref[pl.ds(0, tok)] = u_ref[:, pl.ds(0, hid)]
+    ca_copy.wait_recv()
+    rows_ref[pl.ds(tok, tok)] = blocks[c_blk, :, pl.ds(0, hid)]
+
+    def swiglu_tile(first, at, rows):
+        lhs = rows_ref[pl.ds(first, 2 * tok)]
+        gate_val = dot_t(lhs, gate_w[pl.ds(at, rows)])
+        up_val = dot_t(lhs, up_w[pl.ds(at, rows)])
+        act_ref[pl.ds(first, 2 * tok), pl.ds(at, rows)] = (jax.nn.silu(gate_val) * up_val).astype(BF16)
+
+    @pl.loop(0, n_full)
+    def _(step):
+        for cp in tile_copies(step, TILE):
+            cp.wait()
+        swiglu_tile(0, pl.multiple_of(step * TILE, TILE), TILE)
+
+    for cp in tile_copies(n_full, tail):
+        cp.wait()
+    swiglu_tile(0, n_full * TILE, tail)
+
+    z_copy.wait_recv()
+    cb_copy.start()
+    if with_expert:
         start_relay(sa)
         sb['x'].start()
         sb['y'].start()
-        sb['c0'].start()
-    else:
-        z_copy = remote(0, u_ref, blocks, zn)
-        z_copy.start()
-        rows_ref[pl.ds(0, tok)] = u_ref[...]
-        z_copy.wait_recv()
-        rows_ref[pl.ds(tok, tok)] = blocks[...]
-
-    def swiglu_tile(slot, rows, offset):
-        gate_val = dot_t(rows_ref[...], gate_ring[slot, pl.ds(0, rows)])
-        up_val = dot_t(rows_ref[...], up_ring[slot, pl.ds(0, rows)])
-        act_ref[:, pl.ds(offset, rows)] = (jax.nn.silu(gate_val) * up_val).astype(BF16)
+    rows_ref[pl.ds(2 * tok, tok)] = blocks[z_blk, :, pl.ds(0, hid)]
+    cb_copy.wait_recv()
+    rows_ref[pl.ds(3 * tok, tok)] = blocks[zc_blk, :, pl.ds(0, hid)]
 
     @pl.loop(0, n_full)
     def _(step):
-        slot = lax.rem(step, n_buf)
-        for cp in ring_copies(step, slot, TILE):
-            cp.wait()
-        swiglu_tile(slot, TILE, pl.multiple_of(step * TILE, TILE))
-
-        @pl.when(step + n_buf < n_full)
-        def _():
-            for cp in ring_copies(step + n_buf, slot, TILE):
-                cp.start()
-
-        @pl.when(step + n_buf == n_full)
-        def _():
-            for cp in ring_copies(n_full, slot, tail):
-                cp.start()
-
-        if with_expert:
-            @pl.when(step == 5)
-            def _():
-                start_last(sa)
-
-    tail_slot = n_full % n_buf
-    for cp in ring_copies(n_full, tail_slot, tail):
-        cp.wait()
-    swiglu_tile(tail_slot, tail, n_full * TILE)
-
-    if with_expert:
-        start_relay(sb)
-
-    def rs_copy(col):
-        return pltpu.make_async_remote_copy(src_ref=send_buf.at[col], dst_ref=recv_buf.at[col], send_sem=rs_send.at[col],
-                                            recv_sem=rs_recv.at[col], device_id=zn, device_id_type=MESH)
+        swiglu_tile(2 * tok, pl.multiple_of(step * TILE, TILE), TILE)
+
+    swiglu_tile(2 * tok, n_full * TILE, tail)
+
+    if with_expert:
+        eg, eu, ed = (gate_w.at[pl.ds(0, hid), pl.ds(0, eg_hbm.shape[2])], up_w.at[pl.ds(0, hid), pl.ds(0, eg_hbm.shape[2])],
+                      down_w.at[pl.ds(0, ed_hbm.shape[1])])
+        eg_cp, eu_cp, ed_cp = (pltpu.make_async_copy(s.at[0], d, ew_sem.at[k])
+                               for k, (s, d) in enumerate(((eg_hbm, eg), (eu_hbm, eu), (ed_hbm, ed))))
+        eg_cp.start()
+        eu_cp.start()
+        start_last(sa)
+
+    def link(src, dst, sems, rems, col, peer):
+        return pltpu.make_async_remote_copy(src_ref=src.at[col], dst_ref=dst.at[col], send_sem=sems.at[col],
+                                            recv_sem=rems.at[col], device_id=peer, device_id_type=MESH)
+
+    def z_link(col):
+        return link(z_out, z_in, z_send, z_recv, col, zn)
+
+    def d_link(col):
+        return link(d_out, d_in, d_send, d_recv, col, cn)
+
+    def p_link(col):
+        return link(p_out, p_in, p_send, p_recv, col, cn)
+
+    def down_tile(first, col):
+        cols = pl.ds(pl.multiple_of(col * COLS, COLS), COLS)
+        lhs = act_ref.at[pl.ds(first, 2 * tok)]
+        val = dot_n(lhs[:, pl.ds(0, k_main)], down_w[pl.ds(0, k_main), cols])
+        return val + dot_n(lhs[:, pl.ds(k_main, ff - k_main)], down_w[pl.ds(k_main, ff - k_main), cols])
+
+    def send_z(col):
+        d_link(col).wait_recv()
+        total = z_out[col] + d_in[col]
+        if not with_expert:
+            total += mix_ref[:, pl.ds(pl.multiple_of(col * COLS, COLS), COLS)]
+        z_out[col] = total
+        z_link(col).start()
+
+    down_cp.wait()
 
     @pl.loop(0, n_col)
     def _(col):
-        slot = lax.rem(col, d_buf)
-        down_copy(col, slot).wait()
-        val = dot_n(act_ref[:, pl.ds(0, k_main)], down_ring[slot, pl.ds(0, k_main)])
-        val += dot_n(act_ref[:, pl.ds(k_main, ff - k_main)], down_ring[slot, pl.ds(k_main, ff - k_main)])
-        send_buf[col] = val[tok:]
+        val = down_tile(2 * tok, col)
+        z_out[col] = val[:tok]
+        d_out[col] = val[tok:]
+        d_link(col).start()
+
+        @pl.when(col >= 2)
+        def _():
+            send_z(col - 2)
+
+    send_z(n_col - 2)
+    send_z(n_col - 1)
+
+    @pl.loop(0, n_col)
+    def _(col):
+        val = down_tile(0, col)
         part_buf[col] = val[:tok]
-        rs_copy(col).start()
-
-        @pl.when(col + d_buf < n_col)
-        def _():
-            down_copy(col + d_buf, slot).start()
-
-    if with_expert:
-        start_last(sb)
+        p_out[col] = val[tok:]
+        p_link(col).start()
+
+    if with_expert:
+        ed_cp.start()
         own_cp.wait()
-        for cp in expert_cps:
-            cp.wait()
-        for s in (sa, sb):
-            for k in ('c0', 'c1', 'c2', 'c3'):
-                s[k].wait_recv()
+        eg_cp.wait()
+        eu_cp.wait()
         lane = lax.broadcasted_iota(jnp.int32, (tok, 128), 1)
         slot_id = lax.broadcasted_iota(jnp.int32, (tok, 2 * SLOT_CAP), 1).astype(F32)
         q_rows = 4 * SLOT_CAP
 
-        def eo_copy(quad, buf):
-            return pltpu.make_async_copy(e_buf.at[buf], eo_hbm.at[pl.ds(pl.multiple_of(quad * q_rows, q_rows), q_rows)],
-                                         eo_sem.at[buf])
+        def eo_copy(it, buf, dst, yq):
+            return pltpu.make_async_copy(e_buf.at[buf], dst.at[pl.ds(pl.multiple_of(yq * q_rows, q_rows), q_rows)], eo_sem.at[buf])
 
         @pl.loop(0, 4)
         def _(it):
+            @pl.when(it == 0)
+            def _():
+                sa['c1'].wait_recv()
+
+            @pl.when(it == 1)
+            def _():
+                start_relay(sb)
+                sa['c2'].wait_recv()
+                sa['c3'].wait_recv()
+
+            @pl.when(it == 2)
+            def _():
+                start_last(sb)
+                sb['c1'].wait_recv()
+
+            @pl.when(it == 3)
+            def _():
+                sb['c2'].wait_recv()
+                sb['c3'].wait_recv()
+
             zq = lax.rem(z + it // 2, 2)
             yq = lax.rem(y + it, 2)
-            quad = zq * 2 + yq
             buf = lax.rem(it, 2)
             for pair in range(2):
                 acc = None
                 for k in range(2):
-                    blk = quad * 4 + pair * 2 + k
+                    blk = zq * 8 + yq * 4 + pair * 2 + k
                     table = blocks[blk, :, pl.ds(hid, 128)].astype(F32)
                     rank = jnp.sum(jnp.where(lane == me, table, 0.0), axis=1, keepdims=True)
                     want = jnp.where(rank >= 0.0, rank + k * SLOT_CAP, -1.0)
@@ -252,22 +290,35 @@
                 up_val = dot_n(x_buf[...], eu[:, pl.ds(off, width)])
                 h_buf[:, pl.ds(off, width)] = (jax.nn.silu(gate_val) * up_val).astype(BF16)
 
+            @pl.when(it == 0)
+            def _():
+                ed_cp.wait()
+
             @pl.when(it >= 2)
             def _():
-                eo_copy(0, buf).wait()
+                eo_copy(it, buf, near_hbm, yq).wait()
 
             for off in range(0, hid, 512):
                 e_buf[buf, :, pl.ds(off, 512)] = dot_n(h_buf[...], ed[:, pl.ds(off, 512)]).astype(BF16)
-            eo_copy(quad, buf).start()
-
-        eo_copy(0, 0).wait()
-        eo_copy(0, 1).wait()
+
+            @pl.when(it < 2)
+            def _():
+                eo_copy(it, buf, near_hbm, yq).start()
+
+            @pl.when(it >= 2)
+            def _():
+                eo_copy(it, buf, far_hbm, yq).start()
+
+        eo_copy(0, 0, far_hbm, 0).wait()
+        eo_copy(0, 1, far_hbm, 0).wait()
 
     @pl.loop(0, n_col)
     def _(col):
-        rs_copy(col).wait()
+        p_link(col).wait()
+        d_link(col).wait_send()
+        z_link(col).wait()
         cols = pl.ds(pl.multiple_of(col * COLS, COLS), COLS)
-        total = h_ref[:, cols].astype(F32) + (part_buf[col] + recv_buf[col])
+        total = h_ref[:, cols].astype(F32) + ((part_buf[col] + p_in[col]) + z_in[col])
         out_ref[:, cols] = total.astype(out_ref.dtype)
 
     z_copy.wait_send()
@@ -275,60 +326,45 @@
         for s in (sa, sb):
             for cp in s.values():
                 cp.wait_send()
-
-
-def dense_call(u, h, w_gate_t, w_up_t, w_down, out_dtype, expert=None):
+    else:
+        ca_copy.wait_send()
+        cb_copy.wait_send()
+
+
+def dense_call(u, h, w_gate_t, w_up_t, w_down, out_dtype, expert=None, mix=None):
     tok, hid = h.shape
-    ff = w_gate_t.shape[0]
+    ff = w_gate_t.shape[0] // 2
     width = u.shape[1]
     with_expert = expert is not None
-    n_buf, d_buf = (3, 3) if with_expert else (7, 4)
     vmem, hbm = pl.BlockSpec(memory_space=pltpu.VMEM), pl.BlockSpec(memory_space=pl.ANY)
     n_col = hid // COLS
+    n_step = ff // TILE + 1
     args = [u, h, w_gate_t, w_up_t, w_down]
     in_specs = [vmem, vmem, hbm, hbm, hbm]
     out_shape = [jax.ShapeDtypeStruct((tok, hid), out_dtype)]
     out_specs = [vmem]
-    ff_pad = (ff // TILE + 1) * TILE
-    n_ex = 17 if with_expert else 1
-    scratch = [
-        pltpu.VMEM((2 * tok, hid), BF16),
-        pltpu.VMEM((2 * tok, ff_pad), BF16),
-        pltpu.VMEM((n_buf, TILE, hid), BF16),
-        pltpu.VMEM((n_buf, TILE, hid), BF16),
-        pltpu.VMEM((d_buf, ff, COLS), BF16),
-        pltpu.VMEM((n_col, tok, COLS), F32),
-        pltpu.VMEM((n_col, tok, COLS), F32),
-        pltpu.VMEM((n_col, tok, COLS), F32),
-        pltpu.SemaphoreType.DMA((2, n_buf)),
-        pltpu.SemaphoreType.DMA((d_buf,)),
-        pltpu.SemaphoreType.DMA((n_ex,)),
-        pltpu.SemaphoreType.DMA((n_ex,)),
-        pltpu.SemaphoreType.DMA((n_col,)),
-        pltpu.SemaphoreType.DMA((n_col,)),
-    ]
+    n_ex = 17 if with_expert else 3
+    dma = pltpu.SemaphoreType.DMA
+    scratch = [pltpu.VMEM((16 if with_expert else 3, tok, width), BF16), pltpu.VMEM((4 * tok, hid), BF16),
+               pltpu.VMEM((4 * tok, n_step * TILE), BF16),
+               pltpu.VMEM((ff, hid), BF16), pltpu.VMEM((ff, hid), BF16), pltpu.VMEM((ff, hid), BF16)]
+    scratch += [pltpu.VMEM((n_col, tok, COLS), F32)] * 7
+    scratch += [dma((3, n_step)), dma((n_ex,)), dma((n_ex,))] + [dma((n_col,))] * 6 + [dma((1,))]
+    flops = 2 * 2 * tok * hid * ff * 6
     if with_expert:
         inner = expert[0].shape[2]
         args += list(expert)
         in_specs += [hbm, hbm, hbm]
-        out_shape.append(jax.ShapeDtypeStruct((16 * SLOT_CAP, hid), BF16))
-        out_specs.append(hbm)
-        scratch += [
-            pltpu.VMEM((16, tok, width), BF16),
-            pltpu.VMEM((hid, inner), BF16),
-            pltpu.VMEM((hid, inner), BF16),
-            pltpu.VMEM((inner, hid), BF16),
-            pltpu.VMEM((4 * SLOT_CAP, hid), BF16),
-            pltpu.VMEM((4 * SLOT_CAP, inner), BF16),
-            pltpu.VMEM((2, 4 * SLOT_CAP, hid), BF16),
-            pltpu.SemaphoreType.DMA((3,)),
-            pltpu.SemaphoreType.DMA((2,)),
-        ]
+        out_shape += [jax.ShapeDtypeStruct((8 * SLOT_CAP, hid), BF16)] * 2
+        out_specs += [hbm, hbm]
+        scratch += [pltpu.VMEM((4 * SLOT_CAP, hid), BF16), pltpu.VMEM((4 * SLOT_CAP, inner), BF16),
+                    pltpu.VMEM((2, 4 * SLOT_CAP, hid), BF16), dma((3,)), dma((2,))]
+        flops += 2 * 16 * SLOT_CAP * hid * inner * 3
     else:
-        scratch.append(pltpu.VMEM((tok, width), BF16))
-    flops = 2 * 2 * tok * hid * ff * 3 + (2 * 16 * SLOT_CAP * hid * 1408 * 3 if with_expert else 0)
+        args.append(mix)
+        in_specs.append(vmem)
     return pl.pallas_call(
-        functools.partial(ffn_kernel, with_expert, n_buf, d_buf),
+        functools.partial(ffn_kernel, with_expert),
         out_shape=out_shape, in_specs=in_specs, out_specs=out_specs, scratch_shapes=scratch,
         compiler_params=pltpu.CompilerParams(collective_id=0 if with_expert else 1, has_side_effects=True,
                                              vmem_limit_bytes=VMEM_LIMIT),
@@ -506,6 +542,10 @@
     return jnp.concatenate([cos] * 4, axis=1), jnp.concatenate([-sin, sin, -sin, sin], axis=1)
 
 
+def by_expert(route_ids, vals, n_dev):
+    return jnp.sum(jnp.where(route_ids[:, :, None] == jnp.arange(n_dev)[None, None, :], vals[:, :, None], 0.0), axis=1)
+
+
 def slot_ranks(route_ids, n_dev):
     tok = route_ids.shape[0]
     member = jnp.any(route_ids[:, :, None] == jnp.arange(n_dev)[None, None, :], axis=1)
@@ -514,24 +554,26 @@
     return jnp.where(member, rank, -1.0)
 
 
-def combine(back, ranks, route_ids, route_wts, normed, n_dev):
-    tok = route_ids.shape[0]
-    by_expert = jnp.sum(jnp.where(route_ids[:, :, None] == jnp.arange(n_dev)[None, None, :], route_wts[:, :, None], 0.0), axis=1)
-    zero_wt = jnp.sum(jnp.where(route_ids >= n_dev, route_wts, 0.0), axis=1)
-    pieces, rest = [], by_expert
+def mix_matrix(ranks, wts):
+    tok, n_exp = ranks.shape
+    pieces, rest = [], wts
     for _ in range(3):
         top = lax.reduce_precision(rest, 8, 7)
         pieces.append(top)
         rest = rest - top
     hit = ranks[:, :, None] == jnp.arange(SLOT_CAP, dtype=F32)[None, None, :]
-    mats = [jnp.where(hit, p[:, :, None], 0.0).astype(BF16).reshape(tok, n_dev * SLOT_CAP) for p in pieces]
-    mixed = jnp.dot(jnp.concatenate(mats, axis=0), back, preferred_element_type=F32)
-    mixed = (mixed[2 * tok:] + mixed[tok:2 * tok]) + mixed[:tok]
-    return mixed + zero_wt[:, None] * normed.astype(F32)
+    return jnp.concatenate([jnp.where(hit, p[:, :, None], 0.0).astype(BF16).reshape(tok, n_exp * SLOT_CAP) for p in pieces], axis=0)
+
+
+def apply_mix(mat, back):
+    tok = mat.shape[0] // 3
+    mixed = jnp.dot(mat, back, preferred_element_type=F32)
+    return (mixed[2 * tok:] + mixed[tok:2 * tok]) + mixed[:tok]
 
 
 def solution(mesh):
     n_dev = mesh.shape['tp'] * mesh.shape['ep']
+    n_ep = mesh.shape['ep']
     rows_spec = P(FLAT_AXES, None)
     cube_spec = P(FLAT_AXES, None, None)
     whole_spec = P(None, None, None)
@@ -543,15 +585,30 @@
                 cube_spec, cube_spec, cube_spec)
 
     def body(hidden_in, cache0, cache1, kv_lens, route_ids, route_wts, att0_q, att0_uk, att0_uv, att0_o, att1_q, att1_uk, att1_uv, att1_o, ffn0_gate, ffn0_up, ffn0_down, ffn1_gate, ffn1_up, ffn1_down, exp_gate, exp_up, exp_down):
+        hid = hidden_in.shape[1]
         ranks = slot_ranks(route_ids, n_dev)
+        wts = by_expert(route_ids, route_wts, n_dev)
+        zero_wt = jnp.sum(jnp.where(route_ids >= n_dev, route_wts, 0.0), axis=1)
         table = jnp.pad(ranks, ((0, 0), (0, 128 - n_dev))).astype(BF16)
+        mine = jnp.concatenate([ranks, wts], axis=1)
+        theirs = lax.ppermute(mine, 'tp', [(0, 1), (1, 0)])
+        low_plane = lax.axis_index('tp') == 0
+
+        def plane_matrix(pair):
+            ranks_at = jnp.where(low_plane, pair[:, :n_ep], pair[:, n_ep:n_dev])
+            wts_at = jnp.where(low_plane, pair[:, n_dev:n_dev + n_ep], pair[:, n_dev + n_ep:])
+            return mix_matrix(ranks_at, wts_at)
+
+        mat_near, mat_far = plane_matrix(mine), plane_matrix(theirs)
         cos, sin = rope_tables(kv_lens, att0_q.shape[2] - att0_uk.shape[1])
         h_zero, u_ext = att_call(hidden_in, cache0, kv_lens, cos, sin, att0_q, att0_uk, att0_uv, att0_o, table)
-        f_zero, exp_out = dense_call(u_ext, h_zero, ffn0_gate.T, ffn0_up.T, ffn0_down, BF16, (exp_gate, exp_up, exp_down))
-        back = lax.all_to_all(exp_out, FLAT_AXES, 0, 0, tiled=True)
+        f_zero, near, far = dense_call(u_ext, h_zero, ffn0_gate.T, ffn0_up.T, ffn0_down, BF16, expert=(exp_gate, exp_up, exp_down))
+        back_far = lax.all_to_all(far, 'ep', 0, 0, tiled=True)
         h_one, u_one = att_call(f_zero, cache1, kv_lens, cos, sin, att1_q, att1_uk, att1_uv, att1_o)
-        dense_one, = dense_call(u_one, h_one, ffn1_gate.T, ffn1_up.T, ffn1_down, F32)
-        mix = combine(back, ranks, route_ids, route_wts, u_ext[:, :hidden_in.shape[1]], n_dev)
+        near, back_far, h_one = lax.optimization_barrier((near, back_far, h_one))
+        back_near = lax.all_to_all(near, 'ep', 0, 0, tiled=True)
+        dense_one, = dense_call(u_one, h_one, ffn1_gate.T, ffn1_up.T, ffn1_down, F32, mix=apply_mix(mat_far, back_far))
+        mix = apply_mix(mat_near, back_near) + zero_wt[:, None] * u_ext[:, :hid].astype(F32)
         return (dense_one + mix).astype(BF16)
 
     return jax.shard_map(body, mesh=mesh, in_specs=in_specs, out_specs=rows_spec, check_vma=False)

time: 204 us -> 184 us (0.902)
  Pallas kernels: 191 us -> 159 us
  starting transfers between devices: 3.64 us -> 9.56 us
  waiting for transfers between devices: 0.01 us -> 2.43 us
    pallas_call x2, Pallas kernels: 140 us -> 108 us  [dense_call(): pl.pallas_call(functools.partial(ffn_kernel, with_expert), out_shape=out_...]
    all_to_all x1 -> x2, starting transfers between devices: 3.64 us -> 8.98 us  [the longest x1 4.6 us: body(): back_near = lax.all_to_all(near, 'ep', 0, 0, tiled=True)]
    all_to_all x1 -> x2, waiting for transfers between devices: 0.01 us -> 2.42 us  [the longest x1 2.41 us: body(): back_far = lax.all_to_all(far, 'ep', 0, 0, tiled=True)]
    dot_general x1 -> x2, matrix products: 4.29 us -> 5.84 us  [apply_mix(): mixed = jnp.dot(mat, back, preferred_element_type=F32)]
  transfers between devices with their start and end apart: 1 -> 3, of which waited for: 0 -> 1; matrix products, arithmetic and copies ran while one was open for 0% -> 3% of each run, Pallas kernels for 48% -> 38%
where the time goes in v4:
time: 184 us
  Pallas kernels  159 us (86%)
  starting transfers between devices  9.56 us (5%)
  matrix products  5.98 us (3%)
  other arithmetic  5.06 us (3%)
  waiting for transfers between devices  2.43 us (1%)
    pallas_call x2, Pallas kernels, dense_call(): pl.pallas_call(functools.partial(ffn_kernel, with_expert), out_shape=out_...  108 us
    pallas_call x2, Pallas kernels, att_call(): pl.pallas_call(functools.partial(att_kernel, with_table), out_shape=[jax....  51 us
    dot_general x2, matrix products, apply_mix(): mixed = jnp.dot(mat, back, preferred_element_type=F32)  5.84 us
    all_to_all x1, starting transfers between devices, body(): back_near = lax.all_to_all(near, 'ep', 0, 0, tiled=True)  4.6 us
    all_to_all x1, starting transfers between devices, body(): back_far = lax.all_to_all(far, 'ep', 0, 0, tiled=True)  4.37 us
  transfers between devices with their start and end apart: 3, of which 1 were waited for; matrix products, arithmetic and copies ran while one was open for 3% of the time, Pallas kernels for 38%

profile of v4, /device:TPU:0, one launch (start us, length us, event | category | flops | bytes accessed | tf_op | source)
XLA Modules:
  0.0 183.9 jit_solution(11439448484849847913)
XLA Ops:
  0.0 0.7 convert_element_type.38
  0.7 0.7 fusion.21
  1.4 0.1 copy.65
  1.5 0.1 fusion.28
  1.6 0.2 fusion.22
  1.9 0.6 pad.5.refs_4_
  2.5 0.8 pad_maximum_fusion
  3.3 25.5 %latent_attention.2 = (bf16[96,2048]{1,0:T(8,128)(2,1)}, bf16[96,2176]{1,0:T(8,128)(2,1)}) custom-call(s32[96]{0:T(128)} %refs_0_.3, bf16[96,2048]{1,0:T(8,128)(2,1)} %refs_1_.1, f32[96,128]{1,0:T(8,128)} %get-tuple-element.49.refs_2_, f32[96,128]{1,0:T(8,128)} %get-tuple-element.50.refs_3_, bf16[96,128]{1,0:T(8,128)(2,1)} %pad.5.refs_4_, ...), custom_call_target="tpu_custom_call" | custom-call | flops 3623878656 | bytes 54000000 | tf_op jit(solution)/shard_map/latent_attention/pallas_call | solution.py:512
  28.8 64.1 %dense_expert.1 = (bf16[96,2048]{1,0:T(8,128)(2,1)}, bf16[576,2048]{1,0:T(8,128)(2,1)}, bf16[576,2048]{1,0:T(8,128)(2,1)}) custom-call(bf16[96,2176]{1,0:T(8,128)(2,1)} %get-tuple-element.15.refs_0_, bf16[96,2048]{1,0:T(8,128)(2,1)} %get-tuple-element.16.refs_1_, bf16[5472,2048]{1,0:T(8,128)(2,1)} %bitcast.67, bf16[5472,2048]{1,0:T(8,128)(2,1)} %bitcast.68, ...), custom_call_target="tpu_custom_call" | custom-call | flops 32841400320 | bytes 33619968 | tf_op jit(solution)/shard_map/dense_expert/pallas_call | solution.py:366
  92.9 0.0 copy-start.2
  92.9 0.0 copy-start.3
  92.9 4.4 %all-to-all-start = ((bf16[8,72,2048]{2,1,0:T(8,128)(2,1)}), bf16[8,72,2048]{2,1,0:T(8,128)(2,1)}, u32[]{:S(2)}, u32[]{:S(2)}) async-start(bf16[8,72,2048]{2,1,0:T(8,128)(2,1)} %bitcast.66), calls=%async_computation | async-start | bytes 4718592 | tf_op jit(solution)/shard_map/all_to_all | solution.py:606
  97.3 0.0 copy-done.2
  97.3 0.0 copy-done.3
  97.3 0.1 copy.67
  97.4 0.1 pad_maximum_fusion.2
  97.5 0.6 collective-permute-start
  98.1 0.1 slice_select_fusion
  98.1 25.5 %latent_attention.3 = (bf16[96,2048]{1,0:T(8,128)(2,1)}, bf16[96,2048]{1,0:T(8,128)(2,1)}) custom-call(s32[96]{0:T(128)} %refs_0_.3, bf16[96,2048]{1,0:T(8,128)(2,1)} %get-tuple-element.17.refs_1_, f32[96,128]{1,0:T(8,128)} %get-tuple-element.49.refs_2_, f32[96,128]{1,0:T(8,128)} %get-tuple-element.50.refs_3_, bf16[16,192,2048]{2,1,0:T(8,128)(2,1)} %bitcast.62, ...), custom_call_target="tpu_custom_call" | custom-call | flops 3623878656 | bytes 54000000 | tf_op jit(solution)/shard_map/latent_attention/pallas_call | solution.py:512
  123.7 0.1 copy.73
  123.8 0.1 copy.74
  123.9 0.1 copy.72
  123.9 0.1 eq.74
  124.0 0.0 collective-permute-done
  124.0 0.1 fusion.25
  124.2 2.4 %all-to-all-done = bf16[8,72,2048]{2,1,0:T(8,128)(2,1)} async-done(((bf16[8,72,2048]{2,1,0:T(8,128)(2,1)}), bf16[8,72,2048]{2,1,0:T(8,128)(2,1)}, u32[]{:S(2)}, u32[]{:S(2)}) %all-to-all-start) | async-done | bytes 2359328 | tf_op jit(solution)/shard_map/all_to_all | solution.py:606
  126.6 4.6 %all-to-all-start.1 = ((bf16[8,72,2048]{2,1,0:T(8,128)(2,1)}), bf16[8,72,2048]{2,1,0:T(8,128)(2,1)}, u32[]{:S(2)}, u32[]{:S(2)}) async-start(bf16[8,72,2048]{2,1,0:T(8,128)(2,1)} %bitcast.65), calls=%async_computation.1 | async-start | bytes 4718592 | tf_op jit(solution)/shard_map/all_to_all | solution.py:609
  131.2 0.1 slice_select_fusion.2
  131.3 0.1 copy.75
  131.3 0.1 copy.77
  131.4 0.1 copy.76
  131.5 0.1 copy.70
  131.6 0.1 copy.68
  131.7 0.1 copy.71
  131.7 0.1 copy.69
  131.8 0.2 fusion.17
  132.1 2.9 %fusion.3 = f32[288,2048]{1,0:T(8,128)S(1)} fusion(bf16[576,2048]{1,0:T(8,128)(2,1)} %bitcast.9, bf16[96,576]{0,1:T(8,128)(2,1)S(1)} %get-tuple-element.42, bf16[96,576]{0,1:T(8,128)(2,1)S(1)} %get-tuple-element.41, bf16[96,576]{0,1:T(8,128)(2,1)S(1)} %get-tuple-element.43), kind=kOutput, calls=%fused_computation.8 | convolution fusion | flops 680472576 | bytes 5050368 | tf_op jit(solution)/shard_map/dot_general | solution.py:570
  134.9 1.0 slice_add_fusion.2.refs_5_
  136.0 43.9 %dense.1 = f32[96,2048]{1,0:T(8,128)} custom-call(bf16[96,2048]{1,0:T(8,128)(2,1)} %get-tuple-element.18.refs_0_, bf16[96,2048]{1,0:T(8,128)(2,1)} %get-tuple-element.22.refs_1_, bf16[5472,2048]{1,0:T(8,128)(2,1)} %bitcast.59, bf16[5472,2048]{1,0:T(8,128)(2,1)} %bitcast.60, bf16[5472,2048]{1,0:T(8,128)(2,1)} %refs_4_.3, f32[96,2048]{1,0:T(8,128)} %slice_add_fusion.2.refs_5_), custom_call_target="tpu_custom_call" | custom-call | flops 12910067712 | bytes 33619968 | tf_op jit(solution)/shard_map/dense/pallas_call | solution.py:366
  179.9 0.0 all-to-all-done.1
  179.9 0.0 copy-start
  179.9 0.0 copy-start.1
  179.9 3.0 %fusion.9 = f32[288,2048]{1,0:T(8,128)S(1)} fusion(bf16[576,2048]{1,0:T(8,128)(2,1)} %bitcast.21, bf16[96,576]{0,1:T(8,128)(2,1)S(1)} %get-tuple-element.34, bf16[96,576]{0,1:T(8,128)(2,1)S(1)} %get-tuple-element.35, bf16[96,576]{0,1:T(8,128)(2,1)S(1)} %get-tuple-element.33), kind=kOutput, calls=%fused_computation.14 | convolution fusion | flops 680472576 | bytes 5050368 | tf_op jit(solution)/shard_map/dot_general | solution.py:570
  182.9 0.0 copy-done
  182.9 0.0 copy-done.1
  182.9 1.0 fusion.2
  (7 shorter events, 0.1 us)
Async XLA Ops:
  92.9 4.4 %copy-start.2 = (s32[96,6]{0,1:T(8,128)S(1)}, s32[96,6]{0,1:T(8,128)}, u32[]{:S(2)}) copy-start(s32[96,6]{0,1:T(8,128)} %param.27) | copy-start | bytes 6916
  92.9 4.4 %copy-start.3 = (f32[96,6]{0,1:T(8,128)S(1)}, f32[96,6]{0,1:T(8,128)}, u32[]{:S(2)}) copy-start(f32[96,6]{0,1:T(8,128)} %param.28) | copy-start | bytes 6916
  92.9 33.7 %all-to-all-start = ((bf16[8,72,2048]{2,1,0:T(8,128)(2,1)}), bf16[8,72,2048]{2,1,0:T(8,128)(2,1)}, u32[]{:S(2)}, u32[]{:S(2)}) async-start(bf16[8,72,2048]{2,1,0:T(8,128)(2,1)} %bitcast.66), calls=%async_computation | async-start | bytes 4718592 | tf_op jit(solution)/shard_map/all_to_all | solution.py:606
  97.5 26.5 %collective-permute-start = (f32[96,32]{1,0:T(8,128)S(1)}, f32[96,32]{1,0:T(8,128)S(1)}, u32[]{:S(2)}, u32[]{:S(2)}) collective-permute-start(f32[96,32]{1,0:T(8,128)S(1)} %pad_maximum_fusion.2), channel_id=1, source_target_pairs={{0,8},{8,0},{1,9},{9,1},{2,10},{10,2},{3,11},{11,3},{4,12},{12,4},... | collective-permute-start | bytes 36872 | tf_op jit(solution)/shard_map/ppermute | solution.py:594
  126.6 53.3 %all-to-all-start.1 = ((bf16[8,72,2048]{2,1,0:T(8,128)(2,1)}), bf16[8,72,2048]{2,1,0:T(8,128)(2,1)}, u32[]{:S(2)}, u32[]{:S(2)}) async-start(bf16[8,72,2048]{2,1,0:T(8,128)(2,1)} %bitcast.65), calls=%async_computation.1 | async-start | bytes 4718592 | tf_op jit(solution)/shard_map/all_to_all | solution.py:609
  179.9 3.0 %copy-start = (f32[96,2048]{1,0:T(8,128)S(1)}, f32[96,2048]{1,0:T(8,128)}, u32[]{:S(2)}) copy-start(f32[96,2048]{1,0:T(8,128)} %dense.1) | copy-start | bytes 2359300
  179.9 3.0 %copy-start.1 = (bf16[96,2176]{1,0:T(8,128)(2,1)S(1)}, bf16[96,2176]{1,0:T(8,128)(2,1)}, u32[]{:S(2)}) copy-start(bf16[96,2176]{1,0:T(8,128)(2,1)} %get-tuple-element.15.refs_0_) | copy-start | bytes 1253380

commit v5 on v4

--- a/solution.py
+++ b/solution.py
@@ -26,6 +26,18 @@
 COLS = 256
 
 
+def exchange_copies(src, dst, send_sem, recv_sem, z, e):
+    n_ep = src.shape[0] // SLOT_CAP
+    copies = []
+    for k in range(1, n_ep):
+        peer = lax.rem(e + k, n_ep)
+        target = dst.at[e] if len(dst.shape) == 3 else dst.at[pl.ds(pl.multiple_of(e * SLOT_CAP, 8), SLOT_CAP)]
+        copies.append(pltpu.make_async_remote_copy(
+            src_ref=src.at[pl.ds(pl.multiple_of(peer * SLOT_CAP, 8), SLOT_CAP)], dst_ref=target, send_sem=send_sem.at[k],
+            recv_sem=recv_sem.at[k], device_id=(z, peer), device_id_type=MESH))
+    return copies
+
+
 def ffn_kernel(with_expert, *refs):
     refs = list(refs)
     u_ref, h_ref, gate_hbm, up_hbm, down_hbm = refs[:5]
@@ -34,7 +46,8 @@
         eg_hbm, eu_hbm, ed_hbm = refs[:3]
         del refs[:3]
     else:
-        mix_ref = refs.pop(0)
+        near_hbm, far_hbm, mat_near, mat_far, u0_ref, zero_ref = refs[:6]
+        del refs[:6]
     out_ref = refs.pop(0)
     if with_expert:
         near_hbm, far_hbm = refs[:2]
@@ -43,6 +56,8 @@
     w_sem, ex_send, ex_recv, z_send, z_recv, d_send, d_recv, p_send, p_recv, own_sem = refs[13:23]
     if with_expert:
         x_buf, h_buf, e_buf, ew_sem, eo_sem = refs[23:]
+    else:
+        near_in, far_in, n_send, n_recv, far_sem = refs[23:]
 
     tok, hid = h_ref.shape
     ff = gate_w.shape[0]
@@ -68,7 +83,6 @@
             cp.start()
     for cp in tile_copies(n_full, tail):
         cp.start()
-    down_cp.start()
 
     if with_expert:
         me = z * 8 + e
@@ -76,7 +90,8 @@
         yn = (z, e + 4 - 8 * y)
         peers = (zn, cn, xn, yn)
     else:
-        peers = (zn, cn)
+        n_ep = near_in.shape[0]
+        peers = (zn,) + tuple((z, lax.rem(e + k, n_ep)) for k in range(1, n_ep))
     barrier = pltpu.get_barrier_semaphore()
     for peer in peers:
         pl.semaphore_signal(barrier, inc=1, device_id=peer, device_id_type=MESH)
@@ -135,12 +150,18 @@
         z_copy = remote(0, u_ref, blocks.at[0], zn)
         ca_copy = remote(1, u_ref, blocks.at[1], cn)
         cb_copy = remote(2, blocks.at[0], blocks.at[2], cn)
+        near_copies = exchange_copies(near_hbm, near_in, n_send, n_recv, z, e)
+        own_cp = pltpu.make_async_copy(near_hbm.at[pl.ds(e * SLOT_CAP, SLOT_CAP)], near_in.at[e], own_sem.at[0])
+        far_cp = pltpu.make_async_copy(far_hbm, far_in, far_sem.at[0])
 
     z_copy.start()
     ca_copy.start()
     if with_expert:
         sa['x'].start()
         sa['y'].start()
+    else:
+        for cp in near_copies:
+            cp.start()
     rows_ref[pl.ds(0, tok)] = u_ref[:, pl.ds(0, hid)]
     ca_copy.wait_recv()
     rows_ref[pl.ds(tok, tok)] = blocks[c_blk, :, pl.ds(0, hid)]
@@ -157,6 +178,10 @@
             cp.wait()
         swiglu_tile(0, pl.multiple_of(step * TILE, TILE), TILE)
 
+        @pl.when(step == 2)
+        def _():
+            down_cp.start()
+
     for cp in tile_copies(n_full, tail):
         cp.wait()
     swiglu_tile(0, n_full * TILE, tail)
@@ -167,6 +192,9 @@
         start_relay(sa)
         sb['x'].start()
         sb['y'].start()
+    else:
+        own_cp.start()
+        far_cp.start()
     rows_ref[pl.ds(2 * tok, tok)] = blocks[z_blk, :, pl.ds(0, hid)]
     cb_copy.wait_recv()
     rows_ref[pl.ds(3 * tok, tok)] = blocks[zc_blk, :, pl.ds(0, hid)]
@@ -205,15 +233,21 @@
         val = dot_n(lhs[:, pl.ds(0, k_main)], down_w[pl.ds(0, k_main), cols])
         return val + dot_n(lhs[:, pl.ds(k_main, ff - k_main)], down_w[pl.ds(k_main, ff - k_main), cols])
 
+    def mixed(mat, back):
+        val = dot_n(mat[...], back)
+        return (val[2 * tok:] + val[tok:2 * tok]) + val[:tok]
+
     def send_z(col):
         d_link(col).wait_recv()
         total = z_out[col] + d_in[col]
         if not with_expert:
-            total += mix_ref[:, pl.ds(pl.multiple_of(col * COLS, COLS), COLS)]
+            total += mixed(mat_far, far_in[:, pl.ds(pl.multiple_of(col * COLS, COLS), COLS)])
         z_out[col] = total
         z_link(col).start()
 
     down_cp.wait()
+    if not with_expert:
+        far_cp.wait()
 
     @pl.loop(0, n_col)
     def _(col):
@@ -312,6 +346,11 @@
         eo_copy(0, 0, far_hbm, 0).wait()
         eo_copy(0, 1, far_hbm, 0).wait()
 
+    if not with_expert:
+        own_cp.wait()
+        for cp in near_copies:
+            cp.wait_recv()
+
     @pl.loop(0, n_col)
     def _(col):
         p_link(col).wait()
@@ -319,6 +358,9 @@
         z_link(col).wait()
         cols = pl.ds(pl.multiple_of(col * COLS, COLS), COLS)
         total = h_ref[:, cols].astype(F32) + ((part_buf[col] + p_in[col]) + z_in[col])
+        if not with_expert:
+            back = jnp.concatenate([near_in[k, :, cols] for k in range(n_ep)], axis=0)
+            total += mixed(mat_near, back) + zero_ref[...] * u0_ref[:, cols].astype(F32)
         out_ref[:, cols] = total.astype(out_ref.dtype)
 
     z_copy.wait_send()
@@ -329,9 +371,11 @@
     else:
         ca_copy.wait_send()
         cb_copy.wait_send()
-
-
-def dense_call(u, h, w_gate_t, w_up_t, w_down, out_dtype, expert=None, mix=None):
+        for cp in near_copies:
+            cp.wait_send()
+
+
+def dense_call(u, h, w_gate_t, w_up_t, w_down, expert=None, mix=None):
     tok, hid = h.shape
     ff = w_gate_t.shape[0] // 2
     width = u.shape[1]
@@ -341,7 +385,7 @@
     n_step = ff // TILE + 1
     args = [u, h, w_gate_t, w_up_t, w_down]
     in_specs = [vmem, vmem, hbm, hbm, hbm]
-    out_shape = [jax.ShapeDtypeStruct((tok, hid), out_dtype)]
+    out_shape = [jax.ShapeDtypeStruct((tok, hid), BF16)]
     out_specs = [vmem]
     n_ex = 17 if with_expert else 3
     dma = pltpu.SemaphoreType.DMA
@@ -361,8 +405,11 @@
                     pltpu.VMEM((2, 4 * SLOT_CAP, hid), BF16), dma((3,)), dma((2,))]
         flops += 2 * 16 * SLOT_CAP * hid * inner * 3
     else:
-        args.append(mix)
-        in_specs.append(vmem)
+        args += list(mix)
+        in_specs += [hbm, hbm, vmem, vmem, vmem, vmem]
+        n_ep = mix[0].shape[0] // SLOT_CAP
+        scratch += [pltpu.VMEM((n_ep, SLOT_CAP, hid), BF16), pltpu.VMEM((n_ep * SLOT_CAP, hid), BF16),
+                    dma((n_ep,)), dma((n_ep,)), dma((1,))]
     return pl.pallas_call(
         functools.partial(ffn_kernel, with_expert),
         out_shape=out_shape, in_specs=in_specs, out_specs=out_specs, scratch_shapes=scratch,
@@ -378,13 +425,18 @@
 SUB = 16
 
 
-def att_kernel(with_table, *refs):
+def att_kernel(with_table, with_far, *refs):
     refs = list(refs)
     lens_ref, x_ref, cos_ref, sin_ref = refs[:4]
     del refs[:4]
     table_ref = refs.pop(0) if with_table else None
+    far_hbm = refs.pop(0) if with_far else None
     wq_hbm, uk_hbm, uv_hbm, wo_hbm, cache_hbm, h_ref, u_ref = refs[:7]
-    wq, uk, uv, wo, ring, xn_buf, q_buf, o_buf, ov_buf, p_buf, w_sem, ring_sem = refs[7:]
+    del refs[:7]
+    back_hbm = refs.pop(0) if with_far else None
+    wq, uk, uv, wo, ring, xn_buf, q_buf, o_buf, ov_buf, p_buf, w_sem, ring_sem = refs[:12]
+    if with_far:
+        own_buf, own_sem, f_send, f_recv = refs[12:]
     tok, hid = x_ref.shape
     heads, nope, latent = uk.shape
     qk_dim = wq.shape[1]
@@ -406,6 +458,22 @@
     uk_cp.start()
     for quad in range(1, heads // 4):
         head_copy(quad).start()
+
+    if with_far:
+        z = lax.axis_index('tp')
+        e = lax.axis_index('ep')
+        n_ep = far_hbm.shape[0] // SLOT_CAP
+        barrier = pltpu.get_barrier_semaphore()
+        for k in range(1, n_ep):
+            pl.semaphore_signal(barrier, inc=1, device_id=(z, lax.rem(e + k, n_ep)), device_id_type=MESH)
+        pl.semaphore_wait(barrier, n_ep - 1)
+        far_copies = exchange_copies(far_hbm, back_hbm, f_send, f_recv, z, e)
+        for cp in far_copies:
+            cp.start()
+        own_rows = pl.ds(pl.multiple_of(e * SLOT_CAP, 8), SLOT_CAP)
+        own_in = pltpu.make_async_copy(far_hbm.at[own_rows], own_buf, own_sem.at[0])
+        own_out = pltpu.make_async_copy(own_buf, back_hbm.at[own_rows], own_sem.at[1])
+        own_in.start()
 
     def norm(val):
         return (val * lax.rsqrt(jnp.mean(val * val, axis=-1, keepdims=True) + 1e-6)).astype(BF16)
@@ -478,6 +546,9 @@
 
 
     uv_cp.wait()
+    if with_far:
+        own_in.wait()
+        own_out.start()
 
     @pl.loop(0, heads, unroll=8)
     def _(h):
@@ -493,9 +564,13 @@
     u_ref[:, pl.ds(0, hid)] = norm(h_ref[...].astype(F32))
     if with_table:
         u_ref[:, pl.ds(hid, 128)] = table_ref[...]
-
-
-def att_call(x, cache, kv_lens, cos, sin, w_q, w_uk, w_uv, w_o, table=None):
+    if with_far:
+        own_out.wait()
+        for cp in far_copies:
+            cp.wait()
+
+
+def att_call(x, cache, kv_lens, cos, sin, w_q, w_uk, w_uv, w_o, table=None, far=None):
     tok, hid = x.shape
     heads, nope, latent = w_uk.shape
     val_dim = w_uv.shape[2]
@@ -506,14 +581,25 @@
     with_table = table is not None
     vmem, hbm = pl.BlockSpec(memory_space=pltpu.VMEM), pl.BlockSpec(memory_space=pl.ANY)
     smem = pl.BlockSpec(memory_space=pltpu.SMEM)
-    args = [kv_lens, x, cos, sin] + ([table] if with_table else [])
+    with_far = far is not None
+    args = [kv_lens, x, cos, sin] + ([table] if with_table else []) + ([far] if with_far else [])
     args += [w_q.transpose(1, 2, 0), w_uk, w_uv, w_o.reshape(heads * val_dim, hid), cache.transpose(0, 2, 1)]
     width = hid + (128 if with_table else 0)
+    out_shape = [jax.ShapeDtypeStruct((tok, hid), BF16), jax.ShapeDtypeStruct((tok, width), BF16)]
+    out_specs = [vmem, vmem]
+    extra, params = [], {}
+    if with_far:
+        n_ep = far.shape[0] // SLOT_CAP
+        out_shape.append(jax.ShapeDtypeStruct(far.shape, BF16))
+        out_specs.append(hbm)
+        dma = pltpu.SemaphoreType.DMA
+        extra = [pltpu.VMEM((SLOT_CAP, hid), BF16), dma((2,)), dma((n_ep,)), dma((n_ep,))]
+        params = {'collective_id': 2, 'has_side_effects': True}
     return pl.pallas_call(
-        functools.partial(att_kernel, with_table),
-        out_shape=[jax.ShapeDtypeStruct((tok, hid), BF16), jax.ShapeDtypeStruct((tok, width), BF16)],
-        in_specs=[smem] + [vmem] * (4 if with_table else 3) + [hbm] * 5,
-        out_specs=[vmem, vmem],
+        functools.partial(att_kernel, with_table, with_far),
+        out_shape=out_shape,
+        in_specs=[smem] + [vmem] * (4 if with_table else 3) + [hbm] * (6 if with_far else 5),
+        out_specs=out_specs,
         scratch_shapes=[
             pltpu.VMEM((heads, qk_dim, hid), BF16),
             pltpu.VMEM((heads, nope, latent), BF16),
@@ -527,8 +613,8 @@
             pltpu.VMEM((GROUP, heads, pos), BF16),
             pltpu.SemaphoreType.DMA((7,)),
             pltpu.SemaphoreType.DMA((RING,)),
-        ],
-        compiler_params=pltpu.CompilerParams(vmem_limit_bytes=VMEM_LIMIT),
+        ] + extra,
+        compiler_params=pltpu.CompilerParams(vmem_limit_bytes=VMEM_LIMIT, **params),
         cost_estimate=pl.CostEstimate(flops=6 * tok * hid * 3072, bytes_accessed=54_000_000, transcendentals=0),
         name='latent_attention',
     )(*args)
@@ -563,12 +649,6 @@
         rest = rest - top
     hit = ranks[:, :, None] == jnp.arange(SLOT_CAP, dtype=F32)[None, None, :]
     return jnp.concatenate([jnp.where(hit, p[:, :, None], 0.0).astype(BF16).reshape(tok, n_exp * SLOT_CAP) for p in pieces], axis=0)
-
-
-def apply_mix(mat, back):
-    tok = mat.shape[0] // 3
-    mixed = jnp.dot(mat, back, preferred_element_type=F32)
-    return (mixed[2 * tok:] + mixed[tok:2 * tok]) + mixed[:tok]
 
 
 def solution(mesh):
@@ -585,7 +665,6 @@
                 cube_spec, cube_spec, cube_spec)
 
     def body(hidden_in, cache0, cache1, kv_lens, route_ids, route_wts, att0_q, att0_uk, att0_uv, att0_o, att1_q, att1_uk, att1_uv, att1_o, ffn0_gate, ffn0_up, ffn0_down, ffn1_gate, ffn1_up, ffn1_down, exp_gate, exp_up, exp_down):
-        hid = hidden_in.shape[1]
         ranks = slot_ranks(route_ids, n_dev)
         wts = by_expert(route_ids, route_wts, n_dev)
         zero_wt = jnp.sum(jnp.where(route_ids >= n_dev, route_wts, 0.0), axis=1)
@@ -602,13 +681,10 @@
         mat_near, mat_far = plane_matrix(mine), plane_matrix(theirs)
         cos, sin = rope_tables(kv_lens, att0_q.shape[2] - att0_uk.shape[1])
         h_zero, u_ext = att_call(hidden_in, cache0, kv_lens, cos, sin, att0_q, att0_uk, att0_uv, att0_o, table)
-        f_zero, near, far = dense_call(u_ext, h_zero, ffn0_gate.T, ffn0_up.T, ffn0_down, BF16, expert=(exp_gate, exp_up, exp_down))
-        back_far = lax.all_to_all(far, 'ep', 0, 0, tiled=True)
-        h_one, u_one = att_call(f_zero, cache1, kv_lens, cos, sin, att1_q, att1_uk, att1_uv, att1_o)
-        near, back_far, h_one = lax.optimization_barrier((near, back_far, h_one))
-        back_near = lax.all_to_all(near, 'ep', 0, 0, tiled=True)
-        dense_one, = dense_call(u_one, h_one, ffn1_gate.T, ffn1_up.T, ffn1_down, F32, mix=apply_mix(mat_far, back_far))
-        mix = apply_mix(mat_near, back_near) + zero_wt[:, None] * u_ext[:, :hid].astype(F32)
-        return (dense_one + mix).astype(BF16)
+        f_zero, near, far = dense_call(u_ext, h_zero, ffn0_gate.T, ffn0_up.T, ffn0_down, expert=(exp_gate, exp_up, exp_down))
+        h_one, u_one, back_far = att_call(f_zero, cache1, kv_lens, cos, sin, att1_q, att1_uk, att1_uv, att1_o, far=far)
+        out, = dense_call(u_one, h_one, ffn1_gate.T, ffn1_up.T, ffn1_down,
+                          mix=(near, back_far, mat_near, mat_far, u_ext, zero_wt[:, None]))
+        return out
 
     return jax.shard_map(body, mesh=mesh, in_specs=in_specs, out_specs=rows_spec, check_vma=False)

time: 184 us -> 179 us (0.973)
  starting transfers between devices: 9.56 us -> 3.35 us
  matrix products: 5.98 us -> 0.13 us
  Pallas kernels: 159 us -> 164 us
  local copies, waits for them, and re-layouts: 1.7 us -> 5.62 us
  waiting for transfers between devices: 2.43 us -> 0.01 us
    all_to_all x2 -> x0, starting transfers between devices: 8.98 us -> none  [the longest x1 4.6 us: body(): back_near = lax.all_to_all(near, 'ep', 0, 0, tiled=True)]
    dot_general x2 -> x0, matrix products: 5.84 us -> none  [apply_mix(): mixed = jnp.dot(mat, back, preferred_element_type=F32)]
    pallas_call x2, Pallas kernels: 51 us -> 55.5 us  [att_call(): pl.pallas_call(functools.partial(att_kernel, with_table, with_far), out_s...]
    ppermute x1, starting transfers between devices: 0.58 us -> 3.35 us  [body(): theirs = lax.ppermute(mine, 'tp', [(0, 1), (1, 0)])]
    all_to_all x2 -> x0, waiting for transfers between devices: 2.42 us -> none  [the longest x1 2.41 us: body(): back_far = lax.all_to_all(far, 'ep', 0, 0, tiled=True)]
    broadcast_in_dim x0 -> x13, local copies, waits for them, and re-layouts: none -> 1.88 us  [the longest x12 1.14 us: mix_matrix(): jnp.where(hit, p[:, :, None], 0.0).astype(BF16)]
  transfers between devices with their start and end apart: 3 -> 1, of which waited for: 1 -> 0; matrix products, arithmetic and copies ran while one was open for 3% -> 2% of each run, Pallas kernels for 38% -> 65%
where the time goes in v5:
time: 179 us; the launch traced here: 178 us
  Pallas kernels  164 us (92%)
  local copies, waits for them, and re-layouts  5.62 us (3%)
  other arithmetic  5.29 us (3%)
  starting transfers between devices  3.35 us (2%)
    pallas_call x2, Pallas kernels, dense_call(): pl.pallas_call(functools.partial(ffn_kernel, with_expert), out_shape=out_...  108 us
    pallas_call x2, Pallas kernels, att_call(): pl.pallas_call(functools.partial(att_kernel, with_table, with_far), out_s...  55.5 us
  transfers between devices with their start and end apart: 1, of which 0 were waited for; matrix products, arithmetic and copies ran while one was open for 2% of the time, Pallas kernels for 65%

profile of v5, /device:TPU:0, one launch (start us, length us, event | category | flops | bytes accessed | tf_op | source)
XLA Modules:
  0.0 178.3 jit_solution(15219422969360993540)
XLA Ops:
  0.0 0.7 fusion
  0.7 0.1 copy.93
  0.8 0.1 fusion.5
  0.9 0.7 select_reduce_fusion
  1.7 0.1 copy.105
  1.7 0.1 pad_maximum_fusion.4
  1.8 3.3 %collective-permute-start = (f32[96,32]{1,0:T(8,128)S(1)}, f32[96,32]{1,0:T(8,128)S(1)}, u32[]{:S(2)}, u32[]{:S(2)}) collective-permute-start(f32[96,32]{1,0:T(8,128)S(1)} %pad_maximum_fusion.4), channel_id=1, source_target_pairs={{0,8},{8,0},{1,9},{9,1},{2,10},{10,2},{3,11},{11,3},{4,12},{12,4},... | collective-permute-start | bytes 36872 | tf_op jit(solution)/shard_map/ppermute | solution.py:673
  5.2 0.7 convert_element_type.32
  5.9 0.1 slice_select_fusion.2
  5.9 0.3 fusion.1
  6.2 0.6 pad.5.refs_4_
  6.8 0.8 pad_maximum_fusion.2
  7.6 25.5 %latent_attention.2 = (bf16[96,2048]{1,0:T(8,128)(2,1)}, bf16[96,2176]{1,0:T(8,128)(2,1)}) custom-call(s32[96]{0:T(128)} %refs_0_.3, bf16[96,2048]{1,0:T(8,128)(2,1)} %refs_1_.1, f32[96,128]{1,0:T(8,128)} %get-tuple-element.46.refs_2_, f32[96,128]{1,0:T(8,128)} %get-tuple-element.47.refs_3_, bf16[96,128]{1,0:T(8,128)(2,1)} %pad.5.refs_4_, ...), custom_call_target="tpu_custom_call" | custom-call | flops 3623878656 | bytes 54000000 | tf_op jit(solution)/shard_map/latent_attention/pallas_call | solution.py:598
  33.1 61.2 %dense_expert.1 = (bf16[96,2048]{1,0:T(8,128)(2,1)}, bf16[576,2048]{1,0:T(8,128)(2,1)}, bf16[576,2048]{1,0:T(8,128)(2,1)}) custom-call(bf16[96,2176]{1,0:T(8,128)(2,1)} %get-tuple-element.13.refs_0_.refs_9_, bf16[96,2048]{1,0:T(8,128)(2,1)} %get-tuple-element.14.refs_1_, bf16[5472,2048]{1,0:T(8,128)(2,1)} %bitcast.37, bf16[5472,2048]{1,0:T(8,128)(2,1)} %bitcast.38, ...), custom_call_target="tpu_custom_call" | custom-call | flops 32841400320 | bytes 33619968 | tf_op jit(solution)/shard_map/dense_expert/pallas_call | solution.py:413
  94.3 0.0 copy-start
  94.4 0.0 copy-start.1
  94.4 30.0 %latent_attention.3 = (bf16[96,2048]{1,0:T(8,128)(2,1)}, bf16[96,2048]{1,0:T(8,128)(2,1)}, bf16[576,2048]{1,0:T(8,128)(2,1)}) custom-call(s32[96]{0:T(128)} %refs_0_.3, bf16[96,2048]{1,0:T(8,128)(2,1)} %get-tuple-element.15.refs_1_, f32[96,128]{1,0:T(8,128)} %get-tuple-element.46.refs_2_, f32[96,128]{1,0:T(8,128)} %get-tuple-element.47.refs_3_, ...), custom_call_target="tpu_custom_call" | custom-call | flops 3623878656 | bytes 54000000 | tf_op jit(solution)/shard_map/latent_attention/pallas_call | solution.py:598
  124.4 0.0 copy-done
  124.4 0.1 copy.97
  124.5 0.1 copy.98
  124.6 0.1 eq.74
  124.7 0.1 copy.95
  124.8 0.2 copy.96
  125.0 0.7 copy.114.refs_10_
  125.7 0.0 collective-permute-done
  125.7 0.1 fusion.2
  125.8 0.1 copy.108
  125.9 0.1 copy.109
  126.1 0.1 slice_select_fusion.1
  126.2 0.1 copy.106
  126.3 0.2 copy.107
  126.4 0.1 copy.99
  126.5 0.1 copy.100
  126.7 0.1 copy.101
  126.8 0.1 copy.102
  127.0 0.1 copy.103
  127.1 0.1 copy.104
  127.3 0.1 copy.110
  127.4 0.1 copy.111
  127.5 0.1 copy.112
  127.6 0.1 copy.113
  127.8 0.1 select_convert_fusion.2
  127.9 0.1 select_convert_fusion.4
  128.0 0.8 pad_maximum_fusion.refs_7_
  128.8 0.1 select_convert_fusion.1
  128.8 0.8 pad_maximum_fusion.1.refs_8_
  129.6 46.9 %dense.1 = bf16[96,2048]{1,0:T(8,128)(2,1)} custom-call(bf16[96,2048]{1,0:T(8,128)(2,1)} %get-tuple-element.17.refs_0_, bf16[96,2048]{1,0:T(8,128)(2,1)} %get-tuple-element.18.refs_1_, bf16[5472,2048]{1,0:T(8,128)(2,1)} %bitcast.22, bf16[5472,2048]{1,0:T(8,128)(2,1)} %bitcast.23, bf16[5472,2048]{1,0:T(8,128)(2,1)} %refs_4_.3, ...), custom_call_target="tpu_custom_call" | custom-call | flops 12910067712 | bytes 33619968 | tf_op jit(solution)/shard_map/dense/pallas_call | solution.py:413
  176.6 1.8 copy.118
  (15 shorter events, 0.4 us)
Async XLA Ops:
  1.8 123.9 %collective-permute-start = (f32[96,32]{1,0:T(8,128)S(1)}, f32[96,32]{1,0:T(8,128)S(1)}, u32[]{:S(2)}, u32[]{:S(2)}) collective-permute-start(f32[96,32]{1,0:T(8,128)S(1)} %pad_maximum_fusion.4), channel_id=1, source_target_pairs={{0,8},{8,0},{1,9},{9,1},{2,10},{10,2},{3,11},{11,3},{4,12},{12,4},... | collective-permute-start | bytes 36872 | tf_op jit(solution)/shard_map/ppermute | solution.py:673
  94.3 30.1 %copy-start = (s32[96,6]{0,1:T(8,128)S(1)}, s32[96,6]{0,1:T(8,128)}, u32[]{:S(2)}) copy-start(s32[96,6]{0,1:T(8,128)} %param.27) | copy-start | bytes 6916
  94.4 30.1 %copy-start.1 = (f32[96,6]{0,1:T(8,128)S(1)}, f32[96,6]{0,1:T(8,128)}, u32[]{:S(2)}) copy-start(f32[96,6]{0,1:T(8,128)} %param.28) | copy-start | bytes 6916

commit v6 on v5

--- a/solution.py
+++ b/solution.py
@@ -26,15 +26,17 @@
 COLS = 256
 
 
-def exchange_copies(src, dst, send_sem, recv_sem, z, e):
-    n_ep = src.shape[0] // SLOT_CAP
+def exchange_copies(src, dst, send_sem, recv_sem, z, e, diagonal):
+    y, x, c = e // 4, (e // 2) % 2, e % 2
     copies = []
-    for k in range(1, n_ep):
-        peer = lax.rem(e + k, n_ep)
-        target = dst.at[e] if len(dst.shape) == 3 else dst.at[pl.ds(pl.multiple_of(e * SLOT_CAP, 8), SLOT_CAP)]
+    for k in range(1, 8):
+        if (k >= 6) not in diagonal:
+            continue
+        peer = lax.rem(y + k // 4, 2) * 4 + lax.rem(x + (k // 2) % 2, 2) * 2 + lax.rem(c + k % 2, 2)
         copies.append(pltpu.make_async_remote_copy(
-            src_ref=src.at[pl.ds(pl.multiple_of(peer * SLOT_CAP, 8), SLOT_CAP)], dst_ref=target, send_sem=send_sem.at[k],
-            recv_sem=recv_sem.at[k], device_id=(z, peer), device_id_type=MESH))
+            src_ref=src.at[pl.ds(pl.multiple_of(peer * SLOT_CAP, 8), SLOT_CAP)],
+            dst_ref=dst.at[e] if len(dst.shape) == 3 else dst.at[pl.ds(pl.multiple_of(e * SLOT_CAP, 8), SLOT_CAP)],
+            send_sem=send_sem.at[k], recv_sem=recv_sem.at[k], device_id=(z, peer), device_id_type=MESH))
     return copies
 
 
@@ -46,18 +48,18 @@
         eg_hbm, eu_hbm, ed_hbm = refs[:3]
         del refs[:3]
     else:
-        near_hbm, far_hbm, mat_near, mat_far, u0_ref, zero_ref = refs[:6]
-        del refs[:6]
+        near_hbm, far_hbm, back_hbm, u0_ref, their_ref = refs[:5]
+        del refs[:5]
     out_ref = refs.pop(0)
     if with_expert:
-        near_hbm, far_hbm = refs[:2]
-        del refs[:2]
+        near_hbm, far_hbm, their_ref = refs[:3]
+        del refs[:3]
     blocks, rows_ref, act_ref, gate_w, up_w, down_w, part_buf, z_out, z_in, d_out, d_in, p_out, p_in = refs[:13]
     w_sem, ex_send, ex_recv, z_send, z_recv, d_send, d_recv, p_send, p_recv, own_sem = refs[13:23]
     if with_expert:
         x_buf, h_buf, e_buf, ew_sem, eo_sem = refs[23:]
     else:
-        near_in, far_in, n_send, n_recv, far_sem = refs[23:]
+        near_in, far_in, mat_near, mat_far, n_send, n_recv, f_send, f_recv, far_sem = refs[23:]
 
     tok, hid = h_ref.shape
     ff = gate_w.shape[0]
@@ -150,9 +152,25 @@
         z_copy = remote(0, u_ref, blocks.at[0], zn)
         ca_copy = remote(1, u_ref, blocks.at[1], cn)
         cb_copy = remote(2, blocks.at[0], blocks.at[2], cn)
-        near_copies = exchange_copies(near_hbm, near_in, n_send, n_recv, z, e)
-        own_cp = pltpu.make_async_copy(near_hbm.at[pl.ds(e * SLOT_CAP, SLOT_CAP)], near_in.at[e], own_sem.at[0])
-        far_cp = pltpu.make_async_copy(far_hbm, far_in, far_sem.at[0])
+        near_copies = exchange_copies(near_hbm, near_in, n_send, n_recv, z, e, (False, True))
+        far_copies = exchange_copies(far_hbm, far_in, f_send, f_recv, z, e, (True,))
+        own_cp = pltpu.make_async_copy(near_hbm.at[pl.ds(pl.multiple_of(e * SLOT_CAP, 8), SLOT_CAP)], near_in.at[e], own_sem.at[0])
+        far_local = []
+        for k in range(6):
+            at = lax.rem(y + k // 4, 2) * 4 + lax.rem(x + (k // 2) % 2, 2) * 2 + lax.rem(c + k % 2, 2)
+            far_local.append(pltpu.make_async_copy(back_hbm.at[pl.ds(pl.multiple_of(at * SLOT_CAP, 8), SLOT_CAP)], far_in.at[at], far_sem.at[k]))
+
+    lane = lax.broadcasted_iota(jnp.int32, (tok, 128), 1)
+
+    def fill_mix(mat, table_vals):
+        vals = table_vals.astype(F32)
+        slot = lax.broadcasted_iota(jnp.int32, (tok, SLOT_CAP), 1).astype(F32)
+        for k in range(n_ep):
+            def column(part):
+                return jnp.sum(jnp.where(lane == part * 16 + z * n_ep + k, vals, 0.0), axis=1, keepdims=True)
+            hit = slot == column(0)
+            for part in range(3):
+                mat[k, pl.ds(part * tok, tok)] = jnp.where(hit, column(part + 1), 0.0).astype(BF16)
 
     z_copy.start()
     ca_copy.start()
@@ -160,7 +178,7 @@
         sa['x'].start()
         sa['y'].start()
     else:
-        for cp in near_copies:
+        for cp in far_copies + near_copies:
             cp.start()
     rows_ref[pl.ds(0, tok)] = u_ref[:, pl.ds(0, hid)]
     ca_copy.wait_recv()
@@ -194,7 +212,10 @@
         sb['y'].start()
     else:
         own_cp.start()
-        far_cp.start()
+        for cp in far_local:
+            cp.start()
+        fill_mix(mat_near, u0_ref[:, pl.ds(hid, 128)])
+        fill_mix(mat_far, their_ref[...])
     rows_ref[pl.ds(2 * tok, tok)] = blocks[z_blk, :, pl.ds(0, hid)]
     cb_copy.wait_recv()
     rows_ref[pl.ds(3 * tok, tok)] = blocks[zc_blk, :, pl.ds(0, hid)]
@@ -233,21 +254,26 @@
         val = dot_n(lhs[:, pl.ds(0, k_main)], down_w[pl.ds(0, k_main), cols])
         return val + dot_n(lhs[:, pl.ds(k_main, ff - k_main)], down_w[pl.ds(k_main, ff - k_main), cols])
 
-    def mixed(mat, back):
-        val = dot_n(mat[...], back)
+    def mixed(mat, back, cols):
+        val = dot_n(mat[0], back[0, :, cols])
+        for k in range(1, n_ep):
+            val += dot_n(mat[k], back[k, :, cols])
         return (val[2 * tok:] + val[tok:2 * tok]) + val[:tok]
 
     def send_z(col):
         d_link(col).wait_recv()
         total = z_out[col] + d_in[col]
         if not with_expert:
-            total += mixed(mat_far, far_in[:, pl.ds(pl.multiple_of(col * COLS, COLS), COLS)])
+            total += mixed(mat_far, far_in, pl.ds(pl.multiple_of(col * COLS, COLS), COLS))
         z_out[col] = total
         z_link(col).start()
 
     down_cp.wait()
     if not with_expert:
-        far_cp.wait()
+        for cp in far_local:
+            cp.wait()
+        for cp in far_copies:
+            cp.wait_recv()
 
     @pl.loop(0, n_col)
     def _(col):
@@ -275,7 +301,7 @@
         own_cp.wait()
         eg_cp.wait()
         eu_cp.wait()
-        lane = lax.broadcasted_iota(jnp.int32, (tok, 128), 1)
+        their_ref[...] = blocks[z_blk, :, pl.ds(hid, 128)]
         slot_id = lax.broadcasted_iota(jnp.int32, (tok, 2 * SLOT_CAP), 1).astype(F32)
         q_rows = 4 * SLOT_CAP
 
@@ -350,6 +376,7 @@
         own_cp.wait()
         for cp in near_copies:
             cp.wait_recv()
+        zero_wt = jnp.sum(jnp.where((lane >= 64) & (lane < 67), u0_ref[:, pl.ds(hid, 128)].astype(F32), 0.0), axis=1, keepdims=True)
 
     @pl.loop(0, n_col)
     def _(col):
@@ -359,8 +386,7 @@
         cols = pl.ds(pl.multiple_of(col * COLS, COLS), COLS)
         total = h_ref[:, cols].astype(F32) + ((part_buf[col] + p_in[col]) + z_in[col])
         if not with_expert:
-            back = jnp.concatenate([near_in[k, :, cols] for k in range(n_ep)], axis=0)
-            total += mixed(mat_near, back) + zero_ref[...] * u0_ref[:, cols].astype(F32)
+            total += mixed(mat_near, near_in, cols) + zero_wt * u0_ref[:, cols].astype(F32)
         out_ref[:, cols] = total.astype(out_ref.dtype)
 
     z_copy.wait_send()
@@ -371,7 +397,7 @@
     else:
         ca_copy.wait_send()
         cb_copy.wait_send()
-        for cp in near_copies:
+        for cp in far_copies + near_copies:
             cp.wait_send()
 
 
@@ -399,17 +425,17 @@
         inner = expert[0].shape[2]
         args += list(expert)
         in_specs += [hbm, hbm, hbm]
-        out_shape += [jax.ShapeDtypeStruct((8 * SLOT_CAP, hid), BF16)] * 2
-        out_specs += [hbm, hbm]
+        out_shape += [jax.ShapeDtypeStruct((8 * SLOT_CAP, hid), BF16)] * 2 + [jax.ShapeDtypeStruct((tok, 128), BF16)]
+        out_specs += [hbm, hbm, vmem]
         scratch += [pltpu.VMEM((4 * SLOT_CAP, hid), BF16), pltpu.VMEM((4 * SLOT_CAP, inner), BF16),
                     pltpu.VMEM((2, 4 * SLOT_CAP, hid), BF16), dma((3,)), dma((2,))]
         flops += 2 * 16 * SLOT_CAP * hid * inner * 3
     else:
         args += list(mix)
-        in_specs += [hbm, hbm, vmem, vmem, vmem, vmem]
+        in_specs += [hbm, hbm, hbm, vmem, vmem]
         n_ep = mix[0].shape[0] // SLOT_CAP
-        scratch += [pltpu.VMEM((n_ep, SLOT_CAP, hid), BF16), pltpu.VMEM((n_ep * SLOT_CAP, hid), BF16),
-                    dma((n_ep,)), dma((n_ep,)), dma((1,))]
+        scratch += [pltpu.VMEM((n_ep, SLOT_CAP, hid), BF16)] * 2 + [pltpu.VMEM((n_ep, 3 * tok, SLOT_CAP), BF16)] * 2
+        scratch += [dma((n_ep,))] * 4 + [dma((6,))]
     return pl.pallas_call(
         functools.partial(ffn_kernel, with_expert),
         out_shape=out_shape, in_specs=in_specs, out_specs=out_specs, scratch_shapes=scratch,
@@ -425,11 +451,34 @@
 SUB = 16
 
 
+def route_table(ids, wts):
+    tok, top_k = ids.shape
+    lane = lax.broadcasted_iota(jnp.int32, (tok, 128), 1)
+    weight = jnp.zeros((tok, 128), F32)
+    member = jnp.zeros((tok, 128), F32)
+    for j in range(top_k):
+        col = ids[:, j:j + 1]
+        hit = ((lane < 64) & (col == lax.rem(lane, 16))) | ((lane >= 64) & (col >= 16))
+        weight += jnp.where(hit, wts[:, j:j + 1], 0.0)
+        member += jnp.where(hit, 1.0, 0.0)
+    before = lax.broadcasted_iota(jnp.int32, (tok, tok), 0) > lax.broadcasted_iota(jnp.int32, (tok, tok), 1)
+    rank = dot_n(jnp.where(before, 1.0, 0.0).astype(BF16), member.astype(BF16))
+    rank = jnp.where(member > 0.0, rank, -1.0)
+    first = weight.astype(BF16).astype(F32)
+    second = (weight - first).astype(BF16).astype(F32)
+    third = (weight - first) - second
+    part = jnp.where(lane < 64, lane // 16 - 1, lane - 64)
+    term = jnp.where(part == 0, first, jnp.where(part == 1, second, third))
+    return jnp.where(lane < 16, rank, jnp.where(lane < 67, term, 0.0)).astype(BF16)
+
+
 def att_kernel(with_table, with_far, *refs):
     refs = list(refs)
     lens_ref, x_ref, cos_ref, sin_ref = refs[:4]
     del refs[:4]
-    table_ref = refs.pop(0) if with_table else None
+    if with_table:
+        ids_ref, wts_ref = refs[:2]
+        del refs[:2]
     far_hbm = refs.pop(0) if with_far else None
     wq_hbm, uk_hbm, uv_hbm, wo_hbm, cache_hbm, h_ref, u_ref = refs[:7]
     del refs[:7]
@@ -467,7 +516,7 @@
         for k in range(1, n_ep):
             pl.semaphore_signal(barrier, inc=1, device_id=(z, lax.rem(e + k, n_ep)), device_id_type=MESH)
         pl.semaphore_wait(barrier, n_ep - 1)
-        far_copies = exchange_copies(far_hbm, back_hbm, f_send, f_recv, z, e)
+        far_copies = exchange_copies(far_hbm, back_hbm, f_send, f_recv, z, e, (False,))
         for cp in far_copies:
             cp.start()
         own_rows = pl.ds(pl.multiple_of(e * SLOT_CAP, 8), SLOT_CAP)
@@ -563,14 +612,14 @@
         h_ref[:, cols] = (x_ref[:, cols].astype(F32) + att).astype(BF16)
     u_ref[:, pl.ds(0, hid)] = norm(h_ref[...].astype(F32))
     if with_table:
-        u_ref[:, pl.ds(hid, 128)] = table_ref[...]
+        u_ref[:, pl.ds(hid, 128)] = route_table(ids_ref[...], wts_ref[...])
     if with_far:
         own_out.wait()
         for cp in far_copies:
             cp.wait()
 
 
-def att_call(x, cache, kv_lens, cos, sin, w_q, w_uk, w_uv, w_o, table=None, far=None):
+def att_call(x, cache, kv_lens, cos, sin, w_q, w_uk, w_uv, w_o, route=None, far=None):
     tok, hid = x.shape
     heads, nope, latent = w_uk.shape
     val_dim = w_uv.shape[2]
@@ -578,11 +627,11 @@
     qk_dim = w_q.shape[2]
     pos = cache.shape[1]
     span = cache.shape[2]
-    with_table = table is not None
+    with_table = route is not None
     vmem, hbm = pl.BlockSpec(memory_space=pltpu.VMEM), pl.BlockSpec(memory_space=pl.ANY)
     smem = pl.BlockSpec(memory_space=pltpu.SMEM)
     with_far = far is not None
-    args = [kv_lens, x, cos, sin] + ([table] if with_table else []) + ([far] if with_far else [])
+    args = [kv_lens, x, cos, sin] + (list(route) if with_table else []) + ([far] if with_far else [])
     args += [w_q.transpose(1, 2, 0), w_uk, w_uv, w_o.reshape(heads * val_dim, hid), cache.transpose(0, 2, 1)]
     width = hid + (128 if with_table else 0)
     out_shape = [jax.ShapeDtypeStruct((tok, hid), BF16), jax.ShapeDtypeStruct((tok, width), BF16)]
@@ -598,7 +647,7 @@
     return pl.pallas_call(
         functools.partial(att_kernel, with_table, with_far),
         out_shape=out_shape,
-        in_specs=[smem] + [vmem] * (4 if with_table else 3) + [hbm] * (6 if with_far else 5),
+        in_specs=[smem] + [vmem] * (5 if with_table else 3) + [hbm] * (6 if with_far else 5),
         out_specs=out_specs,
         scratch_shapes=[
             pltpu.VMEM((heads, qk_dim, hid), BF16),
@@ -621,39 +670,14 @@
 
 
 def rope_tables(kv_lens, rope):
-    half = rope // 2
-    inv_freq = 10000.0 ** (-2.0 * jnp.arange(half, dtype=F32) / rope)
-    angle = kv_lens.astype(F32)[:, None] * inv_freq
-    cos, sin = jnp.cos(angle), jnp.sin(angle)
-    return jnp.concatenate([cos] * 4, axis=1), jnp.concatenate([-sin, sin, -sin, sin], axis=1)
-
-
-def by_expert(route_ids, vals, n_dev):
-    return jnp.sum(jnp.where(route_ids[:, :, None] == jnp.arange(n_dev)[None, None, :], vals[:, :, None], 0.0), axis=1)
-
-
-def slot_ranks(route_ids, n_dev):
-    tok = route_ids.shape[0]
-    member = jnp.any(route_ids[:, :, None] == jnp.arange(n_dev)[None, None, :], axis=1)
-    before = (jnp.arange(tok)[:, None] > jnp.arange(tok)[None, :]).astype(BF16)
-    rank = jnp.dot(before, member.astype(BF16), preferred_element_type=F32)
-    return jnp.where(member, rank, -1.0)
-
-
-def mix_matrix(ranks, wts):
-    tok, n_exp = ranks.shape
-    pieces, rest = [], wts
-    for _ in range(3):
-        top = lax.reduce_precision(rest, 8, 7)
-        pieces.append(top)
-        rest = rest - top
-    hit = ranks[:, :, None] == jnp.arange(SLOT_CAP, dtype=F32)[None, None, :]
-    return jnp.concatenate([jnp.where(hit, p[:, :, None], 0.0).astype(BF16).reshape(tok, n_exp * SLOT_CAP) for p in pieces], axis=0)
+    lane = jnp.arange(128)
+    inv_freq = 10000.0 ** (-2.0 * (lane % (rope // 2)).astype(F32) / rope)
+    angle = kv_lens.astype(F32)[:, None] * inv_freq[None, :]
+    return jnp.cos(angle), jnp.where(lane % rope < rope // 2, -1.0, 1.0) * jnp.sin(angle)
 
 
 def solution(mesh):
-    n_dev = mesh.shape['tp'] * mesh.shape['ep']
-    n_ep = mesh.shape['ep']
+    assert mesh.shape['tp'] == 2 and mesh.shape['ep'] == 8
     rows_spec = P(FLAT_AXES, None)
     cube_spec = P(FLAT_AXES, None, None)
     whole_spec = P(None, None, None)
@@ -665,26 +689,11 @@
                 cube_spec, cube_spec, cube_spec)
 
     def body(hidden_in, cache0, cache1, kv_lens, route_ids, route_wts, att0_q, att0_uk, att0_uv, att0_o, att1_q, att1_uk, att1_uv, att1_o, ffn0_gate, ffn0_up, ffn0_down, ffn1_gate, ffn1_up, ffn1_down, exp_gate, exp_up, exp_down):
-        ranks = slot_ranks(route_ids, n_dev)
-        wts = by_expert(route_ids, route_wts, n_dev)
-        zero_wt = jnp.sum(jnp.where(route_ids >= n_dev, route_wts, 0.0), axis=1)
-        table = jnp.pad(ranks, ((0, 0), (0, 128 - n_dev))).astype(BF16)
-        mine = jnp.concatenate([ranks, wts], axis=1)
-        theirs = lax.ppermute(mine, 'tp', [(0, 1), (1, 0)])
-        low_plane = lax.axis_index('tp') == 0
-
-        def plane_matrix(pair):
-            ranks_at = jnp.where(low_plane, pair[:, :n_ep], pair[:, n_ep:n_dev])
-            wts_at = jnp.where(low_plane, pair[:, n_dev:n_dev + n_ep], pair[:, n_dev + n_ep:])
-            return mix_matrix(ranks_at, wts_at)
-
-        mat_near, mat_far = plane_matrix(mine), plane_matrix(theirs)
         cos, sin = rope_tables(kv_lens, att0_q.shape[2] - att0_uk.shape[1])
-        h_zero, u_ext = att_call(hidden_in, cache0, kv_lens, cos, sin, att0_q, att0_uk, att0_uv, att0_o, table)
-        f_zero, near, far = dense_call(u_ext, h_zero, ffn0_gate.T, ffn0_up.T, ffn0_down, expert=(exp_gate, exp_up, exp_down))
-        h_one, u_one, back_far = att_call(f_zero, cache1, kv_lens, cos, sin, att1_q, att1_uk, att1_uv, att1_o, far=far)
-        out, = dense_call(u_one, h_one, ffn1_gate.T, ffn1_up.T, ffn1_down,
-                          mix=(near, back_far, mat_near, mat_far, u_ext, zero_wt[:, None]))
+        h_zero, u_ext = att_call(hidden_in, cache0, kv_lens, cos, sin, att0_q, att0_uk, att0_uv, att0_o, route=(route_ids, route_wts))
+        f_zero, near, far, theirs = dense_call(u_ext, h_zero, ffn0_gate.T, ffn0_up.T, ffn0_down, expert=(exp_gate, exp_up, exp_down))
+        h_one, u_one, back = att_call(f_zero, cache1, kv_lens, cos, sin, att1_q, att1_uk, att1_uv, att1_o, far=far)
+        out, = dense_call(u_one, h_one, ffn1_gate.T, ffn1_up.T, ffn1_down, mix=(near, far, back, u_ext, theirs))
         return out
 
     return jax.shard_map(body, mesh=mesh, in_specs=in_specs, out_specs=rows_spec, check_vma=False)

time: 179 us -> 170 us (0.950)
  other arithmetic: 5.29 us -> 1.57 us
  starting transfers between devices: 3.35 us -> 0 us
    pallas_call x2, Pallas kernels: 55.5 us -> 51.5 us  [att_call(): pl.pallas_call(functools.partial(att_kernel, with_table, with_far), out_s...]
    pallas_call x2, Pallas kernels: 108 us -> 112 us  [dense_call(): pl.pallas_call(functools.partial(ffn_kernel, with_expert), out_shape=out_...]
    ppermute x1 -> x0, starting transfers between devices: 3.35 us -> none  [body(): theirs = lax.ppermute(mine, 'tp', [(0, 1), (1, 0)])]
    unnamed x5 -> x3, local copies, waits for them, and re-layouts: 1.78 us -> 4.57 us
    concatenate x4 -> x0, other arithmetic: 2.41 us -> none  [the longest x2 1.55 us: mix_matrix(): jnp.concatenate([jnp.where(hit, p[:, :, None], 0.0).astype(BF16).reshape(...]
    broadcast_in_dim x13 -> x0, local copies, waits for them, and re-layouts: 1.88 us -> none  [the longest x12 1.14 us: mix_matrix(): jnp.where(hit, p[:, :, None], 0.0).astype(BF16)]
  transfers between devices with their start and end apart: 1 -> 0, of which waited for: 0 -> 0; matrix products, arithmetic and copies ran while one was open for 2% -> 0% of each run, Pallas kernels for 65% -> 0%
where the time goes in v6:
time: 170 us
  Pallas kernels  164 us (96%)
  local copies, waits for them, and re-layouts  4.57 us (3%)
    pallas_call x2, Pallas kernels, dense_call(): pl.pallas_call(functools.partial(ffn_kernel, with_expert), out_shape=out_...  112 us
    pallas_call x2, Pallas kernels, att_call(): pl.pallas_call(functools.partial(att_kernel, with_table, with_far), out_s...  51.5 us
    unnamed x3, local copies, waits for them, and re-layouts  4.57 us

profile of v6, /device:TPU:0, one launch (start us, length us, event | category | flops | bytes accessed | tf_op | source)
XLA Modules:
  0.0 169.8 jit_solution(1517987985865331600)
XLA Ops:
  0.0 0.7 convert_element_type.10
  0.7 1.4 copy.24.refs_4_
  2.1 1.4 copy.25.refs_5_
  3.5 0.9 fusion
  4.4 25.6 %latent_attention.2 = (bf16[96,2048]{1,0:T(8,128)(2,1)}, bf16[96,2176]{1,0:T(8,128)(2,1)}) custom-call(s32[96]{0:T(128)} %refs_0_.3, bf16[96,2048]{1,0:T(8,128)(2,1)} %refs_1_.1, f32[96,128]{1,0:T(8,128)} %get-tuple-element.24.refs_2_, f32[96,128]{1,0:T(8,128)} %get-tuple-element.23.refs_3_, s32[96,6]{1,0:T(8,128)} %copy.24.refs_4_, f32[96,6]{1,0:T(8,128)} %copy.25.refs_5_, ...), custom_call_target="tpu_custom_call" | custom-call | flops 3623878656 | bytes 54000000 | tf_op jit(solution)/shard_map/latent_attention/pallas_call | solution.py:647
  30.0 64.0 %dense_expert.1 = (bf16[96,2048]{1,0:T(8,128)(2,1)}, bf16[576,2048]{1,0:T(8,128)(2,1)}, bf16[576,2048]{1,0:T(8,128)(2,1)}, bf16[96,128]{1,0:T(8,128)(2,1)}) custom-call(bf16[96,2176]{1,0:T(8,128)(2,1)} %get-tuple-element.14.refs_0_.refs_8_, bf16[96,2048]{1,0:T(8,128)(2,1)} %get-tuple-element.15.refs_1_, bf16[5472,2048]{1,0:T(8,128)(2,1)} %bitcast.18, ...), custom_call_target="tpu_custom_call" | custom-call | flops 32841400320 | bytes 33619968 | tf_op jit(solution)/shard_map/dense_expert/pallas_call | solution.py:439
  94.0 25.8 %latent_attention.3 = (bf16[96,2048]{1,0:T(8,128)(2,1)}, bf16[96,2048]{1,0:T(8,128)(2,1)}, bf16[576,2048]{1,0:T(8,128)(2,1)}) custom-call(s32[96]{0:T(128)} %refs_0_.3, bf16[96,2048]{1,0:T(8,128)(2,1)} %get-tuple-element.16.refs_1_, f32[96,128]{1,0:T(8,128)} %get-tuple-element.24.refs_2_, f32[96,128]{1,0:T(8,128)} %get-tuple-element.23.refs_3_, ...), custom_call_target="tpu_custom_call" | custom-call | flops 3623878656 | bytes 54000000 | tf_op jit(solution)/shard_map/latent_attention/pallas_call | solution.py:647
  119.8 48.2 %dense.1 = bf16[96,2048]{1,0:T(8,128)(2,1)} custom-call(bf16[96,2048]{1,0:T(8,128)(2,1)} %get-tuple-element.18.refs_0_, bf16[96,2048]{1,0:T(8,128)(2,1)} %get-tuple-element.19.refs_1_, bf16[5472,2048]{1,0:T(8,128)(2,1)} %bitcast.12, bf16[5472,2048]{1,0:T(8,128)(2,1)} %bitcast.13, bf16[5472,2048]{1,0:T(8,128)(2,1)} %refs_4_.4, ...), custom_call_target="tpu_custom_call" | custom-call | flops 12910067712 | bytes 33619968 | tf_op jit(solution)/shard_map/dense/pallas_call | solution.py:439
  168.0 1.8 %copy.27 = bf16[96,2048]{1,0:T(8,128)(2,1)} copy(bf16[96,2048]{1,0:T(8,128)(2,1)} %dense.1) | data formatting | bytes 786432
  (1 shorter events, 0.0 us)

commit v7 on v6

--- a/solution.py
+++ b/solution.py
@@ -204,6 +204,8 @@
         cp.wait()
     swiglu_tile(0, n_full * TILE, tail)
 
+    if not with_expert:
+        fill_mix(mat_far, their_ref[...])
     z_copy.wait_recv()
     cb_copy.start()
     if with_expert:
@@ -214,8 +216,6 @@
         own_cp.start()
         for cp in far_local:
             cp.start()
-        fill_mix(mat_near, u0_ref[:, pl.ds(hid, 128)])
-        fill_mix(mat_far, their_ref[...])
     rows_ref[pl.ds(2 * tok, tok)] = blocks[z_blk, :, pl.ds(0, hid)]
     cb_copy.wait_recv()
     rows_ref[pl.ds(3 * tok, tok)] = blocks[zc_blk, :, pl.ds(0, hid)]
@@ -282,12 +282,13 @@
         d_out[col] = val[tok:]
         d_link(col).start()
 
-        @pl.when(col >= 2)
+        @pl.when(col >= 1)
         def _():
-            send_z(col - 2)
-
-    send_z(n_col - 2)
+            send_z(col - 1)
+
     send_z(n_col - 1)
+    if not with_expert:
+        fill_mix(mat_near, u0_ref[:, pl.ds(hid, 128)])
 
     @pl.loop(0, n_col)
     def _(col):
@@ -345,10 +346,12 @@
                                           preferred_element_type=F32)
                     acc = got if acc is None else acc + got
                 x_buf[pl.ds(pair * 2 * SLOT_CAP, 2 * SLOT_CAP)] = acc.astype(BF16)
-            for off, width in ((0, 512), (512, 512), (1024, 384)):
+            for off, width in ((0, 512), (512, 512), (1024, 256)):
                 gate_val = dot_n(x_buf[...], eg[:, pl.ds(off, width)])
                 up_val = dot_n(x_buf[...], eu[:, pl.ds(off, width)])
                 h_buf[:, pl.ds(off, width)] = (jax.nn.silu(gate_val) * up_val).astype(BF16)
+            both = dot_n(x_buf[...], jnp.concatenate([eg[:, pl.ds(1280, 128)], eu[:, pl.ds(1280, 128)]], axis=1))
+            h_buf[:, pl.ds(1280, 128)] = (jax.nn.silu(both[:, :128]) * both[:, 128:]).astype(BF16)
 
             @pl.when(it == 0)
             def _():
@@ -411,7 +414,7 @@
     n_step = ff // TILE + 1
     args = [u, h, w_gate_t, w_up_t, w_down]
     in_specs = [vmem, vmem, hbm, hbm, hbm]
-    out_shape = [jax.ShapeDtypeStruct((tok, hid), BF16)]
+    out_shape = [jax.ShapeDtypeStruct((tok, hid), BF16 if with_expert else F32)]
     out_specs = [vmem]
     n_ex = 17 if with_expert else 3
     dma = pltpu.SemaphoreType.DMA
@@ -451,15 +454,16 @@
 SUB = 16
 
 
-def route_table(ids, wts):
-    tok, top_k = ids.shape
+def route_table(route, top_k):
+    tok = route.shape[0]
     lane = lax.broadcasted_iota(jnp.int32, (tok, 128), 1)
+    lane16 = lax.rem(lane, 16).astype(F32)
     weight = jnp.zeros((tok, 128), F32)
     member = jnp.zeros((tok, 128), F32)
     for j in range(top_k):
-        col = ids[:, j:j + 1]
-        hit = ((lane < 64) & (col == lax.rem(lane, 16))) | ((lane >= 64) & (col >= 16))
-        weight += jnp.where(hit, wts[:, j:j + 1], 0.0)
+        col = route[:, j:j + 1]
+        hit = ((lane < 64) & (col == lane16)) | ((lane >= 64) & (col >= 16.0))
+        weight += jnp.where(hit, route[:, 8 + j:9 + j], 0.0)
         member += jnp.where(hit, 1.0, 0.0)
     before = lax.broadcasted_iota(jnp.int32, (tok, tok), 0) > lax.broadcasted_iota(jnp.int32, (tok, tok), 1)
     rank = dot_n(jnp.where(before, 1.0, 0.0).astype(BF16), member.astype(BF16))
@@ -472,13 +476,13 @@
     return jnp.where(lane < 16, rank, jnp.where(lane < 67, term, 0.0)).astype(BF16)
 
 
-def att_kernel(with_table, with_far, *refs):
+def att_kernel(top_k, with_far, *refs):
     refs = list(refs)
+    with_table = top_k > 0
     lens_ref, x_ref, cos_ref, sin_ref = refs[:4]
     del refs[:4]
     if with_table:
-        ids_ref, wts_ref = refs[:2]
-        del refs[:2]
+        route_ref = refs.pop(0)
     far_hbm = refs.pop(0) if with_far else None
     wq_hbm, uk_hbm, uv_hbm, wo_hbm, cache_hbm, h_ref, u_ref = refs[:7]
     del refs[:7]
@@ -612,11 +616,17 @@
         h_ref[:, cols] = (x_ref[:, cols].astype(F32) + att).astype(BF16)
     u_ref[:, pl.ds(0, hid)] = norm(h_ref[...].astype(F32))
     if with_table:
-        u_ref[:, pl.ds(hid, 128)] = route_table(ids_ref[...], wts_ref[...])
+        u_ref[:, pl.ds(hid, 128)] = route_table(route_ref[...].T[:tok], top_k)
     if with_far:
         own_out.wait()
         for cp in far_copies:
             cp.wait()
+
+
+def pack_route(ids, wts):
+    tok, top_k = ids.shape
+    pad = ((0, 8 - top_k), (0, 128 - tok))
+    return jnp.concatenate([jnp.pad(ids.T.astype(F32), pad), jnp.pad(wts.T, pad)], axis=0)
 
 
 def att_call(x, cache, kv_lens, cos, sin, w_q, w_uk, w_uv, w_o, route=None, far=None):
@@ -631,7 +641,8 @@
     vmem, hbm = pl.BlockSpec(memory_space=pltpu.VMEM), pl.BlockSpec(memory_space=pl.ANY)
     smem = pl.BlockSpec(memory_space=pltpu.SMEM)
     with_far = far is not None
-    args = [kv_lens, x, cos, sin] + (list(route) if with_table else []) + ([far] if with_far else [])
+    top_k = route[0].shape[1] if with_table else 0
+    args = [kv_lens, x, cos, sin] + ([pack_route(*route)] if with_table else []) + ([far] if with_far else [])
     args += [w_q.transpose(1, 2, 0), w_uk, w_uv, w_o.reshape(heads * val_dim, hid), cache.transpose(0, 2, 1)]
     width = hid + (128 if with_table else 0)
     out_shape = [jax.ShapeDtypeStruct((tok, hid), BF16), jax.ShapeDtypeStruct((tok, width), BF16)]
@@ -645,9 +656,9 @@
         extra = [pltpu.VMEM((SLOT_CAP, hid), BF16), dma((2,)), dma((n_ep,)), dma((n_ep,))]
         params = {'collective_id': 2, 'has_side_effects': True}
     return pl.pallas_call(
-        functools.partial(att_kernel, with_table, with_far),
+        functools.partial(att_kernel, top_k, with_far),
         out_shape=out_shape,
-        in_specs=[smem] + [vmem] * (5 if with_table else 3) + [hbm] * (6 if with_far else 5),
+        in_specs=[smem] + [vmem] * (4 if with_table else 3) + [hbm] * (6 if with_far else 5),
         out_specs=out_specs,
         scratch_shapes=[
             pltpu.VMEM((heads, qk_dim, hid), BF16),
@@ -694,6 +705,6 @@
         f_zero, near, far, theirs = dense_call(u_ext, h_zero, ffn0_gate.T, ffn0_up.T, ffn0_down, expert=(exp_gate, exp_up, exp_down))
         h_one, u_one, back = att_call(f_zero, cache1, kv_lens, cos, sin, att1_q, att1_uk, att1_uv, att1_o, far=far)
         out, = dense_call(u_one, h_one, ffn1_gate.T, ffn1_up.T, ffn1_down, mix=(near, far, back, u_ext, theirs))
-        return out
+        return out.astype(BF16)
 
     return jax.shard_map(body, mesh=mesh, in_specs=in_specs, out_specs=rows_spec, check_vma=False)

time: 170 us -> 173 us (1.018)
  local copies, waits for them, and re-layouts: 4.57 us -> 0 us
  other arithmetic: 1.57 us -> 5.45 us
  Pallas kernels: 164 us -> 167 us
    unnamed x3 -> x0, local copies, waits for them, and re-layouts: 4.57 us -> none
    pallas_call x2, Pallas kernels: 112 us -> 116 us  [dense_call(): pl.pallas_call(functools.partial(ffn_kernel, with_expert), out_shape=out_...]
    convert_element_type x0 -> x2, other arithmetic: none -> 2.62 us  [the longest x1 1.92 us: body(): return out.astype(BF16)]
where the time goes in v7:
time: 173 us
  Pallas kernels  167 us (97%)
  other arithmetic  5.45 us (3%)
    pallas_call x2, Pallas kernels, dense_call(): pl.pallas_call(functools.partial(ffn_kernel, with_expert), out_shape=out_...  116 us
    pallas_call x2, Pallas kernels, att_call(): pl.pallas_call(functools.partial(att_kernel, top_k, with_far), out_shape=...  51.4 us

profile of v7, /device:TPU:0, one launch (start us, length us, event | category | flops | bytes accessed | tf_op | source)
XLA Modules:
  0.0 172.6 jit_solution(637785986576412897)
XLA Ops:
  0.0 0.7 convert_element_type.22
  0.7 0.7 convert_bitcast_fusion
  1.4 1.3 select_maximum_fusion.refs_4_
  2.6 0.9 fusion
  3.5 25.6 %latent_attention.2 = (bf16[96,2048]{1,0:T(8,128)(2,1)}, bf16[96,2176]{1,0:T(8,128)(2,1)}) custom-call(s32[96]{0:T(128)} %refs_0_.3, bf16[96,2048]{1,0:T(8,128)(2,1)} %refs_1_.1, f32[96,128]{1,0:T(8,128)} %get-tuple-element.24.refs_2_, f32[96,128]{1,0:T(8,128)} %get-tuple-element.23.refs_3_, f32[16,128]{1,0:T(8,128)} %select_maximum_fusion.refs_4_, ...), custom_call_target="tpu_custom_call" | custom-call | flops 3623878656 | bytes 54000000 | tf_op jit(solution)/shard_map/latent_attention/pallas_call | solution.py:658
  29.1 67.2 %dense_expert.1 = (bf16[96,2048]{1,0:T(8,128)(2,1)}, bf16[576,2048]{1,0:T(8,128)(2,1)}, bf16[576,2048]{1,0:T(8,128)(2,1)}, bf16[96,128]{1,0:T(8,128)(2,1)}) custom-call(bf16[96,2176]{1,0:T(8,128)(2,1)} %get-tuple-element.14.refs_0_.refs_8_, bf16[96,2048]{1,0:T(8,128)(2,1)} %get-tuple-element.15.refs_1_, bf16[5472,2048]{1,0:T(8,128)(2,1)} %bitcast.22, ...), custom_call_target="tpu_custom_call" | custom-call | flops 32841400320 | bytes 33619968 | tf_op jit(solution)/shard_map/dense_expert/pallas_call | solution.py:442
  96.3 25.9 %latent_attention.3 = (bf16[96,2048]{1,0:T(8,128)(2,1)}, bf16[96,2048]{1,0:T(8,128)(2,1)}, bf16[576,2048]{1,0:T(8,128)(2,1)}) custom-call(s32[96]{0:T(128)} %refs_0_.3, bf16[96,2048]{1,0:T(8,128)(2,1)} %get-tuple-element.16.refs_1_, f32[96,128]{1,0:T(8,128)} %get-tuple-element.24.refs_2_, f32[96,128]{1,0:T(8,128)} %get-tuple-element.23.refs_3_, ...), custom_call_target="tpu_custom_call" | custom-call | flops 3623878656 | bytes 54000000 | tf_op jit(solution)/shard_map/latent_attention/pallas_call | solution.py:658
  122.2 48.5 %dense.1 = f32[96,2048]{1,0:T(8,128)} custom-call(bf16[96,2048]{1,0:T(8,128)(2,1)} %get-tuple-element.18.refs_0_, bf16[96,2048]{1,0:T(8,128)(2,1)} %get-tuple-element.19.refs_1_, bf16[5472,2048]{1,0:T(8,128)(2,1)} %bitcast.15, bf16[5472,2048]{1,0:T(8,128)(2,1)} %bitcast.16, bf16[5472,2048]{1,0:T(8,128)(2,1)} %refs_4_.3, ...), custom_call_target="tpu_custom_call" | custom-call | flops 12910067712 | bytes 33619968 | tf_op jit(solution)/shard_map/dense/pallas_call | solution.py:442
  170.6 1.9 %convert_element_type.26 = bf16[96,2048]{1,0:T(8,128)(2,1)} convert(f32[96,2048]{1,0:T(8,128)} %dense.1) | non-fusion elementwise | flops 196608 | bytes 1179648 | tf_op jit(solution)/shard_map/convert_element_type | solution.py:708
  (1 shorter events, 0.0 us)

commit v8 on v7

--- a/solution.py
+++ b/solution.py
@@ -2,6 +2,7 @@
 
 import jax
 import jax.numpy as jnp
+import numpy as np
 from jax import lax
 from jax.experimental import pallas as pl
 from jax.experimental.pallas import tpu as pltpu
@@ -282,10 +283,11 @@
         d_out[col] = val[tok:]
         d_link(col).start()
 
-        @pl.when(col >= 1)
+        @pl.when(col >= 2)
         def _():
-            send_z(col - 1)
-
+            send_z(col - 2)
+
+    send_z(n_col - 2)
     send_z(n_col - 1)
     if not with_expert:
         fill_mix(mat_near, u0_ref[:, pl.ds(hid, 128)])
@@ -346,12 +348,10 @@
                                           preferred_element_type=F32)
                     acc = got if acc is None else acc + got
                 x_buf[pl.ds(pair * 2 * SLOT_CAP, 2 * SLOT_CAP)] = acc.astype(BF16)
-            for off, width in ((0, 512), (512, 512), (1024, 256)):
+            for off, width in ((0, 512), (512, 512), (1024, 384)):
                 gate_val = dot_n(x_buf[...], eg[:, pl.ds(off, width)])
                 up_val = dot_n(x_buf[...], eu[:, pl.ds(off, width)])
                 h_buf[:, pl.ds(off, width)] = (jax.nn.silu(gate_val) * up_val).astype(BF16)
-            both = dot_n(x_buf[...], jnp.concatenate([eg[:, pl.ds(1280, 128)], eu[:, pl.ds(1280, 128)]], axis=1))
-            h_buf[:, pl.ds(1280, 128)] = (jax.nn.silu(both[:, :128]) * both[:, 128:]).astype(BF16)
 
             @pl.when(it == 0)
             def _():
@@ -414,7 +414,7 @@
     n_step = ff // TILE + 1
     args = [u, h, w_gate_t, w_up_t, w_down]
     in_specs = [vmem, vmem, hbm, hbm, hbm]
-    out_shape = [jax.ShapeDtypeStruct((tok, hid), BF16 if with_expert else F32)]
+    out_shape = [jax.ShapeDtypeStruct((tok, hid), BF16)]
     out_specs = [vmem]
     n_ex = 17 if with_expert else 3
     dma = pltpu.SemaphoreType.DMA
@@ -479,14 +479,20 @@
 def att_kernel(top_k, with_far, *refs):
     refs = list(refs)
     with_table = top_k > 0
-    lens_ref, x_ref, cos_ref, sin_ref = refs[:4]
-    del refs[:4]
+    lens_ref, x_ref = refs[:2]
+    del refs[:2]
     if with_table:
         route_ref = refs.pop(0)
+    else:
+        cos_ref, sin_ref = refs[:2]
+        del refs[:2]
     far_hbm = refs.pop(0) if with_far else None
     wq_hbm, uk_hbm, uv_hbm, wo_hbm, cache_hbm, h_ref, u_ref = refs[:7]
     del refs[:7]
     back_hbm = refs.pop(0) if with_far else None
+    if with_table:
+        cos_ref, sin_ref = refs[:2]
+        del refs[:2]
     wq, uk, uv, wo, ring, xn_buf, q_buf, o_buf, ov_buf, p_buf, w_sem, ring_sem = refs[:12]
     if with_far:
         own_buf, own_sem, f_send, f_recv = refs[12:]
@@ -532,6 +538,10 @@
         return (val * lax.rsqrt(jnp.mean(val * val, axis=-1, keepdims=True) + 1e-6)).astype(BF16)
 
     xn_buf[...] = norm(x_ref[...].astype(F32))
+    if with_table:
+        angle = route_ref[...].T[:tok, 6:7] * route_ref[pl.ds(14, 1)]
+        cos_ref[...] = jnp.cos(angle)
+        sin_ref[...] = route_ref[pl.ds(15, 1)] * jnp.sin(angle)
     uk_cp.wait()
     lane = lax.broadcasted_iota(jnp.int32, (tok, 128), 1)
     first_half = lax.rem(lane, rope) < rope // 2
@@ -623,13 +633,17 @@
             cp.wait()
 
 
-def pack_route(ids, wts):
+def pack_route(ids, wts, kv_lens, rope):
     tok, top_k = ids.shape
-    pad = ((0, 8 - top_k), (0, 128 - tok))
-    return jnp.concatenate([jnp.pad(ids.T.astype(F32), pad), jnp.pad(wts.T, pad)], axis=0)
-
-
-def att_call(x, cache, kv_lens, cos, sin, w_q, w_uk, w_uv, w_o, route=None, far=None):
+    lane = np.arange(128)
+    freq = 10000.0 ** (-2.0 * (lane % (rope // 2)) / rope)
+    sign = np.where(lane % rope < rope // 2, -1.0, 1.0)
+    pad = ((0, 0), (0, 128 - tok))
+    top = jnp.pad(jnp.concatenate([ids.T, kv_lens[None, :], kv_lens[None, :]], axis=0).astype(F32), pad)
+    return jnp.concatenate([top, jnp.pad(wts.T, pad), jnp.asarray(np.stack([freq, sign]), F32)], axis=0)
+
+
+def att_call(x, cache, kv_lens, w_q, w_uk, w_uv, w_o, route=None, rotary=None, far=None):
     tok, hid = x.shape
     heads, nope, latent = w_uk.shape
     val_dim = w_uv.shape[2]
@@ -642,12 +656,15 @@
     smem = pl.BlockSpec(memory_space=pltpu.SMEM)
     with_far = far is not None
     top_k = route[0].shape[1] if with_table else 0
-    args = [kv_lens, x, cos, sin] + ([pack_route(*route)] if with_table else []) + ([far] if with_far else [])
+    args = [kv_lens, x] + ([pack_route(*route, kv_lens, w_q.shape[2] - w_uk.shape[1])] if with_table else list(rotary)) + ([far] if with_far else [])
     args += [w_q.transpose(1, 2, 0), w_uk, w_uv, w_o.reshape(heads * val_dim, hid), cache.transpose(0, 2, 1)]
     width = hid + (128 if with_table else 0)
     out_shape = [jax.ShapeDtypeStruct((tok, hid), BF16), jax.ShapeDtypeStruct((tok, width), BF16)]
     out_specs = [vmem, vmem]
     extra, params = [], {}
+    if with_table:
+        out_shape += [jax.ShapeDtypeStruct((tok, 128), F32)] * 2
+        out_specs += [vmem, vmem]
     if with_far:
         n_ep = far.shape[0] // SLOT_CAP
         out_shape.append(jax.ShapeDtypeStruct(far.shape, BF16))
@@ -658,7 +675,7 @@
     return pl.pallas_call(
         functools.partial(att_kernel, top_k, with_far),
         out_shape=out_shape,
-        in_specs=[smem] + [vmem] * (4 if with_table else 3) + [hbm] * (6 if with_far else 5),
+        in_specs=[smem] + [vmem] * (2 if with_table else 3) + [hbm] * (6 if with_far else 5),
         out_specs=out_specs,
         scratch_shapes=[
             pltpu.VMEM((heads, qk_dim, hid), BF16),
@@ -680,13 +697,6 @@
     )(*args)
 
 
-def rope_tables(kv_lens, rope):
-    lane = jnp.arange(128)
-    inv_freq = 10000.0 ** (-2.0 * (lane % (rope // 2)).astype(F32) / rope)
-    angle = kv_lens.astype(F32)[:, None] * inv_freq[None, :]
-    return jnp.cos(angle), jnp.where(lane % rope < rope // 2, -1.0, 1.0) * jnp.sin(angle)
-
-
 def solution(mesh):
     assert mesh.shape['tp'] == 2 and mesh.shape['ep'] == 8
     rows_spec = P(FLAT_AXES, None)
@@ -700,11 +710,10 @@
                 cube_spec, cube_spec, cube_spec)
 
     def body(hidden_in, cache0, cache1, kv_lens, route_ids, route_wts, att0_q, att0_uk, att0_uv, att0_o, att1_q, att1_uk, att1_uv, att1_o, ffn0_gate, ffn0_up, ffn0_down, ffn1_gate, ffn1_up, ffn1_down, exp_gate, exp_up, exp_down):
-        cos, sin = rope_tables(kv_lens, att0_q.shape[2] - att0_uk.shape[1])
-        h_zero, u_ext = att_call(hidden_in, cache0, kv_lens, cos, sin, att0_q, att0_uk, att0_uv, att0_o, route=(route_ids, route_wts))
+        h_zero, u_ext, cos, sin = att_call(hidden_in, cache0, kv_lens, att0_q, att0_uk, att0_uv, att0_o, route=(route_ids, route_wts))
         f_zero, near, far, theirs = dense_call(u_ext, h_zero, ffn0_gate.T, ffn0_up.T, ffn0_down, expert=(exp_gate, exp_up, exp_down))
-        h_one, u_one, back = att_call(f_zero, cache1, kv_lens, cos, sin, att1_q, att1_uk, att1_uv, att1_o, far=far)
+        h_one, u_one, back = att_call(f_zero, cache1, kv_lens, att1_q, att1_uk, att1_uv, att1_o, rotary=(cos, sin), far=far)
         out, = dense_call(u_one, h_one, ffn1_gate.T, ffn1_up.T, ffn1_down, mix=(near, far, back, u_ext, theirs))
-        return out.astype(BF16)
+        return out
 
     return jax.shard_map(body, mesh=mesh, in_specs=in_specs, out_specs=rows_spec, check_vma=False)

time: 173 us -> 168 us (0.971)
  other arithmetic: 5.45 us -> 2.04 us
  Pallas kernels: 167 us -> 164 us
  local copies, waits for them, and re-layouts: 0 us -> 1.77 us
    pallas_call x2, Pallas kernels: 116 us -> 112 us  [dense_call(): pl.pallas_call(functools.partial(ffn_kernel, with_expert), out_shape=out_...]
    convert_element_type x3 -> x1, other arithmetic: 3.27 us -> 0.74 us  [pack_route(): jnp.concatenate([ids.T, kv_lens[None, :], kv_lens[None, :]], axis=0)]
    unnamed x0 -> x1, local copies, waits for them, and re-layouts: none -> 1.77 us
where the time goes in v8:
time: 168 us; the launch traced here: 167 us
  Pallas kernels  164 us (98%)
  other arithmetic  2.04 us (1%)
  local copies, waits for them, and re-layouts  1.77 us (1%)
    pallas_call x2, Pallas kernels, dense_call(): pl.pallas_call(functools.partial(ffn_kernel, with_expert), out_shape=out_...  112 us
    pallas_call x2, Pallas kernels, att_call(): pl.pallas_call(functools.partial(att_kernel, top_k, with_far), out_shape=...  51.3 us

profile of v8, /device:TPU:0, one launch (start us, length us, event | category | flops | bytes accessed | tf_op | source)
XLA Modules:
  0.0 167.4 jit_solution(9103887064370312125)
XLA Ops:
  0.0 0.7 add_convert_fusion
  0.7 1.3 fusion.refs_2_
  2.0 25.5 %latent_attention.2 = (bf16[96,2048]{1,0:T(8,128)(2,1)}, bf16[96,2176]{1,0:T(8,128)(2,1)}, f32[96,128]{1,0:T(8,128)}, f32[96,128]{1,0:T(8,128)}) custom-call(s32[96]{0:T(128)} %refs_0_.3, bf16[96,2048]{1,0:T(8,128)(2,1)} %refs_1_.1, f32[16,128]{1,0:T(8,128)} %fusion.refs_2_, bf16[16,192,2048]{2,1,0:T(8,128)(2,1)} %bitcast.17, bf16[16,128,512]{2,1,0:T(8,128)(2,1)} %refs_4_.3, ...), custom_call_target="tpu_custom_call" | custom-call | flops 3623878656 | bytes 54000000 | tf_op jit(solution)/shard_map/latent_attention/pallas_call | solution.py:675
  27.6 64.0 %dense_expert.1 = (bf16[96,2048]{1,0:T(8,128)(2,1)}, bf16[576,2048]{1,0:T(8,128)(2,1)}, bf16[576,2048]{1,0:T(8,128)(2,1)}, bf16[96,128]{1,0:T(8,128)(2,1)}) custom-call(bf16[96,2176]{1,0:T(8,128)(2,1)} %get-tuple-element.16.refs_0_.refs_8_, bf16[96,2048]{1,0:T(8,128)(2,1)} %get-tuple-element.17.refs_1_, bf16[5472,2048]{1,0:T(8,128)(2,1)} %bitcast.24, ...), custom_call_target="tpu_custom_call" | custom-call | flops 32841400320 | bytes 33619968 | tf_op jit(solution)/shard_map/dense_expert/pallas_call | solution.py:442
  91.6 25.8 %latent_attention.3 = (bf16[96,2048]{1,0:T(8,128)(2,1)}, bf16[96,2048]{1,0:T(8,128)(2,1)}, bf16[576,2048]{1,0:T(8,128)(2,1)}) custom-call(s32[96]{0:T(128)} %refs_0_.3, bf16[96,2048]{1,0:T(8,128)(2,1)} %get-tuple-element.18.refs_1_, f32[96,128]{1,0:T(8,128)} %get-tuple-element.19.refs_2_, f32[96,128]{1,0:T(8,128)} %get-tuple-element.20.refs_3_, ...), custom_call_target="tpu_custom_call" | custom-call | flops 3623878656 | bytes 54000000 | tf_op jit(solution)/shard_map/latent_attention/pallas_call | solution.py:675
  117.4 48.1 %dense.1 = bf16[96,2048]{1,0:T(8,128)(2,1)} custom-call(bf16[96,2048]{1,0:T(8,128)(2,1)} %get-tuple-element.22.refs_0_, bf16[96,2048]{1,0:T(8,128)(2,1)} %get-tuple-element.23.refs_1_, bf16[5472,2048]{1,0:T(8,128)(2,1)} %bitcast.15, bf16[5472,2048]{1,0:T(8,128)(2,1)} %bitcast.16, bf16[5472,2048]{1,0:T(8,128)(2,1)} %refs_4_.5, ...), custom_call_target="tpu_custom_call" | custom-call | flops 12910067712 | bytes 33619968 | tf_op jit(solution)/shard_map/dense/pallas_call | solution.py:442
  165.6 1.8 %copy.26 = bf16[96,2048]{1,0:T(8,128)(2,1)} copy(bf16[96,2048]{1,0:T(8,128)(2,1)} %dense.1) | data formatting | bytes 786432
